TPU v7x, 512 devices: a 4x2x32 block of a 4x16x32 slice. The times are simulated.
512 devices in a mesh: groups: 2 (over y), slab: 32 (over z), coil: 4 (over x), row: 2 (over core).
Axes of the slice: x: 4, y: 2, z: 32, core: 2. Of those that a mesh axis runs over, the one named last changes fastest.
The devices are a block of a 4x16x32 slice.
Arguments:
- image: float32 [4, 128, 256, 128], P('groups', None, ('slab', 'row')), parts along dimension 0, may hold values from -6 to 6
- sens: bfloat16 [4, 16, 128, 256, 128], P('groups', 'coil', None, ('slab', 'row')), parts along dimension 0, may hold values from -1.5 to 1.5
- measured: bfloat16 [4, 16, 128, 256, 128], P('groups', 'coil', ('slab', 'row')), parts along dimension 0, may hold values from -3 to 3
- mask: int32 [128, 256], P(('slab', 'row')), may hold values from 0 to 1, as said below
- thresholds: float32 [2, 7], replicated, may hold values from 0.1 to 1.5
Outputs:
- image_next: float32 [4, 128, 256, 128], P('groups', None, ('slab', 'row')), parts along dimension 0
There are 2 independent parts, one for each index of `groups`. A program takes and returns all parts, laid end to end along the dimension named above; an argument that names none is the same for every part. Nothing has to cross between parts.
Inputs may be any that keep to these rules, and one draw needn't show every extreme that they name: `mask`: A calibration block of the 8 central phase-encode lines (ky from 60 to 67) is sampled at every kz; outside it each (ky, kz) is sampled independently at random.
All inputs are finite; a program needn't handle non-finite values.
Results may differ from a plain program's by a relative error of at most 0.013.
Values may be sent and summed in bfloat16 or wider, within the bound.
No kernel may reach another device: no remote copies, remote signals or barrier semaphores. Data moves between devices by JAX's collectives and lax.ppermute only.
A program may use at most 128 MiB of HBM per device.

v0:
```python
import math

import jax
import jax.numpy as jnp
from jax import lax
from jax.sharding import PartitionSpec as P

half_root = 0.7071067811865476
quarter_root = 0.3535533905932738
step_size = 0.5


def padded(block, sides, width):
    for axis, dim in sides:
        count = lax.axis_size(axis)
        forward = [(i, i + 1) for i in range(count - 1)]
        forward.append((count - 1, 0))
        backward = [(target, source) for source, target in forward]
        low = lax.ppermute(
            lax.slice_in_dim(block, block.shape[dim] - width, None, axis=dim), axis, forward
        )
        high = lax.ppermute(lax.slice_in_dim(block, 0, width, axis=dim), axis, backward)
        block = jnp.concatenate([low, block, high], axis=dim)
    return block


def copy_for_each(x, axis):
    size = lax.axis_size(axis)
    return lax.all_to_all(jnp.broadcast_to(x[None], (size, *x.shape)), axis, 0, 0, tiled=True)


def over_copies(x, axis):
    return copy_for_each(x, axis).astype(jnp.float32).sum(axis=0)


def fourier_table(length, sign):
    index = jnp.arange(length, dtype=jnp.int32)
    phase = index[:, None] * index[None, :] % length
    theta = phase.astype(jnp.float32) * jnp.float32(2.0 * math.pi / length)
    scale = jnp.float32(1.0 / math.sqrt(length))
    real = jnp.cos(theta) * scale
    imaginary = jnp.sin(theta) * (sign * scale)
    upper = jnp.stack([real, -imaginary])
    lower = jnp.stack([imaginary, real])
    return jnp.stack([upper, lower]).astype(jnp.bfloat16)


def contract(form, values, table):
    return jnp.einsum(form, values, table, preferred_element_type=jnp.float32)


def complex_product(left, right):
    return jnp.stack(
        [left[0] * right[0] - left[1] * right[1], left[0] * right[1] + left[1] * right[0]]
    )


def roll_after(values, along, offset):
    return jnp.roll(values, -offset, axis=along)


def roll_before(values, along, offset):
    return jnp.roll(values, offset, axis=along)


def split_bands(bands, along, offset, after):
    moved = after(bands, along, offset)
    return jnp.concatenate([(bands + moved) * half_root, (bands - moved) * half_root], axis=0)


def merge_bands(bands, along, offset, before):
    half = bands.shape[0] // 2
    lower = bands[:half]
    upper = bands[half:]
    return (lower + upper + before(lower - upper, along, offset)) * quarter_root


def shrink_detail(detail, limit):
    magnitude = jnp.sqrt(detail[:, 0] * detail[:, 0] + detail[:, 1] * detail[:, 1])
    limit = limit.reshape((-1, 1, 1, 1))
    factor = jnp.maximum(magnitude - limit, 0.0) / jnp.maximum(magnitude, limit)
    return detail * factor[:, None]


def wavelet_shrink(descent, thresholds, moves):
    coarse = descent[None]
    details = []
    for level in range(thresholds.shape[0]):
        offset = 2**level
        bands = coarse
        for along, after, before in moves:
            bands = split_bands(bands, along, offset, after)
        coarse = bands[:1]
        details.append(shrink_detail(bands[1:], thresholds[level]))
    for level in reversed(range(thresholds.shape[0])):
        offset = 2**level
        bands = jnp.concatenate([coarse, details[level]], axis=0)
        for along, after, before in reversed(moves):
            bands = merge_bands(bands, along, offset, before)
        coarse = bands
    return coarse[0]


def margin_shrink(descent, thresholds, moves):
    margin = 2 ** thresholds.shape[0] - 1
    planes_own = descent.shape[2]
    widened = padded(descent.astype(jnp.bfloat16), ((("slab", "row"), 2),), margin).astype(
        descent.dtype
    )
    result = wavelet_shrink(widened, thresholds, moves)
    return lax.slice_in_dim(result, margin, margin + planes_own, axis=2)


def local(image, sens, measured, mask, thresholds):
    readout_cells = image.shape[3]
    phase_cells = image.shape[1]
    plane_count = image.shape[2]
    coil_count = sens.shape[1]
    line_count = measured.shape[2]
    depth_cells = measured.shape[3]
    slab_count = lax.axis_size("slab")
    row_count = lax.axis_size("row")
    table_readout = fourier_table(readout_cells, -1.0)
    table_phase = fourier_table(phase_cells, -1.0)
    table_depth = fourier_table(depth_cells, -1.0)
    inverse_readout = fourier_table(readout_cells, 1.0)
    inverse_phase = fourier_table(phase_cells, 1.0)
    inverse_depth = fourier_table(depth_cells, 1.0)
    sens_wide = sens.astype(jnp.float32)
    coil_image = complex_product(sens_wide, image[:, None]).astype(jnp.bfloat16)
    readout_done = contract("tcyzj,stjk->scyzk", coil_image, table_readout).astype(jnp.bfloat16)
    phase_done = contract("tcjzx,stjk->sckzx", readout_done, table_phase).astype(jnp.bfloat16)
    shaped = phase_done.reshape(
        2, coil_count, slab_count, row_count, line_count, 1, 1, plane_count, readout_cells
    )
    moved = lax.all_to_all(
        lax.all_to_all(shaped, "slab", split_axis=2, concat_axis=5, tiled=True),
        "row",
        split_axis=3,
        concat_axis=6,
        tiled=True,
    )
    spread = moved.reshape(2, coil_count, line_count, depth_cells, readout_cells)
    spectrum = contract("tcyjx,stjk->scykx", spread, table_depth)
    sampled = mask.astype(jnp.float32)[None, None, :, :, None]
    residual = (sampled * (spectrum - measured.astype(jnp.float32))).astype(jnp.bfloat16)
    depth_back = contract("tcyjx,stjk->scykx", residual, inverse_depth).astype(jnp.bfloat16)
    shaped_back = depth_back.reshape(
        2, coil_count, 1, 1, line_count, slab_count, row_count, plane_count, readout_cells
    )
    moved_back = lax.all_to_all(
        lax.all_to_all(shaped_back, "slab", split_axis=5, concat_axis=2, tiled=True),
        "row",
        split_axis=6,
        concat_axis=3,
        tiled=True,
    )
    gathered = moved_back.reshape(2, coil_count, phase_cells, plane_count, readout_cells)
    phase_back = contract("tcjzx,stjk->sckzx", gathered, inverse_phase).astype(jnp.bfloat16)
    readout_back = contract("tcyzj,stjk->scyzk", phase_back, inverse_readout)
    partial_value = jnp.stack(
        [
            jnp.sum(sens_wide[0] * readout_back[0] + sens_wide[1] * readout_back[1], axis=0),
            jnp.sum(sens_wide[0] * readout_back[1] - sens_wide[1] * readout_back[0], axis=0),
        ]
    )
    gradient = over_copies(partial_value.astype(jnp.bfloat16), "coil").astype(jnp.float32)
    descent = image - step_size * gradient
    moves = [
        (4, roll_after, roll_before),
        (2, roll_after, roll_before),
        (3, roll_after, roll_before),
    ]
    return margin_shrink(descent, thresholds, moves)


def solution(mesh):
    return jax.shard_map(
        local,
        mesh=mesh,
        in_specs=(
            P("groups", None, ("slab", "row"), None),
            P("groups", "coil", None, ("slab", "row"), None),
            P("groups", "coil", ("slab", "row"), None, None),
            P(("slab", "row"), None),
            P(),
        ),
        out_specs=P("groups", None, ("slab", "row"), None),
        check_vma=False,
    )
```

profile of v0, /device:TPU:40, one launch (start us, length us, event | category | flops | bytes accessed | tf_op | source)
XLA Modules:
  0.0 369.0 jit_solution(7721524944372572918)
XLA Ops:
  0.8 1.5 copy_convert_fusion
  2.4 1.3 subtract_convert_fusion
  3.7 1.9 bitcast_convert_fusion.2
  5.7 2.4 copy.37
  8.1 45.8 %all-to-all-start = ((bf16[2,4,32,2,2,1,1,4,128]{8,7,3,4,1,0,6,5,2:T(4,128)(2,1)}), bf16[2,4,32,2,2,1,1,4,128]{8,7,3,4,1,0,6,5,2:T(4,128)(2,1)S(1)}, u32[]{:S(2)}, u32[]{:S(2)}) async-start(bf16[2,4,32,2,2,1,1,4,128]{8,7,3,4,1,0,6,5,2:T(4,128)(2,1)} %copy.37), calls=%async_computation | async-start | bytes 2097152 | tf_op jit(solution)/shard_map/all_to_all | solution.py:137
  53.9 1.0 multiply_convert_fusion.2
  54.9 1.1 multiply_convert_fusion
  56.0 1.0 negate_convert_fusion
  57.0 0.9 fusion.47
  57.9 100.4 %all-to-all-done = bf16[2,4,32,2,2,1,1,4,128]{8,7,3,4,1,0,6,5,2:T(4,128)(2,1)S(1)} async-done(((bf16[2,4,32,2,2,1,1,4,128]{8,7,3,4,1,0,6,5,2:T(4,128)(2,1)}), bf16[2,4,32,2,2,1,1,4,128]{8,7,3,4,1,0,6,5,2:T(4,128)(2,1)S(1)}, u32[]{:S(2)}, u32[]{:S(2)}) %all-to-all-start) | async-done | bytes 1048608 | tf_op jit(solution)/shard_map/all_to_all | solution.py:137
  158.3 0.5 copy.38
  158.9 4.7 %all_to_all.71 = bf16[2,4,1,2,2,32,1,4,128]{8,7,5,4,1,0,6,2,3:T(4,128)(2,1)S(1)} all-to-all(bf16[2,4,1,2,2,32,1,4,128]{8,7,5,4,1,0,6,2,3:T(4,128)(2,1)S(1)} %copy.38), channel_id=1, replica_groups=mesh['groups'=2,'slab'=32,'coil'=4,'row'=2] {'row'}, dimensions={3} | all-to-all | bytes 2097152 | tf_op jit(solution)/shard_map/all_to_all | solution.py:136
  164.1 0.7 fusion.23
  165.0 0.7 bitcast_convert_fusion.1
  165.7 1.6 copy.42
  167.3 112.7 %all_to_all.72 = bf16[2,4,1,1,2,32,2,4,128]{8,4,6,7,1,0,3,2,5:T(2,128)(2,1)S(1)} all-to-all(bf16[2,4,1,1,2,32,2,4,128]{8,4,6,7,1,0,3,2,5:T(2,128)(2,1)S(1)} %copy.42), channel_id=1, replica_groups=mesh['groups'=2,'slab'=32,'coil'=4,'row'=2] {'slab'}, dimensions={5} | all-to-all | bytes 2097152 | tf_op jit(solution)/shard_map/all_to_all | solution.py:152
  280.0 1.1 copy.43
  281.1 4.6 %all_to_all.73 = bf16[2,4,32,1,2,1,2,4,128]{8,4,2,7,1,0,5,3,6:T(2,128)(2,1)S(1)} all-to-all(bf16[2,4,32,1,2,1,2,4,128]{8,4,2,7,1,0,5,3,6:T(2,128)(2,1)S(1)} %copy.43), channel_id=1, replica_groups=mesh['groups'=2,'slab'=32,'coil'=4,'row'=2] {'row'}, dimensions={6} | all-to-all | bytes 2097152 | tf_op jit(solution)/shard_map/all_to_all | solution.py:151
  285.7 0.9 copy.44
  286.6 2.1 convolution_bitcast_fusion
  288.7 2.0 add_reduce_fusion
  291.4 19.8 %all_to_all.74 = bf16[4,2,128,4,128]{4,2,3,1,0:T(8,128)(2,1)S(1)} all-to-all(bf16[4,2,128,4,128]{4,2,3,1,0:T(8,128)(2,1)S(1)} %broadcast_in_dim.2), channel_id=1, replica_groups=mesh['groups'=2,'slab'=32,'coil'=4,'row'=2] {'coil'}, dimensions={0} | all-to-all | bytes 2097152 | tf_op jit(solution)/shard_map/all_to_all | solution.py:29
  311.6 0.5 collective-permute-start
  312.1 2.7 collective-permute-done.1
  314.8 3.2 collective-permute-done
  318.4 0.6 add_multiply_fusion.5
  319.3 1.0 subtract_multiply_fusion.3
  320.4 0.6 fusion.6
  320.9 2.9 subtract_multiply_fusion
  324.4 0.5 add_multiply_fusion.4
  325.2 1.1 subtract_multiply_fusion.2
  326.4 0.5 fusion.17
  326.9 1.6 subtract_multiply_fusion.1
  328.6 2.2 copy-done.1
  330.8 1.5 copy-done.2
  332.3 3.7 divide_bitcast_fusion.1
  336.0 5.6 %fusion.3 = f32[7,2,128,10,128]{4,2,3,1,0:T(8,128)S(1)} fusion(f32[4,2,128,10,128]{4,2,3,1,0:T(8,128)} %copy-done.1, f32[4,2,128,10,128]{4,2,3,1,0:T(8,128)} %copy-done.2, f32[7,128,10,128]{3,1,2,0:T(8,128)} %divide_bitcast_fusion.1), kind=kLoop, calls=%fused_computation.11 | loop fusion | flops 4587520 | bytes 24248320 | tf_op jit(solution)/shard_map/mul | solution.py:82
  341.7 3.4 slice_subtract_fusion.1
  345.0 5.4 %divide_bitcast_fusion = f32[7,128,10,128]{3,1,2,0:T(8,128)} fusion(f32[4,2,128,10,128]{4,2,3,1,0:T(8,128)} %get-tuple-element.9, f32[4,2,128,10,128]{4,2,3,1,0:T(8,128)S(1)} %get-tuple-element.10, f32[7]{0:T(128)S(1)} %get-tuple-element.34), kind=kLoop, calls=%fused_computation.49 | loop fusion | flops 10321920 | bytes 15073308 | tf_op jit(solution)/shard_map/mul | solution.py:82
  350.4 5.8 %fusion.1 = f32[7,2,128,10,128]{4,2,3,1,0:T(8,128)S(1)} fusion(f32[4,2,128,10,128]{4,2,3,1,0:T(8,128)} %copy-done, f32[4,2,128,10,128]{4,2,3,1,0:T(8,128)} %get-tuple-element.9, f32[7,128,10,128]{3,1,2,0:T(8,128)} %divide_bitcast_fusion), kind=kLoop, calls=%fused_computation.9 | loop fusion | flops 4587520 | bytes 24248320 | tf_op jit(solution)/shard_map/mul | solution.py:82
  356.9 1.7 fusion.4
  358.6 0.5 slice_subtract_fusion.3
  359.1 1.2 fusion.20
  361.3 1.5 slice_subtract_fusion
  362.8 0.5 slice.315
  363.4 1.7 fusion.5
  365.6 1.2 fusion.21
  367.8 1.1 copy.51
  (65 shorter events, 7.7 us)
Async XLA Ops:
  0.0 2.3 copy-start.3
  5.7 48.1 %copy-start.8 = (s32[2,256]{1,0:T(2,128)S(1)}, s32[2,256]{1,0:T(2,128)}, u32[]{:S(2)}) copy-start(s32[2,256]{1,0:T(2,128)} %param.8) | copy-start | bytes 6148
  8.1 150.3 %all-to-all-start = ((bf16[2,4,32,2,2,1,1,4,128]{8,7,3,4,1,0,6,5,2:T(4,128)(2,1)}), bf16[2,4,32,2,2,1,1,4,128]{8,7,3,4,1,0,6,5,2:T(4,128)(2,1)S(1)}, u32[]{:S(2)}, u32[]{:S(2)}) async-start(bf16[2,4,32,2,2,1,1,4,128]{8,7,3,4,1,0,6,5,2:T(4,128)(2,1)} %copy.37), calls=%async_computation | async-start | bytes 2097152 | tf_op jit(solution)/shard_map/all_to_all | solution.py:137
  158.9 5.2 %copy-start.6 = (bf16[1,2,256,256]{2,3,1,0:T(8,128)(2,1)S(1)}, bf16[1,2,256,256]{2,3,1,0:T(8,128)(2,1)}, u32[]{:S(2)}) copy-start(bf16[1,2,256,256]{2,3,1,0:T(8,128)(2,1)} %get-tuple-element.26) | copy-start | bytes 786436
  158.9 5.2 %copy-start.7 = (bf16[1,2,256,256]{2,3,1,0:T(8,128)(2,1)S(1)}, bf16[1,2,256,256]{2,3,1,0:T(8,128)(2,1)}, u32[]{:S(2)}) copy-start(bf16[1,2,256,256]{2,3,1,0:T(8,128)(2,1)} %get-tuple-element.27) | copy-start | bytes 786436
  158.9 5.2 %copy-start.10 = (bf16[2,4,2,256,128]{4,3,2,1,0:T(8,128)(2,1)S(1)}, bf16[2,4,2,256,128]{4,3,2,1,0:T(8,128)(2,1)}, u32[]{:S(2)}) copy-start(bf16[2,4,2,256,128]{4,3,2,1,0:T(8,128)(2,1)} %param.7) | copy-start | bytes 3145732
  164.0 1.0 copy-start.5
  291.2 20.2 %copy-start.4 = (f32[2,128,4,128]{3,2,1,0:T(4,128)S(1)}, f32[2,128,4,128]{3,2,1,0:T(4,128)}, u32[]{:S(2)}) copy-start(f32[2,128,4,128]{3,2,1,0:T(4,128)} %param.5) | copy-start | bytes 1572868
  291.4 20.7 %copy-start.9 = (f32[2,7]{1,0:T(2,128)S(1)}, f32[2,7]{1,0:T(2,128)}, u32[]{:S(2)}) copy-start(f32[2,7]{1,0:T(2,128)} %param.9) | copy-start | bytes 172
  311.5 3.3 collective-permute-start.1
  311.6 6.4 %collective-permute-start = (bf16[2,128,3,128]{3,1,2,0:T(8,128)(2,1)S(1)}, bf16[2,128,3,128]{3,1,2,0:T(8,128)(2,1)S(1)}, u32[]{:S(2)}, u32[]{:S(2)}) collective-permute-start(bf16[2,128,3,128]{3,1,2,0:T(8,128)(2,1)S(1)} %get-tuple-element.23), channel_id=1, source_target_pairs={{0,1},{1,8},{8,9},{9,16},{16,17},{17,24},{24,25},{25,32},{32,33},{... | collective-permute-start | bytes 589832 | tf_op jit(solution)/shard_map/ppermute | solution.py:19
  323.9 21.2 %copy-start = (f32[4,2,128,10,128]{4,2,3,1,0:T(8,128)}, f32[4,2,128,10,128]{4,2,3,1,0:T(8,128)S(1)}, u32[]{:S(2)}) copy-start(f32[4,2,128,10,128]{4,2,3,1,0:T(8,128)S(1)} %get-tuple-element.10) | copy-start | bytes 15728644
  328.5 2.3 copy-start.1
  328.5 3.8 %copy-start.2 = (f32[4,2,128,10,128]{4,2,3,1,0:T(8,128)}, f32[4,2,128,10,128]{4,2,3,1,0:T(8,128)S(1)}, u32[]{:S(2)}) copy-start(f32[4,2,128,10,128]{4,2,3,1,0:T(8,128)S(1)} %get-tuple-element.7) | copy-start | bytes 15728644
  350.4 6.2 %slice-start = ((f32[4,2,128,10,128]{4,2,3,1,0:T(8,128)}), f32[4,2,128,8,128]{4,2,3,1,0:T(8,128)S(1)}, s32[]{:S(2)}) async-start(f32[4,2,128,10,128]{4,2,3,1,0:T(8,128)} %slice_subtract_fusion.1), calls=%async_computation.5 | async-start | bytes 8388608 | tf_op jit(solution)/shard_map/jit(_roll_static)/slice | solution.py:63
  350.4 6.5 %slice-start.1 = ((f32[4,2,128,10,128]{4,2,3,1,0:T(8,128)}), f32[4,2,128,2,128]{4,2,3,1,0:T(8,128)S(1)}, s32[]{:S(2)}) async-start(f32[4,2,128,10,128]{4,2,3,1,0:T(8,128)} %slice_subtract_fusion.1), calls=%async_computation.6 | async-start | bytes 2097152 | tf_op jit(solution)/shard_map/jit(_roll_static)/slice | solution.py:63
where the time goes:
time: 370 us; the launch traced here: 369 us
  blocking collectives  142 us (38%)
  waiting for transfers between devices  106 us (29%)
  other arithmetic  52.7 us (14%)
  starting transfers between devices  46.3 us (13%)
  local copies, waits for them, and re-layouts  15.9 us (4%)
  matrix products  5.47 us (1%)
    all_to_all x1, blocking collectives, local(): lax.all_to_all(shaped_back, 'slab', split_axis=5, concat_axis=2, tiled=True)  113 us
    all_to_all x1, waiting for transfers between devices, local(): lax.all_to_all(shaped, 'slab', split_axis=2, concat_axis=5, tiled=True)  100 us
    all_to_all x1, starting transfers between devices, local(): lax.all_to_all(shaped, 'slab', split_axis=2, concat_axis=5, tiled=True)  45.8 us
    mul x4, other arithmetic, shrink_detail(): return detail * factor[:, None]  20.5 us
    all_to_all x1, blocking collectives, copy_for_each(): lax.all_to_all(jnp.broadcast_to(x[None], (size, *x.shape)), axis, 0, 0, t...  19.8 us
  transfers between devices with their start and end apart: 3, of which 3 were waited for; matrix products, arithmetic and copies ran while one was open for 1% of the time, Pallas kernels for 0%

commit v1 on v0

v1 whole, which is shorter than its diff:
```python
import math

import jax
import jax.numpy as jnp
import ml_dtypes
import numpy as np
from jax import lax
from jax.experimental import pallas as pl
from jax.experimental.pallas import tpu as pltpu
from jax.sharding import PartitionSpec as P

step_size = 0.5
lines_axes = ("slab", "row")
chunk_count = 1


def fourier_table(length, sign, rows=None, columns=None):
    index = np.arange(length, dtype=np.int64)
    phase = (index[:, None] * index[None, :]) % length
    theta = phase.astype(np.float32) * np.float32(2.0 * math.pi / length)
    scale = np.float32(1.0 / math.sqrt(length))
    real = (np.cos(theta) * scale).astype(np.float32)
    imaginary = (np.sin(theta) * np.float32(sign) * scale).astype(np.float32)
    if rows is not None:
        real, imaginary = real[rows], imaginary[rows]
    if columns is not None:
        real, imaginary = real[:, columns], imaginary[:, columns]
    return np.block([[real, -imaginary], [imaginary, real]]).astype(ml_dtypes.bfloat16)


def dot(left, right):
    return jnp.dot(left, right, preferred_element_type=jnp.float32)


def forward_kernel(devices, lines, planes, sens_ref, image_ref, table_ref, out_ref, product, mixed):
    cells = product.shape[1] // planes
    group = lines * planes
    sr = sens_ref[0, 0].astype(jnp.float32)
    si = sens_ref[1, 0].astype(jnp.float32)
    ir = image_ref[0]
    ii = image_ref[1]
    product[0] = sr * ir - si * ii
    product[1] = sr * ii + si * ir
    columns = [
        jnp.concatenate(
            [product[t, pl.ds(z, cells, stride=planes), :].astype(jnp.bfloat16) for t in range(2)],
            axis=0,
        )
        for z in range(planes)
    ]
    done = dot(table_ref[...], jnp.concatenate(columns, axis=1))
    width = product.shape[2]
    for s in range(2):
        for z in range(planes):
            for line in range(lines):
                first = s * cells + line * devices
                mixed[s, pl.ds(z * lines + line, devices, stride=group), :] = done[
                    first : first + devices, z * width : (z + 1) * width
                ]
        out_ref[:, s, 0] = mixed[s].astype(jnp.bfloat16).reshape(devices, group, width)


def middle_kernel(lines, in_ref, measured_ref, mask_ref, table_ref, inverse_ref, out_ref, mixed, back):
    devices, _, _, group, width = in_ref.shape
    cells = devices * group // lines
    for t in range(2):
        mixed[t] = in_ref[:, t, 0].astype(jnp.float32).reshape(devices * group, width)
    columns = [
        jnp.concatenate(
            [mixed[t, pl.ds(line, cells, stride=lines), :].astype(jnp.bfloat16) for t in range(2)],
            axis=0,
        )
        for line in range(lines)
    ]
    spectrum = dot(table_ref[...], jnp.concatenate(columns, axis=1))
    residual = []
    for line in range(lines):
        parts = []
        for t in range(2):
            value = spectrum[t * cells : (t + 1) * cells, line * width : (line + 1) * width]
            value = mask_ref[line] * (value - measured_ref[t, 0, line].astype(jnp.float32))
            parts.append(value.astype(jnp.bfloat16))
        residual.append(jnp.concatenate(parts, axis=0))
    result = dot(inverse_ref[...], jnp.concatenate(residual, axis=1))
    for s in range(2):
        for line in range(lines):
            back[s, pl.ds(line, cells, stride=lines), :] = result[
                s * cells : (s + 1) * cells, line * width : (line + 1) * width
            ]
        out_ref[:, s, 0] = back[s].astype(jnp.bfloat16).reshape(devices, group, width)


def backward_kernel(lines, planes, first_ref, in_ref, sens_ref, table_ref, out_ref, mixed, wide, total):
    devices, _, _, group, width = in_ref.shape
    cells = devices * lines
    coil = pl.program_id(0)

    @pl.when(coil == 0)
    def _():
        if first_ref is None:
            total[...] = jnp.zeros(total.shape, jnp.float32)
        else:
            total[...] = first_ref[...]

    for t in range(2):
        mixed[t] = in_ref[:, t, 0].astype(jnp.float32).reshape(devices * group, width)
        wide[t] = sens_ref[t, 0].astype(jnp.float32)
    columns = [
        jnp.concatenate(
            [
                mixed[t, pl.ds(z * lines + line, devices, stride=group), :].astype(jnp.bfloat16)
                for t in range(2)
                for line in range(lines)
            ],
            axis=0,
        )
        for z in range(planes)
    ]
    done = dot(table_ref[...], jnp.concatenate(columns, axis=1))
    for z in range(planes):
        rr = done[:cells, z * width : (z + 1) * width]
        ri = done[cells:, z * width : (z + 1) * width]
        sr = wide[0, pl.ds(z, cells, stride=planes), :]
        si = wide[1, pl.ds(z, cells, stride=planes), :]
        total[0, z] += sr * rr + si * ri
        total[1, z] += sr * ri - si * rr

    @pl.when(coil == pl.num_programs(0) - 1)
    def _():
        out_ref[...] = total[...].astype(out_ref.dtype)


def removed(real, imaginary, limit):
    factor = jnp.minimum(lax.rsqrt(real * real + imaginary * imaginary) * limit, 1.0)
    return real * factor, imaginary * factor


def wavelet_kernel(planes, own_ref, low_ref, high_ref, limits_ref, out_ref, a0, lo0, hi0, a1, lo1, hi1, sums, diffs):
    rows, width = own_ref.shape[2], own_ref.shape[3]
    margin = low_ref.shape[1]
    count = planes + 2 * margin
    steps = rows // 8
    pad = 8
    for t in range(2):
        for p in range(margin):
            a0[t, p] = low_ref[t, p].astype(jnp.float32)
            a0[t, margin + planes + p] = high_ref[t, p].astype(jnp.float32)
        for p in range(planes):
            a0[t, margin + p] = own_ref[t, p]

    def split_lanes(source, lo, hi, lo_planes, hi_planes, offset):
        def step(j, carry):
            y = pl.multiple_of(j * 8, 8)
            for t in range(2):
                for p in lo_planes:
                    v = source[t, p, pl.ds(y, 8), :]
                    s = pltpu.roll(v, width - offset, 1)
                    lo[t, p, pl.ds(y, 8), :] = v + s
                    if p in hi_planes:
                        hi[t, p, pl.ds(y, 8), :] = v - s
            return carry

        lax.fori_loop(0, steps, step, 0)
        for t in range(2):
            for p in lo_planes:
                lo[t, p, rows : rows + 8] = lo[t, p, 0:8]
                if p in hi_planes:
                    hi[t, p, rows : rows + 8] = hi[t, p, 0:8]

    def detail_step(y, lo, hi, offset, level, first, last, coarse):
        for x_band, source in ((0, lo), (1, hi)):
            merged = []
            for y_band in range(2):
                band = x_band + 2 * y_band
                v = {}
                for p in range(first, last + offset + 1):
                    for t in range(2):
                        here = source[t, p, pl.ds(y, 8), :]
                        there = source[t, p, pl.ds(y + offset, 8), :]
                        v[p, t] = here + there if y_band == 0 else here - there
                plus, minus = {}, {}
                for p in range(first, last + 1):
                    high = removed(
                        v[p, 0] - v[p + offset, 0], v[p, 1] - v[p + offset, 1], limits_ref[level, band + 3]
                    )
                    if band:
                        low = removed(
                            v[p, 0] + v[p + offset, 0], v[p, 1] + v[p + offset, 1], limits_ref[level, band - 1]
                        )
                    elif coarse is not None:
                        low = (coarse[0, p, pl.ds(y, 8), :], coarse[1, p, pl.ds(y, 8), :])
                    else:
                        low = None
                    for t in range(2):
                        plus[p, t] = high[t] if low is None else low[t] + high[t]
                        minus[p, t] = -high[t] if low is None else low[t] - high[t]
                merged.append(
                    {
                        (p, t): plus[p, t] + minus[p - offset, t]
                        for p in range(first + offset, last + 1)
                        for t in range(2)
                    }
                )
            for p, t in merged[0]:
                sums[x_band, t, p, pl.ds(y, 8), :] = merged[0][p, t] + merged[1][p, t]
                diffs[x_band, t, p, pl.ds(y + pad, 8), :] = merged[0][p, t] - merged[1][p, t]

    def wrap_diffs(merged_planes):
        for x_band in range(2):
            for t in range(2):
                for p in merged_planes:
                    diffs[x_band, t, p, 0:pad] = diffs[x_band, t, p, rows : rows + pad]

    def merged_rows(y, t, p, offset):
        lower = sums[0, t, p, pl.ds(y, 8), :] + diffs[0, t, p, pl.ds(y + pad - offset, 8), :]
        upper = sums[1, t, p, pl.ds(y, 8), :] + diffs[1, t, p, pl.ds(y + pad - offset, 8), :]
        return lower + upper + pltpu.roll(lower - upper, offset, 1)

    split_lanes(a0, lo0, hi0, range(count), range(2, planes + 4), 1)

    def coarse_step(j, carry):
        y = pl.multiple_of(j * 8, 8)
        for t in range(2):
            v = [lo0[t, p, pl.ds(y, 8), :] + lo0[t, p, pl.ds(y + 1, 8), :] for p in range(count)]
            for p in range(count - 1):
                w = v[p] + v[p + 1]
                a1[t, p, pl.ds(y, 8), :] = w
        return carry

    lax.fori_loop(0, steps, coarse_step, 0)

    split_lanes(a1, lo1, hi1, range(count - 1), range(count - 1), 2)

    def level_one(j, carry):
        detail_step(pl.multiple_of(j * 8, 8), lo1, hi1, 2, 1, 0, planes + 2, None)
        return carry

    lax.fori_loop(0, steps, level_one, 0)
    wrap_diffs(range(2, planes + 3))

    def level_one_merge(j, carry):
        y = pl.multiple_of(j * 8, 8)
        for t in range(2):
            for p in range(2, planes + 3):
                a1[t, p, pl.ds(y, 8), :] = merged_rows(y, t, p, 2) * (1.0 / 64.0)
        return carry

    lax.fori_loop(0, steps, level_one_merge, 0)

    def level_zero(j, carry):
        detail_step(pl.multiple_of(j * 8, 8), lo0, hi0, 1, 0, 2, planes + 2, a1)
        return carry

    lax.fori_loop(0, steps, level_zero, 0)
    wrap_diffs(range(3, planes + 3))

    def level_zero_merge(j, carry):
        y = pl.multiple_of(j * 8, 8)
        for t in range(2):
            for p in range(planes):
                value = a0[t, margin + p, pl.ds(y, 8), :] - merged_rows(y, t, margin + p, 1) * (1.0 / 64.0)
                out_ref[t, pl.ds(y * planes + p, 8, stride=planes), :] = value
        return carry

    lax.fori_loop(0, steps, level_zero_merge, 0)


def whole(array):
    shape = array.shape
    return pl.BlockSpec(shape, lambda *_: (0,) * len(shape))


def shrink(own, low, high, thresholds):
    _, planes, rows, width = own.shape
    margin = low.shape[1]
    count = planes + 2 * margin
    scale = np.array([[2.0 ** (1.5 * (level + 1))] for level in range(thresholds.shape[0])], np.float32)
    limits = thresholds * scale
    f32 = jnp.float32
    buffers = [
        pltpu.VMEM((2, count, rows, width), f32),
        pltpu.VMEM((2, count, rows + 8, width), f32),
        pltpu.VMEM((2, count, rows + 8, width), f32),
        pltpu.VMEM((2, count, rows, width), f32),
        pltpu.VMEM((2, count, rows + 8, width), f32),
        pltpu.VMEM((2, count, rows + 8, width), f32),
        pltpu.VMEM((2, 2, count, rows, width), f32),
        pltpu.VMEM((2, 2, count, rows + 8, width), f32),
    ]

    def kernel(*refs):
        wavelet_kernel(planes, *refs)

    return pl.pallas_call(
        kernel,
        out_shape=jax.ShapeDtypeStruct((2, rows * planes, width), f32),
        in_specs=[
            pl.BlockSpec(memory_space=pltpu.VMEM),
            pl.BlockSpec(memory_space=pltpu.VMEM),
            pl.BlockSpec(memory_space=pltpu.VMEM),
            pl.BlockSpec(memory_space=pltpu.SMEM),
        ],
        out_specs=pl.BlockSpec(memory_space=pltpu.VMEM),
        scratch_shapes=buffers,
        name="wavelet",
    )(own, low, high, limits)


def local(image, sens, measured, mask, thresholds):
    _, phase_cells, planes, width = image.shape
    coils = sens.shape[1]
    lines, depth_cells = measured.shape[2], measured.shape[3]
    devices = lax.axis_size(lines_axes)
    group = lines * planes
    per_chunk = coils // chunk_count
    bf16, f32 = jnp.bfloat16, jnp.float32

    order = (np.arange(devices)[None, :] * lines + np.arange(lines)[:, None]).reshape(-1)
    table_phase = fourier_table(phase_cells, -1.0, rows=order)
    inverse_phase = fourier_table(phase_cells, 1.0, columns=order)
    table_depth = fourier_table(depth_cells, -1.0)
    inverse_depth = fourier_table(depth_cells, 1.0)
    inverse_readout = fourier_table(width, 1.0).T.reshape(2, width, 2, width)

    image_rows = image.reshape(2, phase_cells * planes, width)
    sens_rows = sens.reshape(2, coils, phase_cells * planes, width)
    block = (devices, 2, 1, group, width)
    exchanged = jax.ShapeDtypeStruct((devices, 2, per_chunk, group, width), bf16)
    exchanged_spec = pl.BlockSpec(block, lambda c: (0, 0, c, 0, 0))
    plane_shape = (2, planes, phase_cells, width)

    def forward(chunk):
        def kernel(*refs):
            forward_kernel(devices, lines, planes, *refs)

        return pl.pallas_call(
            kernel,
            grid=(per_chunk,),
            out_shape=exchanged,
            in_specs=[
                pl.BlockSpec((2, 1, phase_cells * planes, width), lambda c: (0, c + chunk * per_chunk, 0, 0)),
                whole(image_rows),
                whole(table_phase),
            ],
            out_specs=exchanged_spec,
            scratch_shapes=[pltpu.VMEM((2, phase_cells * planes, width), f32)] * 2,
            name="forward",
        )(sens_rows, image_rows, table_phase)

    def middle(received, own_measured, wide_mask, chunk):
        def kernel(*refs):
            middle_kernel(lines, *refs)

        return pl.pallas_call(
            kernel,
            grid=(per_chunk,),
            out_shape=exchanged,
            in_specs=[
                exchanged_spec,
                pl.BlockSpec((2, 1, lines, depth_cells, width), lambda c: (0, c + chunk * per_chunk, 0, 0, 0)),
                whole(wide_mask),
                whole(table_depth),
                whole(inverse_depth),
            ],
            out_specs=exchanged_spec,
            scratch_shapes=[pltpu.VMEM((2, depth_cells * lines, width), f32)] * 2,
            name="middle",
        )(received, own_measured, wide_mask, table_depth, inverse_depth)

    def backward(received, chunk, first):
        specs = [
            exchanged_spec,
            pl.BlockSpec((2, 1, phase_cells * planes, width), lambda c: (0, c + chunk * per_chunk, 0, 0)),
            whole(inverse_phase),
        ]
        operands = [received, sens_rows, inverse_phase]
        if first is None:

            def kernel(*refs):
                backward_kernel(lines, planes, None, *refs)

        else:
            specs.insert(0, whole(first))
            operands.insert(0, first)

            def kernel(*refs):
                backward_kernel(lines, planes, *refs)

        return pl.pallas_call(
            kernel,
            grid=(per_chunk,),
            out_shape=jax.ShapeDtypeStruct(plane_shape, bf16 if chunk == chunk_count - 1 else f32),
            in_specs=specs,
            out_specs=pl.BlockSpec(plane_shape, lambda c: (0, 0, 0, 0)),
            scratch_shapes=[pltpu.VMEM((2, phase_cells * planes, width), f32)] * 2
            + [pltpu.VMEM(plane_shape, f32)],
            name="backward",
        )(*operands)

    def exchange(values):
        return lax.all_to_all(values, lines_axes, 0, 0, tiled=True)

    received = [exchange(forward(chunk)) for chunk in range(chunk_count)]
    own_measured = jnp.einsum(
        "tclzk,tksx->sclzx", measured, inverse_readout, preferred_element_type=f32
    ).astype(bf16)
    wide_mask = jnp.broadcast_to(mask.astype(f32)[:, :, None], (lines, depth_cells, width))
    image_planes = jnp.transpose(image, (0, 2, 1, 3))
    returned = [
        exchange(middle(received[chunk], own_measured, wide_mask, chunk)) for chunk in range(chunk_count)
    ]
    total = None
    for chunk in range(chunk_count):
        total = backward(returned[chunk], chunk, total)

    size = lax.axis_size("coil")
    copies = lax.all_to_all(jnp.broadcast_to(total[None], (size, *total.shape)), "coil", 0, 0, tiled=True)
    gradient = copies.astype(f32).sum(axis=0)
    own = image_planes - step_size * gradient
    margin = 2 ** thresholds.shape[0] - 1
    up = [(i, (i + 1) % devices) for i in range(devices)]
    down = [(target, source) for source, target in up]
    narrow = own.astype(bf16)
    low = lax.ppermute(narrow[:, planes - margin :], lines_axes, up)
    high = lax.ppermute(narrow[:, :margin], lines_axes, down)
    result = shrink(own, low, high, thresholds)
    return result.reshape(2, phase_cells, planes, width)


def solution(mesh):
    return jax.shard_map(
        local,
        mesh=mesh,
        in_specs=(
            P("groups", None, lines_axes, None),
            P("groups", "coil", None, lines_axes, None),
            P("groups", "coil", lines_axes, None, None),
            P(lines_axes, None),
            P(),
        ),
        out_specs=P("groups", None, lines_axes, None),
        check_vma=False,
    )
```

time: 370 us -> 328 us (0.89)
  other arithmetic: 52.7 us -> 1.71 us
  Pallas kernels: 0 us -> 25.1 us
  local copies, waits for them, and re-layouts: 15.9 us -> 3.93 us
  blocking collectives: 142 us -> 134 us
  starting transfers between devices: 46.3 us -> 50.5 us
  matrix products: 5.47 us -> 1.44 us
  waiting for transfers between devices: 106 us -> 110 us
    mul x15 -> x1, other arithmetic: 34.3 us -> 0.65 us  [shrink(): limits = thresholds * scale]
    pallas_call x0 -> x4, Pallas kernels: none -> 25.1 us  [the longest x1 10.9 us: shrink(): pl.pallas_call(kernel, out_shape=jax.ShapeDtypeStruct((2, rows * planes,...]
    all_to_all x4 -> x2, blocking collectives: 142 us -> 134 us  [the longest x1 117 us: exchange(): return lax.all_to_all(values, lines_axes, 0, 0, tiled=True)]
    all_to_all x1, waiting for transfers between devices: 100 us -> 108 us  [exchange(): return lax.all_to_all(values, lines_axes, 0, 0, tiled=True)]
    another operation x10 -> x0, other arithmetic: 6.18 us -> none
    sub x6 -> x0, other arithmetic: 6.12 us -> none  [merge_bands(): return (lower + upper + before(lower - upper, along, offset)) * quarter_root]
    slice x17 -> x1, local copies, waits for them, and re-layouts: 4.27 us -> 0.05 us  [local(): high = lax.ppermute(narrow[:, :margin], lines_axes, down)]
    dot_general x4 -> x1, matrix products: 5.47 us -> 1.44 us  [local(): jnp.einsum('tclzk,tksx->sclzx', measured, inverse_readout, preferred_elem...]
  transfers between devices with their start and end apart: 3 -> 3, of which waited for: 3 -> 2; matrix products, arithmetic and copies ran while one was open for 1% -> 1% of each run, Pallas kernels for 0% -> 0%
where the time goes in v1:
time: 328 us; the launch traced here: 327 us
  blocking collectives  134 us (41%)
  waiting for transfers between devices  110 us (34%)
  starting transfers between devices  50.5 us (15%)
  Pallas kernels  25.1 us (8%)
  local copies, waits for them, and re-layouts  3.93 us (1%)
    all_to_all x1, blocking collectives, exchange(): return lax.all_to_all(values, lines_axes, 0, 0, tiled=True)  117 us
    all_to_all x1, waiting for transfers between devices, exchange(): return lax.all_to_all(values, lines_axes, 0, 0, tiled=True)  108 us
    all_to_all x1, starting transfers between devices, exchange(): return lax.all_to_all(values, lines_axes, 0, 0, tiled=True)  47.5 us
    all_to_all x1, blocking collectives, local(): lax.all_to_all(jnp.broadcast_to(total[None], (size, *total.shape)), 'coil...  17.8 us
    pallas_call x1, Pallas kernels, shrink(): pl.pallas_call(kernel, out_shape=jax.ShapeDtypeStruct((2, rows * planes,...  10.9 us
  transfers between devices with their start and end apart: 3, of which 2 were waited for; matrix products, arithmetic and copies ran while one was open for 1% of the time, Pallas kernels for 0%

profile of v1, /device:TPU:40, one launch (start us, length us, event | category | flops | bytes accessed | tf_op | source)
XLA Modules:
  0.0 327.4 jit_solution(14920924026501415782)
XLA Ops:
  0.0 4.3 %forward.1 = bf16[64,2,4,8,128]{4,3,2,1,0:T(8,128)(2,1)} custom-call(bf16[2,4,512,128]{3,2,1,0:T(8,128)(2,1)} %bitcast.19, f32[2,512,128]{2,1,0:T(8,128)} %bitcast.21, bf16[256,256]{1,0:T(8,128)(2,1)} %constant.16.clone.refs_2_), custom_call_target="tpu_custom_call" | custom-call | tf_op jit(solution)/shard_map/forward/pallas_call | solution.py:336
  4.3 0.0 copy-start.6
  4.3 0.0 copy-start.2
  4.3 0.0 copy-start.5
  4.3 47.5 %all-to-all-start = ((bf16[64,2,4,8,128]{4,3,2,1,0:T(8,128)(2,1)}), bf16[64,2,4,8,128]{4,3,2,1,0:T(8,128)(2,1)S(1)}, u32[]{:S(2)}, u32[]{:S(2)}) async-start(bf16[64,2,4,8,128]{4,3,2,1,0:T(8,128)(2,1)} %forward.1), calls=%async_computation | async-start | bytes 2097152 | tf_op jit(solution)/shard_map/all_to_all | solution.py:401
  51.8 0.0 copy-done.6
  51.8 0.0 copy-done.2
  51.9 0.0 copy-done.5
  51.9 1.4 fusion.refs_1_
  53.3 107.7 %all-to-all-done.refs_0_ = bf16[64,2,4,8,128]{4,3,2,1,0:T(8,128)(2,1)S(1)} async-done(((bf16[64,2,4,8,128]{4,3,2,1,0:T(8,128)(2,1)}), bf16[64,2,4,8,128]{4,3,2,1,0:T(8,128)(2,1)S(1)}, u32[]{:S(2)}, u32[]{:S(2)}) %all-to-all-start) | async-done | bytes 1048608 | tf_op jit(solution)/shard_map/all_to_all | solution.py:401
  161.0 0.0 copy-start
  161.0 1.0 broadcast_in_dim.4.refs_2_
  162.0 0.1 copy-done
  162.0 5.9 %middle.1 = bf16[64,2,4,8,128]{4,3,2,1,0:T(8,128)(2,1)} custom-call(bf16[64,2,4,8,128]{4,3,2,1,0:T(8,128)(2,1)} %copy-done, bf16[2,4,2,256,128]{4,3,2,1,0:T(8,128)(2,1)} %fusion.refs_1_, f32[2,256,128]{2,1,0:T(8,128)} %broadcast_in_dim.4.refs_2_, bf16[512,512]{1,0:T(8,128)(2,1)} %constant.18.clone.refs_3_, bf16[512,512]{1,0:T(8,128)(2,1)} %constant.19.clone.refs_4_), custom_call_target="tpu_custom_call" | custom-call | tf_op jit(solution)/shard_map/middle/pallas_call | solution.py:354
  167.9 116.5 %all_to_all.15.refs_0_ = bf16[64,2,4,8,128]{4,3,2,1,0:T(8,128)(2,1)} all-to-all(bf16[64,2,4,8,128]{4,3,2,1,0:T(8,128)(2,1)} %middle.1), channel_id=1, replica_groups=mesh['groups'=2,'slab'=32,'coil'=4,'row'=2] {'slab','row'}, dimensions={0} | all-to-all | bytes 2097152 | tf_op jit(solution)/shard_map/all_to_all | solution.py:401
  284.4 4.0 %backward.1 = bf16[2,4,128,128]{3,2,1,0:T(8,128)(2,1)} custom-call(bf16[64,2,4,8,128]{4,3,2,1,0:T(8,128)(2,1)} %all_to_all.15.refs_0_, bf16[2,4,512,128]{3,2,1,0:T(8,128)(2,1)} %bitcast.20, bf16[256,256]{1,0:T(8,128)(2,1)} %constant.20.clone.refs_2_), custom_call_target="tpu_custom_call" | custom-call | tf_op jit(solution)/shard_map/backward/pallas_call | solution.py:389
  288.4 1.2 broadcast_in_dim.5
  289.6 17.8 %all_to_all.16 = bf16[4,2,4,128,128]{4,3,2,1,0:T(8,128)(2,1)S(1)} all-to-all(bf16[4,2,4,128,128]{4,3,2,1,0:T(8,128)(2,1)S(1)} %broadcast_in_dim.5), channel_id=1, replica_groups=mesh['groups'=2,'slab'=32,'coil'=4,'row'=2] {'coil'}, dimensions={0} | all-to-all | bytes 2097152 | tf_op jit(solution)/shard_map/all_to_all | solution.py:417
  307.4 0.0 copy-start.1
  307.4 0.2 convert_reduce_fusion
  307.5 0.9 copy-done.1
  308.4 0.0 copy-start.7
  308.4 0.0 copy-start.8
  308.4 0.9 fusion.3
  309.3 0.1 fusion.4
  309.4 0.1 collective-permute-start
  309.5 2.9 collective-permute-start.1
  312.4 0.0 copy-done.7
  312.4 0.0 copy-done.8
  312.4 0.6 broadcast_multiply_fusion.refs_3_
  313.0 2.7 collective-permute-done.refs_1_
  315.7 0.0 copy-start.3
  315.7 0.0 collective-permute-done.1.refs_2_
  315.7 0.0 copy-start.4
  315.7 0.7 copy-done.3
  316.4 0.1 copy-done.4
  316.5 10.9 %wavelet.1 = f32[2,512,128]{2,1,0:T(8,128)} custom-call(f32[2,4,128,128]{3,2,1,0:T(8,128)} %get-tuple-element.6.refs_0_, bf16[2,3,128,128]{3,2,1,0:T(8,128)(2,1)} %copy-done.3, bf16[2,3,128,128]{3,2,1,0:T(8,128)(2,1)} %copy-done.4, f32[2,7]{1,0:T(2,128)} %broadcast_multiply_fusion.refs_3_), custom_call_target="tpu_custom_call" | custom-call | tf_op jit(solution)/shard_map/wavelet/pallas_call | solution.py:294
  (1 shorter events, 0.0 us)
Async XLA Ops:
  4.3 47.5 %copy-start.6 = (s32[2,256]{1,0:T(2,128)S(1)}, s32[2,256]{1,0:T(2,128)}, u32[]{:S(2)}) copy-start(s32[2,256]{1,0:T(2,128)} %param.14) | copy-start | bytes 6148
  4.3 47.5 %copy-start.2 = (bf16[2,4,2,256,128]{4,3,2,1,0:T(8,128)(2,1)S(1)}, bf16[2,4,2,256,128]{4,3,2,1,0:T(8,128)(2,1)}, u32[]{:S(2)}) copy-start(bf16[2,4,2,256,128]{4,3,2,1,0:T(8,128)(2,1)} %param.13) | copy-start | bytes 3145732
  4.3 47.5 %copy-start.5 = (bf16[2,128,2,128,1,1]{1,3,0,5,4,2:T(8,128)(2,1)S(1)}, bf16[2,128,2,128,1,1]{1,3,0,5,4,2:T(8,128)(2,1)}, u32[]{:S(2)}) copy-start(bf16[2,128,2,128,1,1]{1,3,0,5,4,2:T(8,128)(2,1)} %constant.27) | copy-start | bytes 393220
  4.3 156.6 %all-to-all-start = ((bf16[64,2,4,8,128]{4,3,2,1,0:T(8,128)(2,1)}), bf16[64,2,4,8,128]{4,3,2,1,0:T(8,128)(2,1)S(1)}, u32[]{:S(2)}, u32[]{:S(2)}) async-start(bf16[64,2,4,8,128]{4,3,2,1,0:T(8,128)(2,1)} %forward.1), calls=%async_computation | async-start | bytes 2097152 | tf_op jit(solution)/shard_map/all_to_all | solution.py:401
  161.0 1.1 copy-start
  307.4 1.0 copy-start.1
  308.4 4.0 %copy-start.7 = (f32[2,7]{1,0:T(2,128)S(1)}, f32[2,7]{1,0:T(2,128)}, u32[]{:S(2)}) copy-start(f32[2,7]{1,0:T(2,128)} %param.15) | copy-start | bytes 172
  308.4 4.0 %copy-start.8 = (f32[2]{0:T(128)S(1)}, f32[2]{0:T(128)}, u32[]{:S(2)}) copy-start(f32[2]{0:T(128)} %constant.26) | copy-start | bytes 28
  309.4 6.4 %collective-permute-start = (bf16[2,3,128,128]{3,2,1,0:T(8,128)(2,1)S(1)}, bf16[2,3,128,128]{3,2,1,0:T(8,128)(2,1)S(1)}, u32[]{:S(2)}, u32[]{:S(2)}) collective-permute-start(bf16[2,3,128,128]{3,2,1,0:T(8,128)(2,1)S(1)} %get-tuple-element.8), channel_id=1, source_target_pairs={{0,1},{1,8},{8,9},{9,16},{16,17},{17,24},{24,25},{25,32},{32,33},{... | collective-permute-start | bytes 589832 | tf_op jit(solution)/shard_map/ppermute | solution.py:424
  309.5 6.3 %collective-permute-start.1 = (bf16[2,3,128,128]{3,2,1,0:T(8,128)(2,1)S(1)}, bf16[2,3,128,128]{3,2,1,0:T(8,128)(2,1)S(1)}, u32[]{:S(2)}, u32[]{:S(2)}) collective-permute-start(bf16[2,3,128,128]{3,2,1,0:T(8,128)(2,1)S(1)} %get-tuple-element.7), channel_id=1, source_target_pairs={{1,0},{8,1},{9,8},{16,9},{17,16},{24,17},{25,24},{32,25},{33,32},{... | collective-permute-start | bytes 589832 | tf_op jit(solution)/shard_map/ppermute | solution.py:425
  315.7 0.7 copy-start.3
  315.7 0.7 copy-start.4

commit v2 on v1

v2 whole, which is shorter than its diff:
```python
import math

import jax
import jax.numpy as jnp
import ml_dtypes
import numpy as np
from jax import lax
from jax.experimental import pallas as pl
from jax.experimental.pallas import tpu as pltpu
from jax.sharding import PartitionSpec as P

step_size = 0.5
lines_axes = ("slab", "row")
pause_steps = 6500


def fourier_table(length, sign, rows=None, columns=None):
    index = np.arange(length, dtype=np.int64)
    phase = (index[:, None] * index[None, :]) % length
    theta = phase.astype(np.float32) * np.float32(2.0 * math.pi / length)
    scale = np.float32(1.0 / math.sqrt(length))
    real = (np.cos(theta) * scale).astype(np.float32)
    imaginary = (np.sin(theta) * np.float32(sign) * scale).astype(np.float32)
    if rows is not None:
        real, imaginary = real[rows], imaginary[rows]
    if columns is not None:
        real, imaginary = real[:, columns], imaginary[:, columns]
    return np.block([[real, -imaginary], [imaginary, real]]).astype(ml_dtypes.bfloat16)


def dot(left, right):
    return jnp.dot(left, right, preferred_element_type=jnp.float32)


def forward_kernel(slabs, lines, planes, sens_ref, image_ref, table_ref, out_ref, product, mixed):
    cells = product.shape[1] // planes
    group = lines * planes
    sr = sens_ref[0, 0].astype(jnp.float32)
    si = sens_ref[1, 0].astype(jnp.float32)
    ir = image_ref[0]
    ii = image_ref[1]
    product[0] = sr * ir - si * ii
    product[1] = sr * ii + si * ir
    columns = [
        jnp.concatenate(
            [product[t, pl.ds(z, cells, stride=planes), :].astype(jnp.bfloat16) for t in range(2)],
            axis=0,
        )
        for z in range(planes)
    ]
    done = dot(table_ref[...], jnp.concatenate(columns, axis=1))
    width = product.shape[2]
    for s in range(2):
        for z in range(planes):
            for line in range(lines):
                first = s * cells + line * slabs
                mixed[s, pl.ds(z * lines + line, slabs, stride=group), :] = done[
                    first : first + slabs, z * width : (z + 1) * width
                ]
        out_ref[:, s, 0] = mixed[s].astype(jnp.bfloat16).reshape(slabs, group, width)


def middle_kernel(lines, lower_ref, upper_ref, measured_ref, mask_ref, table_ref, inverse_ref, out_ref, mixed, back):
    slabs, _, _, _, group, width = lower_ref.shape
    half = slabs * group // lines
    cells = 2 * half
    for row, ref in enumerate((lower_ref, upper_ref)):
        for t in range(2):
            mixed[row, t] = ref[:, 0, t, 0].astype(jnp.float32).reshape(slabs * group, width)
    columns = [
        jnp.concatenate(
            [
                mixed[row, t, pl.ds(line, half, stride=lines), :].astype(jnp.bfloat16)
                for t in range(2)
                for row in range(2)
            ],
            axis=0,
        )
        for line in range(lines)
    ]
    spectrum = dot(table_ref[...], jnp.concatenate(columns, axis=1))
    residual = []
    for line in range(lines):
        parts = []
        for t in range(2):
            value = spectrum[t * cells : (t + 1) * cells, line * width : (line + 1) * width]
            value = mask_ref[line] * (value - measured_ref[t, 0, line].astype(jnp.float32))
            parts.append(value.astype(jnp.bfloat16))
        residual.append(jnp.concatenate(parts, axis=0))
    result = dot(inverse_ref[...], jnp.concatenate(residual, axis=1))
    for row in range(2):
        for s in range(2):
            first = s * cells + row * half
            for line in range(lines):
                back[row, s, pl.ds(line, half, stride=lines), :] = result[
                    first : first + half, line * width : (line + 1) * width
                ]
            out_ref[:, row, s, 0] = back[row, s].astype(jnp.bfloat16).reshape(slabs, group, width)


def backward_kernel(lines, planes, edge, in_ref, sens_ref, table_ref, out_ref, mixed, wide, total, framed):
    slabs, rows, _, _, group, width = in_ref.shape
    cells = slabs * lines
    coil = pl.program_id(0)

    @pl.when(coil == 0)
    def _():
        total[...] = jnp.zeros(total.shape, jnp.float32)

    for row in range(rows):
        for t in range(2):
            mixed[row, t] = in_ref[:, row, t, 0].astype(jnp.float32).reshape(slabs * group, width)
            wide[row, t] = sens_ref[t, 0, row].astype(jnp.float32)
    columns = [
        jnp.concatenate(
            [
                mixed[row, t, pl.ds(z * lines + line, slabs, stride=group), :].astype(jnp.bfloat16)
                for t in range(2)
                for line in range(lines)
            ],
            axis=0,
        )
        for row in range(rows)
        for z in range(planes)
    ]
    done = dot(table_ref[...], jnp.concatenate(columns, axis=1))
    for row in range(rows):
        for z in range(planes):
            plane = row * planes + z
            rr = done[:cells, plane * width : (plane + 1) * width]
            ri = done[cells:, plane * width : (plane + 1) * width]
            sr = wide[row, 0, pl.ds(z, cells, stride=planes), :]
            si = wide[row, 1, pl.ds(z, cells, stride=planes), :]
            total[row, 0, z] += sr * rr + si * ri
            total[row, 1, z] += sr * ri - si * rr

    @pl.when(coil == pl.num_programs(0) - 1)
    def _():
        pieces, _, _, tall, _ = out_ref.shape
        step = tall - 2 * edge
        for row in range(rows):
            for t in range(2):
                for z in range(planes):
                    framed[0:edge] = total[row, t, z, cells - edge : cells]
                    framed[edge : edge + cells] = total[row, t, z]
                    framed[edge + cells :] = total[row, t, z, 0:edge]
                    for q in range(pieces // rows):
                        out_ref[q * rows + row, t, z] = framed[q * step : q * step + tall].astype(out_ref.dtype)


def removed(real, imaginary, limit):
    factor = jnp.minimum(lax.rsqrt(real * real + imaginary * imaginary) * limit, 1.0)
    return real * factor, imaginary * factor


def wavelet_kernel(edge, image_ref, own_ref, low_ref, high_ref, limits_ref, out_ref, a0, lo0, hi0, a1, lo1, hi1, sums, diffs, mixed):
    planes, rows, width = own_ref.shape[1:]
    margin = low_ref.shape[1]
    count = planes + 2 * margin
    steps = rows // 8
    pad = 8
    for t in range(2):
        for p in range(margin):
            a0[t, p] = low_ref[t, p].astype(jnp.float32)
            a0[t, margin + planes + p] = high_ref[t, p].astype(jnp.float32)
        for p in range(planes):
            a0[t, margin + p] = own_ref[t, p]

    def split_lanes(source, lo, hi, lo_planes, hi_planes, offset):
        def step(j, carry):
            y = pl.multiple_of(j * 8, 8)
            for t in range(2):
                for p in lo_planes:
                    v = source[t, p, pl.ds(y, 8), :]
                    s = pltpu.roll(v, width - offset, 1)
                    lo[t, p, pl.ds(y, 8), :] = v + s
                    if p in hi_planes:
                        hi[t, p, pl.ds(y, 8), :] = v - s
            return carry

        lax.fori_loop(0, steps, step, 0)

    def detail_step(y, lo, hi, offset, level, first, last, coarse):
        for x_band, source in ((0, lo), (1, hi)):
            merged = []
            for y_band in range(2):
                band = x_band + 2 * y_band
                v = {}
                for p in range(first, last + offset + 1):
                    for t in range(2):
                        here = source[t, p, pl.ds(y, 8), :]
                        there = source[t, p, pl.ds(y + offset, 8), :]
                        v[p, t] = here + there if y_band == 0 else here - there
                plus, minus = {}, {}
                for p in range(first, last + 1):
                    high = removed(
                        v[p, 0] - v[p + offset, 0], v[p, 1] - v[p + offset, 1], limits_ref[level, band + 3]
                    )
                    if band:
                        low = removed(
                            v[p, 0] + v[p + offset, 0], v[p, 1] + v[p + offset, 1], limits_ref[level, band - 1]
                        )
                    elif coarse is not None:
                        low = (coarse[0, p, pl.ds(y, 8), :], coarse[1, p, pl.ds(y, 8), :])
                    else:
                        low = None
                    for t in range(2):
                        plus[p, t] = high[t] if low is None else low[t] + high[t]
                        minus[p, t] = -high[t] if low is None else low[t] - high[t]
                merged.append(
                    {
                        (p, t): plus[p, t] + minus[p - offset, t]
                        for p in range(first + offset, last + 1)
                        for t in range(2)
                    }
                )
            for p, t in merged[0]:
                sums[x_band, t, p, pl.ds(y, 8), :] = merged[0][p, t] + merged[1][p, t]
                diffs[x_band, t, p, pl.ds(y + pad, 8), :] = merged[0][p, t] - merged[1][p, t]

    def merged_rows(y, t, p, offset):
        lower = sums[0, t, p, pl.ds(y, 8), :] + diffs[0, t, p, pl.ds(y + pad - offset, 8), :]
        upper = sums[1, t, p, pl.ds(y, 8), :] + diffs[1, t, p, pl.ds(y + pad - offset, 8), :]
        return lower + upper + pltpu.roll(lower - upper, offset, 1)

    split_lanes(a0, lo0, hi0, range(count), range(2, planes + 4), 1)

    def coarse_step(j, carry):
        y = pl.multiple_of(j * 8, 8)
        for t in range(2):
            v = [lo0[t, p, pl.ds(y, 8), :] + lo0[t, p, pl.ds(y + 1, 8), :] for p in range(count)]
            for p in range(count - 1):
                w = v[p] + v[p + 1]
                a1[t, p, pl.ds(y, 8), :] = w
        return carry

    lax.fori_loop(0, steps, coarse_step, 0)

    split_lanes(a1, lo1, hi1, range(count - 1), range(count - 1), 2)

    def level_one(j, carry):
        detail_step(pl.multiple_of(j * 8, 8), lo1, hi1, 2, 1, 0, planes + 2, None)
        return carry

    lax.fori_loop(0, steps, level_one, 0)

    def level_one_merge(j, carry):
        y = pl.multiple_of(j * 8, 8)
        for t in range(2):
            for p in range(2, planes + 3):
                a1[t, p, pl.ds(y, 8), :] = merged_rows(y, t, p, 2) * (1.0 / 64.0)
        return carry

    lax.fori_loop(0, steps, level_one_merge, 0)

    def level_zero(j, carry):
        detail_step(pl.multiple_of(j * 8, 8), lo0, hi0, 1, 0, 2, planes + 2, a1)
        return carry

    lax.fori_loop(0, steps, level_zero, 0)

    def level_zero_merge(j, carry):
        y = pl.multiple_of(j * 8, 8)
        for t in range(2):
            for p in range(planes):
                change = own_ref[t, p, pl.ds(y, 8), :] - image_ref[t, p, pl.ds(y, 8), :]
                change = change - merged_rows(y, t, margin + p, 1) * (1.0 / 64.0)
                mixed[t, pl.ds(y * planes + p, 8, stride=planes), :] = change
        return carry

    lax.fori_loop(0, steps, level_zero_merge, 0)
    for t in range(2):
        kept = mixed[t, edge * planes : (rows - edge) * planes].astype(out_ref.dtype)
        for copy in range(out_ref.shape[0]):
            out_ref[copy, t] = kept


def whole(array):
    shape = array.shape
    return pl.BlockSpec(shape, lambda *_: (0,) * len(shape))


def shrink(image, own, low, high, thresholds, edge, copies):
    _, planes, rows, width = own.shape
    margin = low.shape[1]
    count = planes + 2 * margin
    scale = np.array([[2.0 ** (1.5 * (level + 1))] for level in range(thresholds.shape[0])], np.float32)
    limits = thresholds * scale
    f32 = jnp.float32
    buffers = [
        pltpu.VMEM((2, count, rows, width), f32),
        pltpu.VMEM((2, count, rows + 8, width), f32),
        pltpu.VMEM((2, count, rows + 8, width), f32),
        pltpu.VMEM((2, count, rows, width), f32),
        pltpu.VMEM((2, count, rows + 8, width), f32),
        pltpu.VMEM((2, count, rows + 8, width), f32),
        pltpu.VMEM((2, 2, count, rows, width), f32),
        pltpu.VMEM((2, 2, count, rows + 8, width), f32),
        pltpu.VMEM((2, rows * planes, width), f32),
    ]

    def kernel(*refs):
        wavelet_kernel(edge, *refs)

    return pl.pallas_call(
        kernel,
        out_shape=jax.ShapeDtypeStruct((copies, 2, (rows - 2 * edge) * planes, width), jnp.bfloat16),
        in_specs=[pl.BlockSpec(memory_space=pltpu.VMEM)] * 4 + [pl.BlockSpec(memory_space=pltpu.SMEM)],
        out_specs=pl.BlockSpec(memory_space=pltpu.VMEM),
        scratch_shapes=buffers,
        name="wavelet",
    )(image, own, low, high, limits)


def local(image, sens, measured, mask, thresholds):
    _, phase_cells, planes, width = image.shape
    coils = sens.shape[1]
    own_lines, depth_cells = measured.shape[2], measured.shape[3]
    slabs, rows, columns = (lax.axis_size(name) for name in ("slab", "row", "coil"))
    row = lax.axis_index("row")
    lines = own_lines * rows
    group = lines * planes
    half = coils // rows
    bf16, f32 = jnp.bfloat16, jnp.float32
    other = [(0, 1), (1, 0)]

    order = (np.arange(slabs)[None, :] * lines + np.arange(lines)[:, None]).reshape(-1)
    depth_order = np.arange(depth_cells).reshape(slabs, rows, planes).transpose(1, 0, 2).reshape(-1)
    table_phase = fourier_table(phase_cells, -1.0, rows=order)
    inverse_phase = fourier_table(phase_cells, 1.0, columns=order)
    table_depth = fourier_table(depth_cells, -1.0, columns=depth_order)
    inverse_depth = fourier_table(depth_cells, 1.0, rows=depth_order)
    inverse_readout = fourier_table(width, 1.0).T.reshape(2, width, 2, width)

    image_rows = image.reshape(2, phase_cells * planes, width)
    sens_rows = sens.reshape(2, coils, phase_cells * planes, width)
    sens_spec = (2, 1, phase_cells * planes, width)
    piece = (slabs, 2, half, group, width)
    exchanged = jax.ShapeDtypeStruct((slabs, rows, 2, half, group, width), bf16)
    stack = pltpu.VMEM((2, phase_cells * planes, width), f32)
    here = row.astype(jnp.int32).reshape(1)

    def given(kernel, grid_spec, out_shape, name):
        return pl.pallas_call(kernel, grid_spec=grid_spec, out_shape=out_shape, name=name)

    def send_kernel(_, *refs):
        forward_kernel(slabs, lines, planes, *refs)

    sent = given(
        send_kernel,
        pltpu.PrefetchScalarGridSpec(
            num_scalar_prefetch=1,
            grid=(half,),
            in_specs=[
                pl.BlockSpec(sens_spec, lambda c, r: (0, (1 - r[0]) * half + c, 0, 0)),
                whole(image_rows),
                whole(table_phase),
            ],
            out_specs=pl.BlockSpec((slabs, 2, 1, group, width), lambda c, r: (0, 0, c, 0, 0)),
            scratch_shapes=[stack, stack],
        ),
        jax.ShapeDtypeStruct(piece, bf16),
        "forward_sent",
    )(here, sens_rows, image_rows, table_phase)
    arrived = lax.ppermute(sent, "row", other)

    def keep_kernel(r_ref, sens_ref, image_ref, table_ref, arrived_ref, out_ref, pause_ref, product, mixed):
        @pl.when(pl.program_id(0) == 0)
        def _():
            pause_ref[...] = lax.fori_loop(
                0, r_ref[0] * pause_steps, lambda _, v: v * 1.0001 + 0.5, jnp.ones(pause_ref.shape, jnp.float32)
            )

        forward_kernel(slabs, lines, planes, sens_ref, image_ref, table_ref, out_ref.at[:, 0], product, mixed)
        out_ref[:, 1] = arrived_ref[...]

    outgoing, _ = given(
        keep_kernel,
        pltpu.PrefetchScalarGridSpec(
            num_scalar_prefetch=1,
            grid=(half,),
            in_specs=[
                pl.BlockSpec(sens_spec, lambda c, r: (0, r[0] * half + c, 0, 0)),
                whole(image_rows),
                whole(table_phase),
                pl.BlockSpec((slabs, 2, 1, group, width), lambda c, r: (0, 0, c, 0, 0)),
            ],
            out_specs=[
                pl.BlockSpec((slabs, rows, 2, 1, group, width), lambda c, r: (0, 0, 0, c, 0, 0)),
                pl.BlockSpec((8, 128), lambda c, r: (0, 0)),
            ],
            scratch_shapes=[stack, stack],
        ),
        [exchanged, jax.ShapeDtypeStruct((8, 128), f32)],
        "forward_kept",
    )(here, sens_rows, image_rows, table_phase, arrived)

    received = lax.all_to_all(outgoing, "slab", 0, 0, tiled=True)

    measured, mask, sens_late, image, _ = lax.optimization_barrier((measured, mask, sens_rows, image, outgoing))

    def both_rows(values, axis):
        kept = lax.dynamic_slice_in_dim(values, row * half, half, axis=1)
        away = lax.dynamic_slice_in_dim(values, (1 - row) * half, half, axis=1)
        return in_row_order(kept, lax.ppermute(away, "row", other), axis)

    def in_row_order(own, others, axis):
        first = row == 0
        return jnp.concatenate([jnp.where(first, own, others), jnp.where(first, others, own)], axis=axis)

    own_measured = jnp.einsum(
        "tclzk,tksx->sclzx", measured, inverse_readout, preferred_element_type=f32
    ).astype(bf16)
    chip_measured = both_rows(own_measured, 2)
    own_mask = mask.astype(f32)
    chip_mask = in_row_order(own_mask, lax.ppermute(own_mask, "row", other), 0)
    wide_mask = jnp.broadcast_to(chip_mask[:, :, None], (lines, depth_cells, width))
    chip_sens = both_rows(sens_late[:, :, None], 2)
    edge = 4
    quarter = phase_cells // columns
    image_planes = jnp.transpose(image, (0, 2, 1, 3))
    framed = jnp.concatenate(
        [image_planes[:, :, phase_cells - edge :], image_planes, image_planes[:, :, :edge]], axis=2
    )
    own_image = lax.dynamic_slice_in_dim(
        framed, lax.axis_index("coil") * quarter, quarter + 2 * edge, axis=2
    )

    def mid_kernel(_, *refs):
        middle_kernel(lines, *refs)

    block = (slabs, 1, 2, 1, group, width)
    buffer = pltpu.VMEM((rows, 2, slabs * group, width), f32)
    returning = given(
        mid_kernel,
        pltpu.PrefetchScalarGridSpec(
            num_scalar_prefetch=1,
            grid=(half,),
            in_specs=[
                pl.BlockSpec(block, lambda c, r: (0, r[0], 0, c, 0, 0)),
                pl.BlockSpec(block, lambda c, r: (0, 1 - r[0], 0, c, 0, 0)),
                pl.BlockSpec((2, 1, lines, depth_cells, width), lambda c, r: (0, c, 0, 0, 0)),
                whole(wide_mask),
                whole(table_depth),
                whole(inverse_depth),
            ],
            out_specs=pl.BlockSpec((slabs, rows, 2, 1, group, width), lambda c, r: (0, 0, 0, c, 0, 0)),
            scratch_shapes=[buffer, buffer],
        ),
        exchanged,
        "middle",
    )(here, received, received, chip_measured, wide_mask, table_depth, inverse_depth)
    returned = lax.all_to_all(returning, "slab", 0, 0, tiled=True)

    tall = quarter + 2 * edge

    def back_kernel(*refs):
        backward_kernel(lines, planes, edge, *refs)

    parts = pl.pallas_call(
        back_kernel,
        grid=(half,),
        out_shape=jax.ShapeDtypeStruct((columns * rows, 2, planes, tall, width), bf16),
        in_specs=[
            pl.BlockSpec((slabs, rows, 2, 1, group, width), lambda c: (0, 0, 0, c, 0, 0)),
            pl.BlockSpec((2, 1, rows, phase_cells * planes, width), lambda c: (0, c, 0, 0, 0)),
            whole(inverse_phase),
        ],
        out_specs=pl.BlockSpec((columns * rows, 2, planes, tall, width), lambda c: (0, 0, 0, 0, 0)),
        scratch_shapes=[
            buffer,
            buffer,
            pltpu.VMEM((rows, 2, planes, phase_cells, width), f32),
            pltpu.VMEM((phase_cells + 2 * edge, width), f32),
        ],
        name="backward",
    )(returned, chip_sens, inverse_phase)
    gradient = lax.all_to_all(parts, ("coil", "row"), 0, 0, tiled=True).astype(f32).sum(axis=0)
    own = own_image - step_size * gradient
    margin = 2 ** thresholds.shape[0] - 1
    devices = slabs * rows
    up = [(i, (i + 1) % devices) for i in range(devices)]
    down = [(target, source) for source, target in up]
    narrow = own.astype(bf16)
    low = lax.ppermute(narrow[:, planes - margin :], lines_axes, up)
    high = lax.ppermute(narrow[:, :margin], lines_axes, down)
    change = shrink(own_image, own, low, high, thresholds, edge, columns)
    gathered = lax.all_to_all(change, "coil", 0, 0, tiled=True)
    change_rows = jnp.swapaxes(gathered, 0, 1).reshape(2, phase_cells * planes, width)
    return (image_rows + change_rows.astype(f32)).reshape(2, phase_cells, planes, width)


def solution(mesh):
    return jax.shard_map(
        local,
        mesh=mesh,
        in_specs=(
            P("groups", None, lines_axes, None),
            P("groups", "coil", None, lines_axes, None),
            P("groups", "coil", lines_axes, None, None),
            P(lines_axes, None),
            P(),
        ),
        out_specs=P("groups", None, lines_axes, None),
        check_vma=False,
    )
```

time: 328 us -> 305 us (0.930)
  blocking collectives: 134 us -> 10.4 us
  starting transfers between devices: 50.5 us -> 162 us
  Pallas kernels: 25.1 us -> 18.3 us
  waiting for transfers between devices: 110 us -> 105 us
    all_to_all x2 -> x1, blocking collectives: 134 us -> 10.4 us  [local(): gathered = lax.all_to_all(change, 'coil', 0, 0, tiled=True)]
    ppermute x0 -> x4, starting transfers between devices: none -> 67.3 us  [the longest x2 63.4 us: both_rows(): return in_row_order(kept, lax.ppermute(away, 'row', other), axis)]
    all_to_all x1 -> x3, starting transfers between devices: 47.5 us -> 91.7 us  [the longest x1 45.9 us: local(): received = lax.all_to_all(outgoing, 'slab', 0, 0, tiled=True)]
    all_to_all x1 -> x3, waiting for transfers between devices: 108 us -> 98.6 us  [the longest x1 50.6 us: local(): returned = lax.all_to_all(returning, 'slab', 0, 0, tiled=True)]
    pallas_call x4 -> x5, Pallas kernels: 25.1 us -> 18.3 us  [the longest x1 4.52 us: shrink(): pl.pallas_call(kernel, out_shape=jax.ShapeDtypeStruct((copies, 2, (rows -...]
    ppermute x0 -> x4, waiting for transfers between devices: none -> 4.73 us  [the longest x1 2.09 us: local(): arrived = lax.ppermute(sent, 'row', other)]
  transfers between devices with their start and end apart: 3 -> 9, of which waited for: 2 -> 7; matrix products, arithmetic and copies ran while one was open for 1% -> 1% of each run, Pallas kernels for 0% -> 0%
where the time goes in v2:
time: 305 us
  starting transfers between devices  162 us (53%)
  waiting for transfers between devices  105 us (34%)
  Pallas kernels  18.3 us (6%)
  blocking collectives  10.4 us (3%)
  other arithmetic  4.89 us (2%)
  local copies, waits for them, and re-layouts  3.75 us (1%)
    ppermute x2, starting transfers between devices, both_rows(): return in_row_order(kept, lax.ppermute(away, 'row', other), axis)  63.4 us
    all_to_all x1, waiting for transfers between devices, local(): returned = lax.all_to_all(returning, 'slab', 0, 0, tiled=True)  50.6 us
    all_to_all x1, starting transfers between devices, local(): received = lax.all_to_all(outgoing, 'slab', 0, 0, tiled=True)  45.9 us
    all_to_all x1, waiting for transfers between devices, local(): received = lax.all_to_all(outgoing, 'slab', 0, 0, tiled=True)  36.4 us
    all_to_all x1, starting transfers between devices, local(): lax.all_to_all(parts, ('coil', 'row'), 0, 0, tiled=True).astype(f32)  33.5 us
    all_to_all x1, starting transfers between devices, local(): returned = lax.all_to_all(returning, 'slab', 0, 0, tiled=True)  12.3 us
    all_to_all x1, waiting for transfers between devices, local(): lax.all_to_all(parts, ('coil', 'row'), 0, 0, tiled=True).astype(f32)  11.6 us
    all_to_all x1, blocking collectives, local(): gathered = lax.all_to_all(change, 'coil', 0, 0, tiled=True)  10.4 us
  transfers between devices with their start and end apart: 9, of which 7 were waited for; matrix products, arithmetic and copies ran while one was open for 1% of the time, Pallas kernels for 0%

profile of v2, /device:TPU:40, one launch (start us, length us, event | category | flops | bytes accessed | tf_op | source)
XLA Modules:
  0.0 304.6 jit_solution(17210046294013193019)
XLA Ops:
  0.0 2.7 forward_sent.1
  2.7 1.9 collective-permute-start
  4.7 2.1 collective-permute-done.arrived_ref
  6.8 0.8 copy-done.4
  7.6 3.0 forward_kept.1
  10.6 45.9 %all-to-all-start = ((bf16[32,2,2,2,16,128]{5,4,3,2,1,0:T(8,128)(2,1)}), bf16[32,2,2,2,16,128]{5,4,3,2,1,0:T(8,128)(2,1)S(1)}, u32[]{:S(2)}, u32[]{:S(2)}) async-start(bf16[32,2,2,2,16,128]{5,4,3,2,1,0:T(8,128)(2,1)} %get-tuple-element.10), calls=%async_computation | async-start | bytes 2097152 | tf_op jit(solution)/shard_map/all_to_all | solution.py:398
  56.5 0.0 copy-done.10
  56.5 0.0 copy-done.11
  56.5 0.4 bitcast_convert_fusion
  56.9 0.0 copy-start.7
  57.0 36.0 %collective-permute-start.1 = (bf16[2,2,2,256,128]{4,3,2,1,0:T(8,128)(2,1)S(1)}, bf16[2,2,2,256,128]{4,3,2,1,0:T(8,128)(2,1)S(1)}, u32[]{:S(2)}, u32[]{:S(2)}) collective-permute-start(bf16[2,2,2,256,128]{4,3,2,1,0:T(8,128)(2,1)S(1)} %dynamic-slice_bitcast_fusion.1), channel_id=1, source_target_pairs={{0,1},{1,0},{2,3},{3,2},{4,5},{5,4},{6,7},{7,6},{8,9},{9,8},{10,11... | collective-permute-start | bytes 1572872 | tf_op jit(solution)/shard_map/ppermute | solution.py:405
  93.0 0.0 copy-done.7
  93.0 2.0 collective-permute-start.2
  95.0 1.1 collective-permute-done.2
  96.1 0.0 collective-permute-done.1
  96.1 0.1 bitcast_select_fusion.3
  96.2 1.1 pad_maximum_fusion.refs_2_
  97.3 36.4 %all-to-all-done.refs_0_.refs_1_ = bf16[32,2,2,2,16,128]{5,4,3,2,1,0:T(8,128)(2,1)S(1)} async-done(((bf16[32,2,2,2,16,128]{5,4,3,2,1,0:T(8,128)(2,1)}), bf16[32,2,2,2,16,128]{5,4,3,2,1,0:T(8,128)(2,1)S(1)}, u32[]{:S(2)}, u32[]{:S(2)}) %all-to-all-start) | async-done | bytes 1048608 | tf_op jit(solution)/shard_map/all_to_all | solution.py:398
  133.7 1.1 broadcast_in_dim.2.refs_3_
  134.9 0.0 copy-done.1
  134.9 4.4 %middle.1 = bf16[32,2,2,2,16,128]{5,4,3,2,1,0:T(8,128)(2,1)} custom-call(s32[1]{0:T(128)} %bitcast.1._.r_ref, bf16[32,2,2,2,16,128]{5,4,3,2,1,0:T(8,128)(2,1)} %copy-done.1, bf16[32,2,2,2,16,128]{5,4,3,2,1,0:T(8,128)(2,1)} %copy-done.1, bf16[2,2,4,256,128]{4,3,2,1,0:T(8,128)(2,1)} %pad_maximum_fusion.refs_2_, f32[4,256,128]{2,1,0:T(8,128)} %broadcast_in_dim.2.refs_3_, ...), custom_call_target="tpu_custom_call" | custom-call | tf_op jit(solution)/shard_map/middle/pallas_call | solution.py:434
  139.2 12.3 %all-to-all-start.1 = ((bf16[32,2,2,2,16,128]{5,4,3,2,1,0:T(8,128)(2,1)}), bf16[32,2,2,2,16,128]{5,4,3,2,1,0:T(8,128)(2,1)S(1)}, u32[]{:S(2)}, u32[]{:S(2)}) async-start(bf16[32,2,2,2,16,128]{5,4,3,2,1,0:T(8,128)(2,1)} %middle.1), calls=%async_computation.1 | async-start | bytes 2097152 | tf_op jit(solution)/shard_map/all_to_all | solution.py:453
  151.5 0.0 copy-done
  151.6 27.4 %collective-permute-start.3 = (bf16[2,2,1,512,128]{4,3,2,1,0:T(8,128)(2,1)S(1)}, bf16[2,2,1,512,128]{4,3,2,1,0:T(8,128)(2,1)S(1)}, u32[]{:S(2)}, u32[]{:S(2)}) collective-permute-start(bf16[2,2,1,512,128]{4,3,2,1,0:T(8,128)(2,1)S(1)} %dynamic-slice_bitcast_fusion), channel_id=1, source_target_pairs={{0,1},{1,0},{2,3},{3,2},{4,5},{5,4},{6,7},{7,6},{8,9},{9,8},{10,11... | collective-permute-start | bytes 1572872 | tf_op jit(solution)/shard_map/ppermute | solution.py:405
  179.0 1.5 collective-permute-done.3
  180.5 0.1 bitcast_select_fusion.1
  180.6 1.1 pad_maximum_fusion.1.refs_1_
  181.7 50.6 %all-to-all-done.1.refs_0_ = bf16[32,2,2,2,16,128]{5,4,3,2,1,0:T(8,128)(2,1)S(1)} async-done(((bf16[32,2,2,2,16,128]{5,4,3,2,1,0:T(8,128)(2,1)}), bf16[32,2,2,2,16,128]{5,4,3,2,1,0:T(8,128)(2,1)S(1)}, u32[]{:S(2)}, u32[]{:S(2)}) %all-to-all-start.1) | async-done | bytes 1048608 | tf_op jit(solution)/shard_map/all_to_all | solution.py:453
  232.3 1.0 copy-done.3
  233.3 3.7 %backward.1 = bf16[8,2,4,40,128]{4,3,2,1,0:T(8,128)(2,1)} custom-call(bf16[32,2,2,2,16,128]{5,4,3,2,1,0:T(8,128)(2,1)} %copy-done.3, bf16[2,2,2,512,128]{4,3,2,1,0:T(8,128)(2,1)} %pad_maximum_fusion.1.refs_1_, bf16[256,256]{1,0:T(8,128)(2,1)} %constant.40.clone.refs_2_), custom_call_target="tpu_custom_call" | custom-call | tf_op jit(solution)/shard_map/backward/pallas_call | solution.py:460
  237.0 33.5 %all-to-all-start.2 = ((bf16[8,2,4,40,128]{4,3,2,1,0:T(8,128)(2,1)}), bf16[8,2,4,40,128]{4,3,2,1,0:T(8,128)(2,1)S(1)}, u32[]{:S(2)}, u32[]{:S(2)}) async-start(bf16[8,2,4,40,128]{4,3,2,1,0:T(8,128)(2,1)} %backward.1), calls=%async_computation.2 | async-start | bytes 1310720 | tf_op jit(solution)/shard_map/all_to_all | solution.py:478
  270.4 0.0 copy-done.2
  270.5 0.0 copy-start.8
  270.5 0.0 copy-start.9
  270.5 11.6 %all-to-all-done.2 = bf16[8,2,4,40,128]{4,3,2,1,0:T(8,128)(2,1)S(1)} async-done(((bf16[8,2,4,40,128]{4,3,2,1,0:T(8,128)(2,1)}), bf16[8,2,4,40,128]{4,3,2,1,0:T(8,128)(2,1)S(1)}, u32[]{:S(2)}, u32[]{:S(2)}) %all-to-all-start.2) | async-done | bytes 655392 | tf_op jit(solution)/shard_map/all_to_all | solution.py:478
  282.1 0.1 convert_reduce_fusion
  282.2 0.8 fusion.4
  283.1 0.1 collective-permute-start.4
  283.1 2.9 collective-permute-start.5
  286.1 0.0 copy-done.8
  286.1 0.7 broadcast_multiply_fusion.refs_4_
  286.7 1.2 collective-permute-done.4.refs_2_
  288.0 0.0 collective-permute-done.5.refs_3_
  288.0 0.6 copy-done.5
  288.6 0.0 copy-done.6
  288.6 4.5 %wavelet.1 = bf16[4,2,128,128]{3,2,1,0:T(8,128)(2,1)} custom-call(f32[2,4,40,128]{3,2,1,0:T(8,128)} %get-tuple-element.17.refs_0_, f32[2,4,40,128]{3,2,1,0:T(8,128)} %get-tuple-element.16.refs_1_, bf16[2,3,40,128]{3,2,1,0:T(8,128)(2,1)} %copy-done.5, bf16[2,3,40,128]{3,2,1,0:T(8,128)(2,1)} %copy-done.6, f32[2,7]{1,0:T(2,128)} %broadcast_multiply_fusion.refs_4_), custom_call_target="tpu_custom_call" | custom-call | tf_op jit(solution)/shard_map/wavelet/pallas_call | solution.py:305
  293.1 10.4 %all_to_all.20 = bf16[4,2,128,128]{3,2,1,0:T(8,128)(2,1)S(1)} all-to-all(bf16[4,2,128,128]{3,2,1,0:T(8,128)(2,1)} %wavelet.1), channel_id=1, replica_groups=mesh['groups'=2,'slab'=32,'coil'=4,'row'=2] {'coil'}, dimensions={0} | all-to-all | bytes 524288 | tf_op jit(solution)/shard_map/all_to_all | solution.py:488
  303.6 0.9 add.18
  (20 shorter events, 0.3 us)
Async XLA Ops:
  2.7 4.0 %collective-permute-start = (bf16[32,2,2,16,128]{4,3,2,1,0:T(8,128)(2,1)}, bf16[32,2,2,16,128]{4,3,2,1,0:T(8,128)(2,1)S(1)}, u32[]{:S(2)}, u32[]{:S(2)}) collective-permute-start(bf16[32,2,2,16,128]{4,3,2,1,0:T(8,128)(2,1)} %forward_sent.1), channel_id=1, source_target_pairs={{0,1},{1,0},{2,3},{3,2},{4,5},{5,4},{6,7},{7,6},{8,9},{9,8},{10,11... | collective-permute-start | bytes 1572872 | tf_op jit(solution)/shard_map/ppermute | solution.py:365
  6.8 0.8 copy-start.4
  10.6 45.9 %copy-start.10 = (bf16[2,4,2,256,128]{4,3,2,1,0:T(8,128)(2,1)S(1)}, bf16[2,4,2,256,128]{4,3,2,1,0:T(8,128)(2,1)}, u32[]{:S(2)}) copy-start(bf16[2,4,2,256,128]{4,3,2,1,0:T(8,128)(2,1)} %param.13) | copy-start | bytes 3145732
  10.6 45.9 %copy-start.11 = (bf16[2,128,2,128,1,1]{3,1,0,5,4,2:T(8,128)(2,1)S(1)}, bf16[2,128,2,128,1,1]{3,1,0,5,4,2:T(8,128)(2,1)}, u32[]{:S(2)}) copy-start(bf16[2,128,2,128,1,1]{3,1,0,5,4,2:T(8,128)(2,1)} %constant.47) | copy-start | bytes 393220
  10.6 123.2 %all-to-all-start = ((bf16[32,2,2,2,16,128]{5,4,3,2,1,0:T(8,128)(2,1)}), bf16[32,2,2,2,16,128]{5,4,3,2,1,0:T(8,128)(2,1)S(1)}, u32[]{:S(2)}, u32[]{:S(2)}) async-start(bf16[32,2,2,2,16,128]{5,4,3,2,1,0:T(8,128)(2,1)} %get-tuple-element.10), calls=%async_computation | async-start | bytes 2097152 | tf_op jit(solution)/shard_map/all_to_all | solution.py:398
  56.9 36.1 %copy-start.7 = (s32[2,256]{1,0:T(2,128)S(1)}, s32[2,256]{1,0:T(2,128)}, u32[]{:S(2)}) copy-start(s32[2,256]{1,0:T(2,128)} %param.14) | copy-start | bytes 6148
  57.0 39.1 %collective-permute-start.1 = (bf16[2,2,2,256,128]{4,3,2,1,0:T(8,128)(2,1)S(1)}, bf16[2,2,2,256,128]{4,3,2,1,0:T(8,128)(2,1)S(1)}, u32[]{:S(2)}, u32[]{:S(2)}) collective-permute-start(bf16[2,2,2,256,128]{4,3,2,1,0:T(8,128)(2,1)S(1)} %dynamic-slice_bitcast_fusion.1), channel_id=1, source_target_pairs={{0,1},{1,0},{2,3},{3,2},{4,5},{5,4},{6,7},{7,6},{8,9},{9,8},{10,11... | collective-permute-start | bytes 1572872 | tf_op jit(solution)/shard_map/ppermute | solution.py:405
  93.0 3.1 %collective-permute-start.2 = (f32[2,256]{1,0:T(2,128)S(1)}, f32[2,256]{1,0:T(2,128)S(1)}, u32[]{:S(2)}, u32[]{:S(2)}) collective-permute-start(f32[2,256]{1,0:T(2,128)S(1)} %convert_element_type.24), channel_id=1, source_target_pairs={{0,1},{1,0},{2,3},{3,2},{4,5},{5,4},{6,7},{7,6},{8,9},{9,8},{10,11... | collective-permute-start | bytes 6152 | tf_op jit(solution)/shard_map/ppermute | solution.py:416
  133.7 1.1 copy-start.1
  139.2 12.3 %copy-start = (bf16[2,4,128,4,128]{4,3,2,1,0:T(4,128)(2,1)S(1)}, bf16[2,4,128,4,128]{4,3,2,1,0:T(4,128)(2,1)}, u32[]{:S(2)}) copy-start(bf16[2,4,128,4,128]{4,3,2,1,0:T(4,128)(2,1)} %param.12) | copy-start | bytes 3145732
  139.2 93.1 %all-to-all-start.1 = ((bf16[32,2,2,2,16,128]{5,4,3,2,1,0:T(8,128)(2,1)}), bf16[32,2,2,2,16,128]{5,4,3,2,1,0:T(8,128)(2,1)S(1)}, u32[]{:S(2)}, u32[]{:S(2)}) async-start(bf16[32,2,2,2,16,128]{5,4,3,2,1,0:T(8,128)(2,1)} %middle.1), calls=%async_computation.1 | async-start | bytes 2097152 | tf_op jit(solution)/shard_map/all_to_all | solution.py:453
  151.6 28.9 %collective-permute-start.3 = (bf16[2,2,1,512,128]{4,3,2,1,0:T(8,128)(2,1)S(1)}, bf16[2,2,1,512,128]{4,3,2,1,0:T(8,128)(2,1)S(1)}, u32[]{:S(2)}, u32[]{:S(2)}) collective-permute-start(bf16[2,2,1,512,128]{4,3,2,1,0:T(8,128)(2,1)S(1)} %dynamic-slice_bitcast_fusion), channel_id=1, source_target_pairs={{0,1},{1,0},{2,3},{3,2},{4,5},{5,4},{6,7},{7,6},{8,9},{9,8},{10,11... | collective-permute-start | bytes 1572872 | tf_op jit(solution)/shard_map/ppermute | solution.py:405
  232.3 1.0 copy-start.3
  237.0 33.5 %copy-start.2 = (f32[2,128,4,128]{3,2,1,0:T(4,128)S(1)}, f32[2,128,4,128]{3,2,1,0:T(4,128)}, u32[]{:S(2)}) copy-start(f32[2,128,4,128]{3,2,1,0:T(4,128)} %param.11) | copy-start | bytes 1572868
  237.0 45.2 %all-to-all-start.2 = ((bf16[8,2,4,40,128]{4,3,2,1,0:T(8,128)(2,1)}), bf16[8,2,4,40,128]{4,3,2,1,0:T(8,128)(2,1)S(1)}, u32[]{:S(2)}, u32[]{:S(2)}) async-start(bf16[8,2,4,40,128]{4,3,2,1,0:T(8,128)(2,1)} %backward.1), calls=%async_computation.2 | async-start | bytes 1310720 | tf_op jit(solution)/shard_map/all_to_all | solution.py:478
  270.5 15.6 %copy-start.8 = (f32[2,7]{1,0:T(2,128)S(1)}, f32[2,7]{1,0:T(2,128)}, u32[]{:S(2)}) copy-start(f32[2,7]{1,0:T(2,128)} %param.15) | copy-start | bytes 172
  270.5 15.6 %copy-start.9 = (f32[2]{0:T(128)S(1)}, f32[2]{0:T(128)}, u32[]{:S(2)}) copy-start(f32[2]{0:T(128)} %constant.46) | copy-start | bytes 28
  283.1 4.9 %collective-permute-start.4 = (bf16[2,3,40,128]{3,2,1,0:T(8,128)(2,1)S(1)}, bf16[2,3,40,128]{3,2,1,0:T(8,128)(2,1)S(1)}, u32[]{:S(2)}, u32[]{:S(2)}) collective-permute-start(bf16[2,3,40,128]{3,2,1,0:T(8,128)(2,1)S(1)} %get-tuple-element.25), channel_id=1, source_target_pairs={{0,1},{1,8},{8,9},{9,16},{16,17},{17,24},{24,25},{25,32},{32,33},{... | collective-permute-start | bytes 184328 | tf_op jit(solution)/shard_map/ppermute | solution.py:485
  283.1 4.8 %collective-permute-start.5 = (bf16[2,3,40,128]{3,2,1,0:T(8,128)(2,1)S(1)}, bf16[2,3,40,128]{3,2,1,0:T(8,128)(2,1)S(1)}, u32[]{:S(2)}, u32[]{:S(2)}) collective-permute-start(bf16[2,3,40,128]{3,2,1,0:T(8,128)(2,1)S(1)} %get-tuple-element.24), channel_id=1, source_target_pairs={{1,0},{8,1},{9,8},{16,9},{17,16},{24,17},{25,24},{32,25},{33,32},{... | collective-permute-start | bytes 184328 | tf_op jit(solution)/shard_map/ppermute | solution.py:486
  288.0 0.6 copy-start.5
  288.0 0.6 copy-start.6

commit v3 on v2

--- a/solution.py
+++ b/solution.py
@@ -144,8 +144,8 @@
                     framed[0:edge] = total[row, t, z, cells - edge : cells]
                     framed[edge : edge + cells] = total[row, t, z]
                     framed[edge + cells :] = total[row, t, z, 0:edge]
-                    for q in range(pieces // rows):
-                        out_ref[q * rows + row, t, z] = framed[q * step : q * step + tall].astype(out_ref.dtype)
+                    for q in range(pieces):
+                        out_ref[q, t, row * planes + z] = framed[q * step : q * step + tall].astype(out_ref.dtype)
 
 
 def removed(real, imaginary, limit):
@@ -153,25 +153,25 @@
     return real * factor, imaginary * factor
 
 
-def wavelet_kernel(edge, image_ref, own_ref, low_ref, high_ref, limits_ref, out_ref, a0, lo0, hi0, a1, lo1, hi1, sums, diffs, mixed):
-    planes, rows, width = own_ref.shape[1:]
-    margin = low_ref.shape[1]
+def wavelet_kernel(edge, margin, row_ref, chip_ref, halo_ref, limits_ref, out_ref, a0, lo0, hi0, a1, lo1, hi1, sums, diffs, mixed):
+    chip_planes, rows, width = chip_ref.shape[1:]
+    planes = chip_planes // 2
     count = planes + 2 * margin
     steps = rows // 8
     pad = 8
+    row = row_ref[0]
     for t in range(2):
+        for p in range(chip_planes):
+            a0[t, (1 - row) * planes + p] = chip_ref[t, p]
         for p in range(margin):
-            a0[t, p] = low_ref[t, p].astype(jnp.float32)
-            a0[t, margin + planes + p] = high_ref[t, p].astype(jnp.float32)
-        for p in range(planes):
-            a0[t, margin + p] = own_ref[t, p]
-
-    def split_lanes(source, lo, hi, lo_planes, hi_planes, offset):
+            a0[t, 1 + row * (margin + planes) + p] = halo_ref[t, p].astype(jnp.float32)
+
+    def split_lanes(source, shift, lo, hi, lo_planes, hi_planes, offset):
         def step(j, carry):
             y = pl.multiple_of(j * 8, 8)
             for t in range(2):
                 for p in lo_planes:
-                    v = source[t, p, pl.ds(y, 8), :]
+                    v = source[t, p + shift, pl.ds(y, 8), :]
                     s = pltpu.roll(v, width - offset, 1)
                     lo[t, p, pl.ds(y, 8), :] = v + s
                     if p in hi_planes:
@@ -223,7 +223,7 @@
         upper = sums[1, t, p, pl.ds(y, 8), :] + diffs[1, t, p, pl.ds(y + pad - offset, 8), :]
         return lower + upper + pltpu.roll(lower - upper, offset, 1)
 
-    split_lanes(a0, lo0, hi0, range(count), range(2, planes + 4), 1)
+    split_lanes(a0, 1, lo0, hi0, range(count), range(2, planes + 4), 1)
 
     def coarse_step(j, carry):
         y = pl.multiple_of(j * 8, 8)
@@ -236,7 +236,7 @@
 
     lax.fori_loop(0, steps, coarse_step, 0)
 
-    split_lanes(a1, lo1, hi1, range(count - 1), range(count - 1), 2)
+    split_lanes(a1, 0, lo1, hi1, range(count - 1), range(count - 1), 2)
 
     def level_one(j, carry):
         detail_step(pl.multiple_of(j * 8, 8), lo1, hi1, 2, 1, 0, planes + 2, None)
@@ -263,9 +263,8 @@
         y = pl.multiple_of(j * 8, 8)
         for t in range(2):
             for p in range(planes):
-                change = own_ref[t, p, pl.ds(y, 8), :] - image_ref[t, p, pl.ds(y, 8), :]
-                change = change - merged_rows(y, t, margin + p, 1) * (1.0 / 64.0)
-                mixed[t, pl.ds(y * planes + p, 8, stride=planes), :] = change
+                value = a0[t, 1 + margin + p, pl.ds(y, 8), :] - merged_rows(y, t, margin + p, 1) * (1.0 / 64.0)
+                mixed[t, pl.ds(y * planes + p, 8, stride=planes), :] = value
         return carry
 
     lax.fori_loop(0, steps, level_zero_merge, 0)
@@ -280,15 +279,16 @@
     return pl.BlockSpec(shape, lambda *_: (0,) * len(shape))
 
 
-def shrink(image, own, low, high, thresholds, edge, copies):
-    _, planes, rows, width = own.shape
-    margin = low.shape[1]
+def shrink(row, chip, halo, thresholds, edge, copies):
+    _, chip_planes, rows, width = chip.shape
+    planes = chip_planes // 2
+    margin = halo.shape[1]
     count = planes + 2 * margin
     scale = np.array([[2.0 ** (1.5 * (level + 1))] for level in range(thresholds.shape[0])], np.float32)
     limits = thresholds * scale
     f32 = jnp.float32
     buffers = [
-        pltpu.VMEM((2, count, rows, width), f32),
+        pltpu.VMEM((2, chip_planes + planes, rows, width), f32),
         pltpu.VMEM((2, count, rows + 8, width), f32),
         pltpu.VMEM((2, count, rows + 8, width), f32),
         pltpu.VMEM((2, count, rows, width), f32),
@@ -300,16 +300,21 @@
     ]
 
     def kernel(*refs):
-        wavelet_kernel(edge, *refs)
+        wavelet_kernel(edge, margin, *refs)
 
     return pl.pallas_call(
         kernel,
         out_shape=jax.ShapeDtypeStruct((copies, 2, (rows - 2 * edge) * planes, width), jnp.bfloat16),
-        in_specs=[pl.BlockSpec(memory_space=pltpu.VMEM)] * 4 + [pl.BlockSpec(memory_space=pltpu.SMEM)],
+        in_specs=[
+            pl.BlockSpec(memory_space=pltpu.SMEM),
+            pl.BlockSpec(memory_space=pltpu.VMEM),
+            pl.BlockSpec(memory_space=pltpu.VMEM),
+            pl.BlockSpec(memory_space=pltpu.SMEM),
+        ],
         out_specs=pl.BlockSpec(memory_space=pltpu.VMEM),
         scratch_shapes=buffers,
         name="wavelet",
-    )(image, own, low, high, limits)
+    )(row, chip, halo, limits)
 
 
 def local(image, sens, measured, mask, thresholds):
@@ -364,17 +369,10 @@
     )(here, sens_rows, image_rows, table_phase)
     arrived = lax.ppermute(sent, "row", other)
 
-    def keep_kernel(r_ref, sens_ref, image_ref, table_ref, arrived_ref, out_ref, pause_ref, product, mixed):
-        @pl.when(pl.program_id(0) == 0)
-        def _():
-            pause_ref[...] = lax.fori_loop(
-                0, r_ref[0] * pause_steps, lambda _, v: v * 1.0001 + 0.5, jnp.ones(pause_ref.shape, jnp.float32)
-            )
-
+    def keep_kernel(_, sens_ref, image_ref, table_ref, out_ref, product, mixed):
         forward_kernel(slabs, lines, planes, sens_ref, image_ref, table_ref, out_ref.at[:, 0], product, mixed)
-        out_ref[:, 1] = arrived_ref[...]
-
-    outgoing, _ = given(
+
+    kept = given(
         keep_kernel,
         pltpu.PrefetchScalarGridSpec(
             num_scalar_prefetch=1,
@@ -383,17 +381,42 @@
                 pl.BlockSpec(sens_spec, lambda c, r: (0, r[0] * half + c, 0, 0)),
                 whole(image_rows),
                 whole(table_phase),
-                pl.BlockSpec((slabs, 2, 1, group, width), lambda c, r: (0, 0, c, 0, 0)),
-            ],
-            out_specs=[
-                pl.BlockSpec((slabs, rows, 2, 1, group, width), lambda c, r: (0, 0, 0, c, 0, 0)),
-                pl.BlockSpec((8, 128), lambda c, r: (0, 0)),
-            ],
+            ],
+            out_specs=pl.BlockSpec((slabs, 1, 2, 1, group, width), lambda c, r: (0, 0, 0, c, 0, 0)),
             scratch_shapes=[stack, stack],
         ),
-        [exchanged, jax.ShapeDtypeStruct((8, 128), f32)],
+        exchanged,
         "forward_kept",
-    )(here, sens_rows, image_rows, table_phase, arrived)
+    )(here, sens_rows, image_rows, table_phase)
+
+    def place_kernel(r_ref, _, arrived_ref, out_ref, pause_ref):
+        @pl.when(pl.program_id(0) == 0)
+        def _():
+            pause_ref[...] = lax.fori_loop(
+                0, r_ref[0] * pause_steps, lambda _, v: v * 1.0001 + 0.5, jnp.ones(pause_ref.shape, jnp.float32)
+            )
+
+        out_ref[:, 0] = arrived_ref[...]
+
+    pieces = 4
+    outgoing, _ = pl.pallas_call(
+        place_kernel,
+        grid_spec=pltpu.PrefetchScalarGridSpec(
+            num_scalar_prefetch=1,
+            grid=(pieces,),
+            in_specs=[
+                pl.BlockSpec(memory_space=pl.ANY),
+                pl.BlockSpec((slabs // pieces, 2, half, group, width), lambda i, r: (i, 0, 0, 0, 0)),
+            ],
+            out_specs=[
+                pl.BlockSpec((slabs // pieces, 1, 2, half, group, width), lambda i, r: (i, 1, 0, 0, 0, 0)),
+                pl.BlockSpec((8, 128), lambda i, r: (0, 0)),
+            ],
+        ),
+        out_shape=[exchanged, jax.ShapeDtypeStruct((8, 128), f32)],
+        input_output_aliases={1: 0},
+        name="place",
+    )(here, kept, arrived)
 
     received = lax.all_to_all(outgoing, "slab", 0, 0, tiled=True)
 
@@ -425,6 +448,7 @@
     own_image = lax.dynamic_slice_in_dim(
         framed, lax.axis_index("coil") * quarter, quarter + 2 * edge, axis=2
     )
+    chip_image = in_row_order(own_image, lax.ppermute(own_image, "row", other), 1)
 
     def mid_kernel(_, *refs):
         middle_kernel(lines, *refs)
@@ -451,6 +475,7 @@
         "middle",
     )(here, received, received, chip_measured, wide_mask, table_depth, inverse_depth)
     returned = lax.all_to_all(returning, "slab", 0, 0, tiled=True)
+    returned, chip_image = lax.optimization_barrier((returned, chip_image))
 
     tall = quarter + 2 * edge
 
@@ -460,13 +485,13 @@
     parts = pl.pallas_call(
         back_kernel,
         grid=(half,),
-        out_shape=jax.ShapeDtypeStruct((columns * rows, 2, planes, tall, width), bf16),
+        out_shape=jax.ShapeDtypeStruct((columns, 2, rows * planes, tall, width), bf16),
         in_specs=[
             pl.BlockSpec((slabs, rows, 2, 1, group, width), lambda c: (0, 0, 0, c, 0, 0)),
             pl.BlockSpec((2, 1, rows, phase_cells * planes, width), lambda c: (0, c, 0, 0, 0)),
             whole(inverse_phase),
         ],
-        out_specs=pl.BlockSpec((columns * rows, 2, planes, tall, width), lambda c: (0, 0, 0, 0, 0)),
+        out_specs=pl.BlockSpec((columns, 2, rows * planes, tall, width), lambda c: (0, 0, 0, 0, 0)),
         scratch_shapes=[
             buffer,
             buffer,
@@ -475,19 +500,22 @@
         ],
         name="backward",
     )(returned, chip_sens, inverse_phase)
-    gradient = lax.all_to_all(parts, ("coil", "row"), 0, 0, tiled=True).astype(f32).sum(axis=0)
-    own = own_image - step_size * gradient
+    share = lax.all_to_all(parts, "coil", 0, 0, tiled=True).astype(f32).sum(axis=0)
+    others = lax.ppermute(share.astype(bf16), "row", other)
+    chip = chip_image - step_size * (share + others.astype(f32))
     margin = 2 ** thresholds.shape[0] - 1
-    devices = slabs * rows
-    up = [(i, (i + 1) % devices) for i in range(devices)]
-    down = [(target, source) for source, target in up]
-    narrow = own.astype(bf16)
-    low = lax.ppermute(narrow[:, planes - margin :], lines_axes, up)
-    high = lax.ppermute(narrow[:, :margin], lines_axes, down)
-    change = shrink(own_image, own, low, high, thresholds, edge, columns)
-    gathered = lax.all_to_all(change, "coil", 0, 0, tiled=True)
-    change_rows = jnp.swapaxes(gathered, 0, 1).reshape(2, phase_cells * planes, width)
-    return (image_rows + change_rows.astype(f32)).reshape(2, phase_cells, planes, width)
+    last = rows * planes - margin
+    edge_planes = lax.dynamic_slice_in_dim(chip, row * last, margin, axis=1).astype(bf16)
+    pairs = []
+    for slab in range(slabs):
+        after = (slab + 1) % slabs
+        pairs.append((slab * rows + rows - 1, after * rows))
+        pairs.append((after * rows, slab * rows + rows - 1))
+    halo = lax.ppermute(edge_planes, lines_axes, pairs)
+    result = shrink(here, chip, halo, thresholds, edge, columns)
+    gathered = lax.all_to_all(result, "coil", 0, 0, tiled=True)
+    result_rows = jnp.swapaxes(gathered, 0, 1).reshape(2, phase_cells * planes, width)
+    return result_rows.astype(f32).reshape(2, phase_cells, planes, width)
 
 
 def solution(mesh):

time: 305 us -> 302 us (level)
  blocking collectives: 10.4 us -> 23.6 us
  starting transfers between devices: 162 us -> 151 us
  waiting for transfers between devices: 105 us -> 96.6 us
    ppermute x2 -> x3, starting transfers between devices: 3 us -> 51.7 us  [the longest x1 28.9 us: local(): lax.ppermute(own_image, 'row', other)]
    all_to_all x1 -> x0, starting transfers between devices: 33.5 us -> none  [local(): lax.all_to_all(parts, ('coil', 'row'), 0, 0, tiled=True).astype(f32)]
    ppermute x2, starting transfers between devices: 63.4 us -> 38.3 us  [both_rows(): return in_row_order(kept, lax.ppermute(away, 'row', other), axis)]
    all_to_all x1 -> x2, blocking collectives: 10.4 us -> 23.6 us  [the longest x1 13.4 us: local(): lax.all_to_all(parts, 'coil', 0, 0, tiled=True).astype(f32).sum(axis=0)]
    all_to_all x1 -> x0, waiting for transfers between devices: 11.6 us -> none  [local(): lax.all_to_all(parts, ('coil', 'row'), 0, 0, tiled=True).astype(f32)]
    ppermute x2 -> x3, waiting for transfers between devices: 1.24 us -> 5.16 us  [the longest x1 4.15 us: local(): halo = lax.ppermute(edge_planes, lines_axes, pairs)]
    pallas_call x0 -> x1, Pallas kernels: none -> 3.16 us  [local(): pl.pallas_call(place_kernel, grid_spec=pltpu.PrefetchScalarGridSpec(num_s...]
  transfers between devices with their start and end apart: 9 -> 9, of which waited for: 7 -> 6; matrix products, arithmetic and copies ran while one was open for 1% -> 1% of each run, Pallas kernels for 0% -> 1%
where the time goes in v3:
time: 302 us; the launch traced here: 301 us
  starting transfers between devices  151 us (50%)
  waiting for transfers between devices  96.6 us (32%)
  blocking collectives  23.6 us (8%)
  Pallas kernels  21.2 us (7%)
  local copies, waits for them, and re-layouts  4.55 us (2%)
  other arithmetic  3.35 us (1%)
    all_to_all x1, waiting for transfers between devices, local(): returned = lax.all_to_all(returning, 'slab', 0, 0, tiled=True)  52.3 us
    all_to_all x1, starting transfers between devices, local(): received = lax.all_to_all(outgoing, 'slab', 0, 0, tiled=True)  45.9 us
    ppermute x2, starting transfers between devices, both_rows(): return in_row_order(kept, lax.ppermute(away, 'row', other), axis)  38.3 us
    all_to_all x1, waiting for transfers between devices, local(): received = lax.all_to_all(outgoing, 'slab', 0, 0, tiled=True)  36.2 us
    ppermute x1, starting transfers between devices, local(): lax.ppermute(own_image, 'row', other)  28.9 us
    ppermute x1, starting transfers between devices, local(): others = lax.ppermute(share.astype(bf16), 'row', other)  20.9 us
    all_to_all x1, blocking collectives, local(): lax.all_to_all(parts, 'coil', 0, 0, tiled=True).astype(f32).sum(axis=0)  13.4 us
    all_to_all x1, starting transfers between devices, local(): returned = lax.all_to_all(returning, 'slab', 0, 0, tiled=True)  10.8 us
  transfers between devices with their start and end apart: 9, of which 6 were waited for; matrix products, arithmetic and copies ran while one was open for 1% of the time, Pallas kernels for 1%

profile of v3, /device:TPU:40, one launch (start us, length us, event | category | flops | bytes accessed | tf_op | source)
XLA Modules:
  0.0 300.7 jit_solution(6901176689776964356)
XLA Ops:
  0.0 2.7 forward_sent.1
  2.7 1.9 collective-permute-start
  4.7 2.8 forward_kept.1._
  7.5 0.0 collective-permute-done.arrived_ref
  7.5 0.8 copy-done.5
  8.3 3.2 %place.1 = (bf16[32,2,2,2,16,128]{5,4,3,2,1,0:T(8,128)(2,1)}, f32[8,128]{1,0:T(8,128)}) custom-call(s32[1]{0:T(128)} %bitcast._.r_ref.refs_0_, bf16[32,2,2,2,16,128]{5,4,3,2,1,0:T(8,128)(2,1)} %forward_kept.1._, bf16[32,2,2,16,128]{4,3,2,1,0:T(8,128)(2,1)} %copy-done.5), custom_call_target="tpu_custom_call", output_to_operand_aliasing={{0}: (1, {})} | custom-call | tf_op jit(solution)/shard_map/place/pallas_call | solution.py:402
  11.5 45.9 %all-to-all-start = ((bf16[32,2,2,2,16,128]{5,4,3,2,1,0:T(8,128)(2,1)}), bf16[32,2,2,2,16,128]{5,4,3,2,1,0:T(8,128)(2,1)S(1)}, u32[]{:S(2)}, u32[]{:S(2)}) async-start(bf16[32,2,2,2,16,128]{5,4,3,2,1,0:T(8,128)(2,1)} %get-tuple-element.12), calls=%async_computation | async-start | bytes 2097152 | tf_op jit(solution)/shard_map/all_to_all | solution.py:421
  57.4 0.0 copy-done.10
  57.4 0.4 bitcast_convert_fusion
  57.8 0.0 copy-start.7
  57.9 36.3 %collective-permute-start.1 = (bf16[2,2,2,256,128]{4,3,2,1,0:T(8,128)(2,1)S(1)}, bf16[2,2,2,256,128]{4,3,2,1,0:T(8,128)(2,1)S(1)}, u32[]{:S(2)}, u32[]{:S(2)}) collective-permute-start(bf16[2,2,2,256,128]{4,3,2,1,0:T(8,128)(2,1)S(1)} %dynamic-slice_bitcast_fusion.1), channel_id=1, source_target_pairs={{0,1},{1,0},{2,3},{3,2},{4,5},{5,4},{6,7},{7,6},{8,9},{9,8},{10,11... | collective-permute-start | bytes 1572872 | tf_op jit(solution)/shard_map/ppermute | solution.py:428
  94.2 0.0 copy-done.7
  94.3 2.0 collective-permute-start.2
  96.2 1.1 collective-permute-done.2
  97.4 0.0 collective-permute-done.1
  97.4 0.1 bitcast_select_fusion.3
  97.5 1.1 pad_maximum_fusion.refs_2_
  98.6 36.2 %all-to-all-done.refs_0_.refs_1_ = bf16[32,2,2,2,16,128]{5,4,3,2,1,0:T(8,128)(2,1)S(1)} async-done(((bf16[32,2,2,2,16,128]{5,4,3,2,1,0:T(8,128)(2,1)}), bf16[32,2,2,2,16,128]{5,4,3,2,1,0:T(8,128)(2,1)S(1)}, u32[]{:S(2)}, u32[]{:S(2)}) %all-to-all-start) | async-done | bytes 1048608 | tf_op jit(solution)/shard_map/all_to_all | solution.py:421
  134.8 1.1 broadcast_in_dim.2.refs_3_
  136.0 0.0 copy-done.1
  136.0 4.3 %middle.1 = bf16[32,2,2,2,16,128]{5,4,3,2,1,0:T(8,128)(2,1)} custom-call(s32[1]{0:T(128)} %bitcast._.r_ref.refs_0_, bf16[32,2,2,2,16,128]{5,4,3,2,1,0:T(8,128)(2,1)} %copy-done.1, bf16[32,2,2,2,16,128]{5,4,3,2,1,0:T(8,128)(2,1)} %copy-done.1, bf16[2,2,4,256,128]{4,3,2,1,0:T(8,128)(2,1)} %pad_maximum_fusion.refs_2_, f32[4,256,128]{2,1,0:T(8,128)} %broadcast_in_dim.2.refs_3_, ...), custom_call_target="tpu_custom_call" | custom-call | tf_op jit(solution)/shard_map/middle/pallas_call | solution.py:458
  140.3 10.8 %all-to-all-start.1 = ((bf16[32,2,2,2,16,128]{5,4,3,2,1,0:T(8,128)(2,1)}), bf16[32,2,2,2,16,128]{5,4,3,2,1,0:T(8,128)(2,1)S(1)}, u32[]{:S(2)}, u32[]{:S(2)}) async-start(bf16[32,2,2,2,16,128]{5,4,3,2,1,0:T(8,128)(2,1)} %middle.1), calls=%async_computation.1 | async-start | bytes 2097152 | tf_op jit(solution)/shard_map/all_to_all | solution.py:477
  151.1 0.0 copy-start
  151.2 0.1 fusion.3
  151.3 28.9 %collective-permute-start.3 = (f32[2,4,40,128]{3,2,1,0:T(8,128)S(1)}, f32[2,4,40,128]{3,2,1,0:T(8,128)S(1)}, u32[]{:S(2)}, u32[]{:S(2)}) collective-permute-start(f32[2,4,40,128]{3,2,1,0:T(8,128)S(1)} %fusion.3), channel_id=1, source_target_pairs={{0,1},{1,0},{2,3},{3,2},{4,5},{5,4},{6,7},{7,6},{8,9},{9,8},{10,11... | collective-permute-start | bytes 491528 | tf_op jit(solution)/shard_map/ppermute | solution.py:451
  180.2 0.0 copy-done
  180.3 2.0 collective-permute-start.4
  182.2 0.0 collective-permute-done.3
  182.3 1.8 collective-permute-done.4
  184.1 0.1 bitcast_select_fusion.1
  184.2 1.1 pad_maximum_fusion.1.refs_1_
  185.3 52.3 %all-to-all-done.1.refs_0_ = bf16[32,2,2,2,16,128]{5,4,3,2,1,0:T(8,128)(2,1)S(1)} async-done(((bf16[32,2,2,2,16,128]{5,4,3,2,1,0:T(8,128)(2,1)}), bf16[32,2,2,2,16,128]{5,4,3,2,1,0:T(8,128)(2,1)S(1)}, u32[]{:S(2)}, u32[]{:S(2)}) %all-to-all-start.1) | async-done | bytes 1048608 | tf_op jit(solution)/shard_map/all_to_all | solution.py:477
  237.6 1.0 copy-done.3
  238.6 3.7 %backward.1 = bf16[4,2,8,40,128]{4,3,2,1,0:T(8,128)(2,1)} custom-call(bf16[32,2,2,2,16,128]{5,4,3,2,1,0:T(8,128)(2,1)} %copy-done.3, bf16[2,2,2,512,128]{4,3,2,1,0:T(8,128)(2,1)} %pad_maximum_fusion.1.refs_1_, bf16[256,256]{1,0:T(8,128)(2,1)} %constant.44.clone.refs_2_), custom_call_target="tpu_custom_call" | custom-call | tf_op jit(solution)/shard_map/backward/pallas_call | solution.py:485
  242.3 13.4 %all_to_all.20 = bf16[4,2,8,40,128]{4,3,2,1,0:T(8,128)(2,1)S(1)} all-to-all(bf16[4,2,8,40,128]{4,3,2,1,0:T(8,128)(2,1)} %backward.1), channel_id=1, replica_groups=mesh['groups'=2,'slab'=32,'coil'=4,'row'=2] {'coil'}, dimensions={0} | all-to-all | bytes 1310720 | tf_op jit(solution)/shard_map/all_to_all | solution.py:503
  255.7 0.1 convert_reduce_fusion
  255.7 0.0 copy-start.8
  255.7 0.0 copy-start.9
  255.8 20.9 %collective-permute-start.5 = (bf16[2,8,40,128]{3,2,1,0:T(8,128)(2,1)S(1)}, bf16[2,8,40,128]{3,2,1,0:T(8,128)(2,1)S(1)}, u32[]{:S(2)}, u32[]{:S(2)}) collective-permute-start(bf16[2,8,40,128]{3,2,1,0:T(8,128)(2,1)S(1)} %convert_element_type.32), channel_id=1, source_target_pairs={{0,1},{1,0},{2,3},{3,2},{4,5},{5,4},{6,7},{7,6},{8,9},{9,8},{10,11... | collective-permute-start | bytes 491528 | tf_op jit(solution)/shard_map/ppermute | solution.py:504
  276.7 1.0 collective-permute-done.5
  277.7 0.0 copy-start.4
  277.8 2.0 collective-permute-start.6
  279.7 0.7 broadcast_multiply_fusion.refs_3_
  280.4 4.1 %collective-permute-done.6.refs_2_ = bf16[2,3,40,128]{3,2,1,0:T(8,128)(2,1)S(1)} collective-permute-done((bf16[2,3,40,128]{3,2,1,0:T(8,128)(2,1)S(1)}, bf16[2,3,40,128]{3,2,1,0:T(8,128)(2,1)S(1)}, u32[]{:S(2)}, u32[]{:S(2)}) %collective-permute-start.6) | collective-permute-done | bytes 61472 | tf_op jit(solution)/shard_map/ppermute | solution.py:514
  284.5 0.6 copy-done.6
  285.2 4.5 %wavelet.1 = bf16[4,2,128,128]{3,2,1,0:T(8,128)(2,1)} custom-call(s32[1]{0:T(128)} %bitcast._.r_ref.refs_0_, f32[2,8,40,128]{3,2,1,0:T(8,128)} %copy-done.4, bf16[2,3,40,128]{3,2,1,0:T(8,128)(2,1)} %copy-done.6, f32[2,7]{1,0:T(2,128)} %broadcast_multiply_fusion.refs_3_), custom_call_target="tpu_custom_call" | custom-call | tf_op jit(solution)/shard_map/wavelet/pallas_call | solution.py:305
  289.7 10.2 %all_to_all.21 = bf16[4,2,128,128]{3,2,1,0:T(8,128)(2,1)S(1)} all-to-all(bf16[4,2,128,128]{3,2,1,0:T(8,128)(2,1)} %wavelet.1), channel_id=1, replica_groups=mesh['groups'=2,'slab'=32,'coil'=4,'row'=2] {'coil'}, dimensions={0} | all-to-all | bytes 524288 | tf_op jit(solution)/shard_map/all_to_all | solution.py:516
  299.9 0.8 copy.19
  (25 shorter events, 0.3 us)
Async XLA Ops:
  2.7 4.8 %collective-permute-start = (bf16[32,2,2,16,128]{4,3,2,1,0:T(8,128)(2,1)}, bf16[32,2,2,16,128]{4,3,2,1,0:T(8,128)(2,1)S(1)}, u32[]{:S(2)}, u32[]{:S(2)}) collective-permute-start(bf16[32,2,2,16,128]{4,3,2,1,0:T(8,128)(2,1)} %forward_sent.1), channel_id=1, source_target_pairs={{0,1},{1,0},{2,3},{3,2},{4,5},{5,4},{6,7},{7,6},{8,9},{9,8},{10,11... | collective-permute-start | bytes 1572872 | tf_op jit(solution)/shard_map/ppermute | solution.py:370
  7.5 0.8 copy-start.5
  11.5 45.9 %copy-start.10 = (bf16[2,4,2,256,128]{4,3,2,1,0:T(8,128)(2,1)S(1)}, bf16[2,4,2,256,128]{4,3,2,1,0:T(8,128)(2,1)}, u32[]{:S(2)}) copy-start(bf16[2,4,2,256,128]{4,3,2,1,0:T(8,128)(2,1)} %param.13) | copy-start | bytes 3145732
  11.5 45.9 %copy-start.11 = (bf16[2,128,2,128,1,1]{3,1,0,5,4,2:T(8,128)(2,1)S(1)}, bf16[2,128,2,128,1,1]{3,1,0,5,4,2:T(8,128)(2,1)}, u32[]{:S(2)}) copy-start(bf16[2,128,2,128,1,1]{3,1,0,5,4,2:T(8,128)(2,1)} %constant.51) | copy-start | bytes 393220
  11.5 123.4 %all-to-all-start = ((bf16[32,2,2,2,16,128]{5,4,3,2,1,0:T(8,128)(2,1)}), bf16[32,2,2,2,16,128]{5,4,3,2,1,0:T(8,128)(2,1)S(1)}, u32[]{:S(2)}, u32[]{:S(2)}) async-start(bf16[32,2,2,2,16,128]{5,4,3,2,1,0:T(8,128)(2,1)} %get-tuple-element.12), calls=%async_computation | async-start | bytes 2097152 | tf_op jit(solution)/shard_map/all_to_all | solution.py:421
  57.8 36.4 %copy-start.7 = (s32[2,256]{1,0:T(2,128)S(1)}, s32[2,256]{1,0:T(2,128)}, u32[]{:S(2)}) copy-start(s32[2,256]{1,0:T(2,128)} %param.14) | copy-start | bytes 6148
  57.9 39.5 %collective-permute-start.1 = (bf16[2,2,2,256,128]{4,3,2,1,0:T(8,128)(2,1)S(1)}, bf16[2,2,2,256,128]{4,3,2,1,0:T(8,128)(2,1)S(1)}, u32[]{:S(2)}, u32[]{:S(2)}) collective-permute-start(bf16[2,2,2,256,128]{4,3,2,1,0:T(8,128)(2,1)S(1)} %dynamic-slice_bitcast_fusion.1), channel_id=1, source_target_pairs={{0,1},{1,0},{2,3},{3,2},{4,5},{5,4},{6,7},{7,6},{8,9},{9,8},{10,11... | collective-permute-start | bytes 1572872 | tf_op jit(solution)/shard_map/ppermute | solution.py:428
  94.3 3.1 %collective-permute-start.2 = (f32[2,256]{1,0:T(2,128)S(1)}, f32[2,256]{1,0:T(2,128)S(1)}, u32[]{:S(2)}, u32[]{:S(2)}) collective-permute-start(f32[2,256]{1,0:T(2,128)S(1)} %convert_element_type.30), channel_id=1, source_target_pairs={{0,1},{1,0},{2,3},{3,2},{4,5},{5,4},{6,7},{7,6},{8,9},{9,8},{10,11... | collective-permute-start | bytes 6152 | tf_op jit(solution)/shard_map/ppermute | solution.py:439
  134.8 1.1 copy-start.1
  140.3 10.8 %copy-start.2 = (f32[2,128,4,128]{3,2,1,0:T(4,128)S(1)}, f32[2,128,4,128]{3,2,1,0:T(4,128)}, u32[]{:S(2)}) copy-start(f32[2,128,4,128]{3,2,1,0:T(4,128)} %param.11) | copy-start | bytes 1572868
  140.3 97.3 %all-to-all-start.1 = ((bf16[32,2,2,2,16,128]{5,4,3,2,1,0:T(8,128)(2,1)}), bf16[32,2,2,2,16,128]{5,4,3,2,1,0:T(8,128)(2,1)S(1)}, u32[]{:S(2)}, u32[]{:S(2)}) async-start(bf16[32,2,2,2,16,128]{5,4,3,2,1,0:T(8,128)(2,1)} %middle.1), calls=%async_computation.1 | async-start | bytes 2097152 | tf_op jit(solution)/shard_map/all_to_all | solution.py:477
  151.1 29.1 %copy-start = (bf16[2,4,128,4,128]{4,3,2,1,0:T(4,128)(2,1)S(1)}, bf16[2,4,128,4,128]{4,3,2,1,0:T(4,128)(2,1)}, u32[]{:S(2)}) copy-start(bf16[2,4,128,4,128]{4,3,2,1,0:T(4,128)(2,1)} %param.12) | copy-start | bytes 3145732
  151.3 31.0 %collective-permute-start.3 = (f32[2,4,40,128]{3,2,1,0:T(8,128)S(1)}, f32[2,4,40,128]{3,2,1,0:T(8,128)S(1)}, u32[]{:S(2)}, u32[]{:S(2)}) collective-permute-start(f32[2,4,40,128]{3,2,1,0:T(8,128)S(1)} %fusion.3), channel_id=1, source_target_pairs={{0,1},{1,0},{2,3},{3,2},{4,5},{5,4},{6,7},{7,6},{8,9},{9,8},{10,11... | collective-permute-start | bytes 491528 | tf_op jit(solution)/shard_map/ppermute | solution.py:451
  180.3 3.8 %collective-permute-start.4 = (bf16[2,2,1,512,128]{4,3,2,1,0:T(8,128)(2,1)S(1)}, bf16[2,2,1,512,128]{4,3,2,1,0:T(8,128)(2,1)S(1)}, u32[]{:S(2)}, u32[]{:S(2)}) collective-permute-start(bf16[2,2,1,512,128]{4,3,2,1,0:T(8,128)(2,1)S(1)} %dynamic-slice_bitcast_fusion), channel_id=1, source_target_pairs={{0,1},{1,0},{2,3},{3,2},{4,5},{5,4},{6,7},{7,6},{8,9},{9,8},{10,11... | collective-permute-start | bytes 1572872 | tf_op jit(solution)/shard_map/ppermute | solution.py:428
  237.6 1.0 copy-start.3
  255.7 24.0 %copy-start.8 = (f32[2,7]{1,0:T(2,128)S(1)}, f32[2,7]{1,0:T(2,128)}, u32[]{:S(2)}) copy-start(f32[2,7]{1,0:T(2,128)} %param.15) | copy-start | bytes 172
  255.7 24.0 %copy-start.9 = (f32[2]{0:T(128)S(1)}, f32[2]{0:T(128)}, u32[]{:S(2)}) copy-start(f32[2]{0:T(128)} %constant.50) | copy-start | bytes 28
  255.8 21.9 %collective-permute-start.5 = (bf16[2,8,40,128]{3,2,1,0:T(8,128)(2,1)S(1)}, bf16[2,8,40,128]{3,2,1,0:T(8,128)(2,1)S(1)}, u32[]{:S(2)}, u32[]{:S(2)}) collective-permute-start(bf16[2,8,40,128]{3,2,1,0:T(8,128)(2,1)S(1)} %convert_element_type.32), channel_id=1, source_target_pairs={{0,1},{1,0},{2,3},{3,2},{4,5},{5,4},{6,7},{7,6},{8,9},{9,8},{10,11... | collective-permute-start | bytes 491528 | tf_op jit(solution)/shard_map/ppermute | solution.py:504
  277.7 6.8 %copy-start.4 = (f32[2,8,40,128]{3,2,1,0:T(8,128)}, f32[2,8,40,128]{3,2,1,0:T(8,128)S(1)}, u32[]{:S(2)}) copy-start(f32[2,8,40,128]{3,2,1,0:T(8,128)S(1)} %multiply_subtract_fusion.refs_1_) | copy-start | bytes 983044
  277.8 6.8 %collective-permute-start.6 = (bf16[2,3,40,128]{3,2,1,0:T(8,128)(2,1)S(1)}, bf16[2,3,40,128]{3,2,1,0:T(8,128)(2,1)S(1)}, u32[]{:S(2)}, u32[]{:S(2)}) collective-permute-start(bf16[2,3,40,128]{3,2,1,0:T(8,128)(2,1)S(1)} %dynamic-slice_convert_fusion), channel_id=1, source_target_pairs={{1,8},{8,1},{9,16},{16,9},{17,24},{24,17},{25,32},{32,25},{33,40},... | collective-permute-start | bytes 184328 | tf_op jit(solution)/shard_map/ppermute | solution.py:514
  284.5 0.6 copy-start.6

commit v4 on v3

--- a/solution.py
+++ b/solution.py
@@ -32,7 +32,7 @@
     return jnp.dot(left, right, preferred_element_type=jnp.float32)
 
 
-def forward_kernel(slabs, lines, planes, sens_ref, image_ref, table_ref, out_ref, product, mixed):
+def forward_kernel(slabs, lines, planes, coil, sens_ref, image_ref, table_ref, out_ref, product, mixed):
     cells = product.shape[1] // planes
     group = lines * planes
     sr = sens_ref[0, 0].astype(jnp.float32)
@@ -57,16 +57,18 @@
                 mixed[s, pl.ds(z * lines + line, slabs, stride=group), :] = done[
                     first : first + slabs, z * width : (z + 1) * width
                 ]
-        out_ref[:, s, 0] = mixed[s].astype(jnp.bfloat16).reshape(slabs, group, width)
-
-
-def middle_kernel(lines, lower_ref, upper_ref, measured_ref, mask_ref, table_ref, inverse_ref, out_ref, mixed, back):
-    slabs, _, _, _, group, width = lower_ref.shape
+        out_ref[:, s, coil] = mixed[s].astype(jnp.bfloat16).reshape(slabs, group, width)
+
+
+def middle_kernel(lines, row_ref, in_ref, measured_ref, mask_ref, table_ref, inverse_ref, out_ref, mixed, back):
+    slabs, _, _, _, group, width = in_ref.shape
     half = slabs * group // lines
     cells = 2 * half
-    for row, ref in enumerate((lower_ref, upper_ref)):
+    coil = pl.program_id(0)
+    for row in range(2):
+        place = row_ref[0] if row == 0 else 1 - row_ref[0]
         for t in range(2):
-            mixed[row, t] = ref[:, 0, t, 0].astype(jnp.float32).reshape(slabs * group, width)
+            mixed[row, t] = in_ref[:, place, t, coil].astype(jnp.float32).reshape(slabs * group, width)
     columns = [
         jnp.concatenate(
             [
@@ -84,7 +86,7 @@
         parts = []
         for t in range(2):
             value = spectrum[t * cells : (t + 1) * cells, line * width : (line + 1) * width]
-            value = mask_ref[line] * (value - measured_ref[t, 0, line].astype(jnp.float32))
+            value = mask_ref[line] * (value - measured_ref[t, coil, line].astype(jnp.float32))
             parts.append(value.astype(jnp.bfloat16))
         residual.append(jnp.concatenate(parts, axis=0))
     result = dot(inverse_ref[...], jnp.concatenate(residual, axis=1))
@@ -109,8 +111,8 @@
 
     for row in range(rows):
         for t in range(2):
-            mixed[row, t] = in_ref[:, row, t, 0].astype(jnp.float32).reshape(slabs * group, width)
-            wide[row, t] = sens_ref[t, 0, row].astype(jnp.float32)
+            mixed[row, t] = in_ref[:, row, t, coil].astype(jnp.float32).reshape(slabs * group, width)
+            wide[row, t] = sens_ref[t, coil, row].astype(jnp.float32)
     columns = [
         jnp.concatenate(
             [
@@ -274,6 +276,13 @@
             out_ref[copy, t] = kept
 
 
+def resident(array):
+    return pltpu.with_memory_space_constraint(array, pltpu.VMEM)
+
+
+in_place = pl.BlockSpec(memory_space=pltpu.VMEM)
+
+
 def whole(array):
     shape = array.shape
     return pl.BlockSpec(shape, lambda *_: (0,) * len(shape))
@@ -304,17 +313,17 @@
 
     return pl.pallas_call(
         kernel,
-        out_shape=jax.ShapeDtypeStruct((copies, 2, (rows - 2 * edge) * planes, width), jnp.bfloat16),
+        out_shape=pltpu.VMEM((copies, 2, (rows - 2 * edge) * planes, width), jnp.bfloat16),
         in_specs=[
             pl.BlockSpec(memory_space=pltpu.SMEM),
-            pl.BlockSpec(memory_space=pltpu.VMEM),
-            pl.BlockSpec(memory_space=pltpu.VMEM),
+            in_place,
+            in_place,
             pl.BlockSpec(memory_space=pltpu.SMEM),
         ],
         out_specs=pl.BlockSpec(memory_space=pltpu.VMEM),
         scratch_shapes=buffers,
         name="wavelet",
-    )(row, chip, halo, limits)
+    )(row, resident(chip), resident(halo), limits)
 
 
 def local(image, sens, measured, mask, thresholds):
@@ -349,7 +358,7 @@
         return pl.pallas_call(kernel, grid_spec=grid_spec, out_shape=out_shape, name=name)
 
     def send_kernel(_, *refs):
-        forward_kernel(slabs, lines, planes, *refs)
+        forward_kernel(slabs, lines, planes, pl.program_id(0), *refs)
 
     sent = given(
         send_kernel,
@@ -361,16 +370,16 @@
                 whole(image_rows),
                 whole(table_phase),
             ],
-            out_specs=pl.BlockSpec((slabs, 2, 1, group, width), lambda c, r: (0, 0, c, 0, 0)),
+            out_specs=in_place,
             scratch_shapes=[stack, stack],
         ),
-        jax.ShapeDtypeStruct(piece, bf16),
+        pltpu.VMEM(piece, bf16),
         "forward_sent",
     )(here, sens_rows, image_rows, table_phase)
     arrived = lax.ppermute(sent, "row", other)
 
     def keep_kernel(_, sens_ref, image_ref, table_ref, out_ref, product, mixed):
-        forward_kernel(slabs, lines, planes, sens_ref, image_ref, table_ref, out_ref.at[:, 0], product, mixed)
+        forward_kernel(slabs, lines, planes, 0, sens_ref, image_ref, table_ref, out_ref.at[:, 0], product, mixed)
 
     kept = given(
         keep_kernel,
@@ -389,34 +398,27 @@
         "forward_kept",
     )(here, sens_rows, image_rows, table_phase)
 
-    def place_kernel(r_ref, _, arrived_ref, out_ref, pause_ref):
-        @pl.when(pl.program_id(0) == 0)
-        def _():
-            pause_ref[...] = lax.fori_loop(
-                0, r_ref[0] * pause_steps, lambda _, v: v * 1.0001 + 0.5, jnp.ones(pause_ref.shape, jnp.float32)
-            )
-
-        out_ref[:, 0] = arrived_ref[...]
-
-    pieces = 4
+    def place_kernel(r_ref, _, arrived_ref, out_ref, pause_ref, done):
+        copy = pltpu.make_async_copy(arrived_ref, out_ref.at[:, 1], done)
+        copy.start()
+        pause_ref[...] = lax.fori_loop(
+            0, r_ref[0] * pause_steps, lambda _, v: v * 1.0001 + 0.5, jnp.ones(pause_ref.shape, jnp.float32)
+        )
+        copy.wait()
+
     outgoing, _ = pl.pallas_call(
         place_kernel,
-        grid_spec=pltpu.PrefetchScalarGridSpec(
-            num_scalar_prefetch=1,
-            grid=(pieces,),
-            in_specs=[
-                pl.BlockSpec(memory_space=pl.ANY),
-                pl.BlockSpec((slabs // pieces, 2, half, group, width), lambda i, r: (i, 0, 0, 0, 0)),
-            ],
-            out_specs=[
-                pl.BlockSpec((slabs // pieces, 1, 2, half, group, width), lambda i, r: (i, 1, 0, 0, 0, 0)),
-                pl.BlockSpec((8, 128), lambda i, r: (0, 0)),
-            ],
-        ),
+        in_specs=[
+            pl.BlockSpec(memory_space=pltpu.SMEM),
+            pl.BlockSpec(memory_space=pl.ANY),
+            in_place,
+        ],
+        out_specs=[pl.BlockSpec(memory_space=pl.ANY), pl.BlockSpec(memory_space=pltpu.VMEM)],
         out_shape=[exchanged, jax.ShapeDtypeStruct((8, 128), f32)],
+        scratch_shapes=[pltpu.SemaphoreType.DMA],
         input_output_aliases={1: 0},
         name="place",
-    )(here, kept, arrived)
+    )(here, kept, resident(arrived))
 
     received = lax.all_to_all(outgoing, "slab", 0, 0, tiled=True)
 
@@ -450,10 +452,9 @@
     )
     chip_image = in_row_order(own_image, lax.ppermute(own_image, "row", other), 1)
 
-    def mid_kernel(_, *refs):
+    def mid_kernel(*refs):
         middle_kernel(lines, *refs)
 
-    block = (slabs, 1, 2, 1, group, width)
     buffer = pltpu.VMEM((rows, 2, slabs * group, width), f32)
     returning = given(
         mid_kernel,
@@ -461,10 +462,9 @@
             num_scalar_prefetch=1,
             grid=(half,),
             in_specs=[
-                pl.BlockSpec(block, lambda c, r: (0, r[0], 0, c, 0, 0)),
-                pl.BlockSpec(block, lambda c, r: (0, 1 - r[0], 0, c, 0, 0)),
-                pl.BlockSpec((2, 1, lines, depth_cells, width), lambda c, r: (0, c, 0, 0, 0)),
-                whole(wide_mask),
+                in_place,
+                in_place,
+                in_place,
                 whole(table_depth),
                 whole(inverse_depth),
             ],
@@ -473,7 +473,7 @@
         ),
         exchanged,
         "middle",
-    )(here, received, received, chip_measured, wide_mask, table_depth, inverse_depth)
+    )(here, *map(resident, (received, chip_measured, wide_mask)), table_depth, inverse_depth)
     returned = lax.all_to_all(returning, "slab", 0, 0, tiled=True)
     returned, chip_image = lax.optimization_barrier((returned, chip_image))
 
@@ -485,13 +485,9 @@
     parts = pl.pallas_call(
         back_kernel,
         grid=(half,),
-        out_shape=jax.ShapeDtypeStruct((columns, 2, rows * planes, tall, width), bf16),
-        in_specs=[
-            pl.BlockSpec((slabs, rows, 2, 1, group, width), lambda c: (0, 0, 0, c, 0, 0)),
-            pl.BlockSpec((2, 1, rows, phase_cells * planes, width), lambda c: (0, c, 0, 0, 0)),
-            whole(inverse_phase),
-        ],
-        out_specs=pl.BlockSpec((columns, 2, rows * planes, tall, width), lambda c: (0, 0, 0, 0, 0)),
+        out_shape=pltpu.VMEM((columns, 2, rows * planes, tall, width), bf16),
+        in_specs=[in_place, in_place, whole(inverse_phase)],
+        out_specs=in_place,
         scratch_shapes=[
             buffer,
             buffer,
@@ -499,7 +495,7 @@
             pltpu.VMEM((phase_cells + 2 * edge, width), f32),
         ],
         name="backward",
-    )(returned, chip_sens, inverse_phase)
+    )(resident(returned), resident(chip_sens), inverse_phase)
     share = lax.all_to_all(parts, "coil", 0, 0, tiled=True).astype(f32).sum(axis=0)
     others = lax.ppermute(share.astype(bf16), "row", other)
     chip = chip_image - step_size * (share + others.astype(f32))

time: 302 us -> 297 us (0.983)
  starting transfers between devices: 151 us -> 159 us
  Pallas kernels: 21.2 us -> 16.2 us
  local copies, waits for them, and re-layouts: 4.55 us -> 1.21 us
    ppermute x1, starting transfers between devices: 20.9 us -> 29.3 us  [local(): others = lax.ppermute(share.astype(bf16), 'row', other)]
    pallas_call x3, Pallas kernels: 11.3 us -> 7.45 us  [the longest x1 3.48 us: shrink(): pl.pallas_call(kernel, out_shape=pltpu.VMEM((copies, 2, (rows - 2 * edge)...]
where the time goes in v4:
time: 297 us
  starting transfers between devices  159 us (54%)
  waiting for transfers between devices  96.1 us (32%)
  blocking collectives  22.3 us (8%)
  Pallas kernels  16.2 us (5%)
    all_to_all x1, waiting for transfers between devices, local(): returned = lax.all_to_all(returning, 'slab', 0, 0, tiled=True)  50.2 us
    all_to_all x1, starting transfers between devices, local(): received = lax.all_to_all(outgoing, 'slab', 0, 0, tiled=True)  45.9 us
    all_to_all x1, waiting for transfers between devices, local(): received = lax.all_to_all(outgoing, 'slab', 0, 0, tiled=True)  37.7 us
    ppermute x2, starting transfers between devices, both_rows(): return in_row_order(kept, lax.ppermute(away, 'row', other), axis)  37.5 us
    ppermute x1, starting transfers between devices, local(): others = lax.ppermute(share.astype(bf16), 'row', other)  29.3 us
    ppermute x1, starting transfers between devices, local(): lax.ppermute(own_image, 'row', other)  26.7 us
    all_to_all x1, starting transfers between devices, local(): returned = lax.all_to_all(returning, 'slab', 0, 0, tiled=True)  13.4 us
    all_to_all x1, blocking collectives, local(): lax.all_to_all(parts, 'coil', 0, 0, tiled=True).astype(f32).sum(axis=0)  13.2 us
  transfers between devices with their start and end apart: 9, of which 6 were waited for; matrix products, arithmetic and copies ran while one was open for 1% of the time, Pallas kernels for 1%

profile of v4, /device:TPU:40, one launch (start us, length us, event | category | flops | bytes accessed | tf_op | source)
XLA Modules:
  0.0 296.6 jit_solution(12328798626710150125)
XLA Ops:
  0.0 2.1 forward_sent.1
  2.1 2.0 collective-permute-start
  4.0 2.8 forward_kept.1._
  6.8 0.0 collective-permute-done.arrived_ref
  6.8 1.4 place.1
  8.2 0.0 copy-start.5
  8.2 0.0 copy-start.6
  8.2 45.9 %all-to-all-start = ((bf16[32,2,2,2,16,128]{5,4,3,2,1,0:T(8,128)(2,1)}), bf16[32,2,2,2,16,128]{5,4,3,2,1,0:T(8,128)(2,1)S(1)}, u32[]{:S(2)}, u32[]{:S(2)}) async-start(bf16[32,2,2,2,16,128]{5,4,3,2,1,0:T(8,128)(2,1)} %get-tuple-element.12), calls=%async_computation | async-start | bytes 2097152 | tf_op jit(solution)/shard_map/all_to_all | solution.py:423
  54.2 0.0 copy-done.5
  54.2 0.0 copy-done.6
  54.2 0.4 bitcast_convert_fusion
  54.6 0.0 copy-start.2
  54.7 35.6 %collective-permute-start.1 = (bf16[2,2,2,256,128]{4,3,2,1,0:T(8,128)(2,1)S(1)}, bf16[2,2,2,256,128]{4,3,2,1,0:T(8,128)(2,1)S(1)}, u32[]{:S(2)}, u32[]{:S(2)}) collective-permute-start(bf16[2,2,2,256,128]{4,3,2,1,0:T(8,128)(2,1)S(1)} %dynamic-slice_bitcast_fusion.1), channel_id=1, source_target_pairs={{0,1},{1,0},{2,3},{3,2},{4,5},{5,4},{6,7},{7,6},{8,9},{9,8},{10,11... | collective-permute-start | bytes 1572872 | tf_op jit(solution)/shard_map/ppermute | solution.py:430
  90.3 0.0 copy-done.2
  90.3 2.0 collective-permute-start.2
  92.2 1.1 collective-permute-done.2
  93.4 0.0 collective-permute-done.1
  93.4 0.1 bitcast_select_fusion.3
  93.5 0.1 pad_maximum_fusion.refs_2_
  93.6 37.7 %all-to-all-done.refs_1_ = bf16[32,2,2,2,16,128]{5,4,3,2,1,0:T(8,128)(2,1)S(1)} async-done(((bf16[32,2,2,2,16,128]{5,4,3,2,1,0:T(8,128)(2,1)}), bf16[32,2,2,2,16,128]{5,4,3,2,1,0:T(8,128)(2,1)S(1)}, u32[]{:S(2)}, u32[]{:S(2)}) %all-to-all-start) | async-done | bytes 1048608 | tf_op jit(solution)/shard_map/all_to_all | solution.py:423
  131.3 0.2 broadcast_in_dim.2.refs_3_
  131.5 3.9 %middle.1 = bf16[32,2,2,2,16,128]{5,4,3,2,1,0:T(8,128)(2,1)} custom-call(s32[1]{0:T(128)} %bitcast._.r_ref.refs_0_, bf16[32,2,2,2,16,128]{5,4,3,2,1,0:T(8,128)(2,1)S(1)} %all-to-all-done.refs_1_, bf16[2,2,4,256,128]{4,3,2,1,0:T(8,128)(2,1)S(1)} %pad_maximum_fusion.refs_2_, f32[4,256,128]{2,1,0:T(8,128)S(1)} %broadcast_in_dim.2.refs_3_, ...), custom_call_target="tpu_custom_call" | custom-call | tf_op jit(solution)/shard_map/middle/pallas_call | solution.py:459
  135.4 13.4 %all-to-all-start.1 = ((bf16[32,2,2,2,16,128]{5,4,3,2,1,0:T(8,128)(2,1)}), bf16[32,2,2,2,16,128]{5,4,3,2,1,0:T(8,128)(2,1)S(1)}, u32[]{:S(2)}, u32[]{:S(2)}) async-start(bf16[32,2,2,2,16,128]{5,4,3,2,1,0:T(8,128)(2,1)} %middle.1), calls=%async_computation.1 | async-start | bytes 2097152 | tf_op jit(solution)/shard_map/all_to_all | solution.py:477
  148.9 0.0 copy-start
  148.9 0.0 copy-done.1
  149.0 0.1 fusion.3
  149.0 26.7 %collective-permute-start.3 = (f32[2,4,40,128]{3,2,1,0:T(8,128)S(1)}, f32[2,4,40,128]{3,2,1,0:T(8,128)S(1)}, u32[]{:S(2)}, u32[]{:S(2)}) collective-permute-start(f32[2,4,40,128]{3,2,1,0:T(8,128)S(1)} %fusion.3), channel_id=1, source_target_pairs={{0,1},{1,0},{2,3},{3,2},{4,5},{5,4},{6,7},{7,6},{8,9},{9,8},{10,11... | collective-permute-start | bytes 491528 | tf_op jit(solution)/shard_map/ppermute | solution.py:453
  175.7 0.0 copy-done
  175.8 2.0 collective-permute-start.4
  177.7 0.0 collective-permute-done.3
  177.8 1.8 collective-permute-done.4
  179.6 0.1 bitcast_select_fusion.1
  179.7 0.1 pad_maximum_fusion.1.refs_1_
  179.8 50.2 %all-to-all-done.1.refs_0_ = bf16[32,2,2,2,16,128]{5,4,3,2,1,0:T(8,128)(2,1)S(1)} async-done(((bf16[32,2,2,2,16,128]{5,4,3,2,1,0:T(8,128)(2,1)}), bf16[32,2,2,2,16,128]{5,4,3,2,1,0:T(8,128)(2,1)S(1)}, u32[]{:S(2)}, u32[]{:S(2)}) %all-to-all-start.1) | async-done | bytes 1048608 | tf_op jit(solution)/shard_map/all_to_all | solution.py:477
  230.0 2.6 backward.1
  232.6 13.2 %all_to_all.20 = bf16[4,2,8,40,128]{4,3,2,1,0:T(8,128)(2,1)S(1)} all-to-all(bf16[4,2,8,40,128]{4,3,2,1,0:T(8,128)(2,1)S(1)} %backward.1), channel_id=1, replica_groups=mesh['groups'=2,'slab'=32,'coil'=4,'row'=2] {'coil'}, dimensions={0} | all-to-all | bytes 1310720 | tf_op jit(solution)/shard_map/all_to_all | solution.py:499
  245.8 0.1 convert_reduce_fusion
  245.9 0.0 copy-start.3
  245.9 0.0 copy-start.4
  245.9 29.3 %collective-permute-start.5 = (bf16[2,8,40,128]{3,2,1,0:T(8,128)(2,1)S(1)}, bf16[2,8,40,128]{3,2,1,0:T(8,128)(2,1)S(1)}, u32[]{:S(2)}, u32[]{:S(2)}) collective-permute-start(bf16[2,8,40,128]{3,2,1,0:T(8,128)(2,1)S(1)} %convert_element_type.32), channel_id=1, source_target_pairs={{0,1},{1,0},{2,3},{3,2},{4,5},{5,4},{6,7},{7,6},{8,9},{9,8},{10,11... | collective-permute-start | bytes 491528 | tf_op jit(solution)/shard_map/ppermute | solution.py:500
  275.2 1.0 collective-permute-done.5
  276.3 2.0 collective-permute-start.6
  278.3 0.0 copy-done.3
  278.3 0.6 broadcast_multiply_fusion.refs_3_
  278.9 4.2 %collective-permute-done.6.refs_2_ = bf16[2,3,40,128]{3,2,1,0:T(8,128)(2,1)S(1)} collective-permute-done((bf16[2,3,40,128]{3,2,1,0:T(8,128)(2,1)S(1)}, bf16[2,3,40,128]{3,2,1,0:T(8,128)(2,1)S(1)}, u32[]{:S(2)}, u32[]{:S(2)}) %collective-permute-start.6) | collective-permute-done | bytes 61472 | tf_op jit(solution)/shard_map/ppermute | solution.py:510
  283.1 3.5 %wavelet.1 = bf16[4,2,128,128]{3,2,1,0:T(8,128)(2,1)S(1)} custom-call(s32[1]{0:T(128)} %bitcast._.r_ref.refs_0_, f32[2,8,40,128]{3,2,1,0:T(8,128)S(1)} %multiply_subtract_fusion.refs_1_, bf16[2,3,40,128]{3,2,1,0:T(8,128)(2,1)S(1)} %collective-permute-done.6.refs_2_, f32[2,7]{1,0:T(2,128)} %broadcast_multiply_fusion.refs_3_), custom_call_target="tpu_custom_call" | custom-call | tf_op jit(solution)/shard_map/wavelet/pallas_call | solution.py:314
  286.6 9.1 %all_to_all.21 = bf16[4,2,128,128]{3,2,1,0:T(8,128)(2,1)S(1)} all-to-all(bf16[4,2,128,128]{3,2,1,0:T(8,128)(2,1)S(1)} %wavelet.1), channel_id=1, replica_groups=mesh['groups'=2,'slab'=32,'coil'=4,'row'=2] {'coil'}, dimensions={0} | all-to-all | bytes 524288 | tf_op jit(solution)/shard_map/all_to_all | solution.py:512
  295.7 0.8 copy.19
  (15 shorter events, 0.3 us)
Async XLA Ops:
  2.1 4.7 %collective-permute-start = (bf16[32,2,2,16,128]{4,3,2,1,0:T(8,128)(2,1)S(1)}, bf16[32,2,2,16,128]{4,3,2,1,0:T(8,128)(2,1)S(1)}, u32[]{:S(2)}, u32[]{:S(2)}) collective-permute-start(bf16[32,2,2,16,128]{4,3,2,1,0:T(8,128)(2,1)S(1)} %forward_sent.1), channel_id=1, source_target_pairs={{0,1},{1,0},{2,3},{3,2},{4,5},{5,4},{6,7},{7,6},{8,9},{9,8},{10,11... | collective-permute-start | bytes 1572872 | tf_op jit(solution)/shard_map/ppermute | solution.py:379
  8.2 45.9 %copy-start.5 = (bf16[2,4,2,256,128]{4,3,2,1,0:T(8,128)(2,1)S(1)}, bf16[2,4,2,256,128]{4,3,2,1,0:T(8,128)(2,1)}, u32[]{:S(2)}) copy-start(bf16[2,4,2,256,128]{4,3,2,1,0:T(8,128)(2,1)} %param.13) | copy-start | bytes 3145732
  8.2 45.9 %copy-start.6 = (bf16[2,128,2,128,1,1]{3,1,0,5,4,2:T(8,128)(2,1)S(1)}, bf16[2,128,2,128,1,1]{3,1,0,5,4,2:T(8,128)(2,1)}, u32[]{:S(2)}) copy-start(bf16[2,128,2,128,1,1]{3,1,0,5,4,2:T(8,128)(2,1)} %constant.51) | copy-start | bytes 393220
  8.2 123.1 %all-to-all-start = ((bf16[32,2,2,2,16,128]{5,4,3,2,1,0:T(8,128)(2,1)}), bf16[32,2,2,2,16,128]{5,4,3,2,1,0:T(8,128)(2,1)S(1)}, u32[]{:S(2)}, u32[]{:S(2)}) async-start(bf16[32,2,2,2,16,128]{5,4,3,2,1,0:T(8,128)(2,1)} %get-tuple-element.12), calls=%async_computation | async-start | bytes 2097152 | tf_op jit(solution)/shard_map/all_to_all | solution.py:423
  54.6 35.7 %copy-start.2 = (s32[2,256]{1,0:T(2,128)S(1)}, s32[2,256]{1,0:T(2,128)}, u32[]{:S(2)}) copy-start(s32[2,256]{1,0:T(2,128)} %param.14) | copy-start | bytes 6148
  54.7 38.7 %collective-permute-start.1 = (bf16[2,2,2,256,128]{4,3,2,1,0:T(8,128)(2,1)S(1)}, bf16[2,2,2,256,128]{4,3,2,1,0:T(8,128)(2,1)S(1)}, u32[]{:S(2)}, u32[]{:S(2)}) collective-permute-start(bf16[2,2,2,256,128]{4,3,2,1,0:T(8,128)(2,1)S(1)} %dynamic-slice_bitcast_fusion.1), channel_id=1, source_target_pairs={{0,1},{1,0},{2,3},{3,2},{4,5},{5,4},{6,7},{7,6},{8,9},{9,8},{10,11... | collective-permute-start | bytes 1572872 | tf_op jit(solution)/shard_map/ppermute | solution.py:430
  90.3 3.1 %collective-permute-start.2 = (f32[2,256]{1,0:T(2,128)S(1)}, f32[2,256]{1,0:T(2,128)S(1)}, u32[]{:S(2)}, u32[]{:S(2)}) collective-permute-start(f32[2,256]{1,0:T(2,128)S(1)} %convert_element_type.30), channel_id=1, source_target_pairs={{0,1},{1,0},{2,3},{3,2},{4,5},{5,4},{6,7},{7,6},{8,9},{9,8},{10,11... | collective-permute-start | bytes 6152 | tf_op jit(solution)/shard_map/ppermute | solution.py:441
  135.4 13.5 %copy-start.1 = (f32[2,128,4,128]{3,2,1,0:T(4,128)S(1)}, f32[2,128,4,128]{3,2,1,0:T(4,128)}, u32[]{:S(2)}) copy-start(f32[2,128,4,128]{3,2,1,0:T(4,128)} %param.11) | copy-start | bytes 1572868
  135.4 94.6 %all-to-all-start.1 = ((bf16[32,2,2,2,16,128]{5,4,3,2,1,0:T(8,128)(2,1)}), bf16[32,2,2,2,16,128]{5,4,3,2,1,0:T(8,128)(2,1)S(1)}, u32[]{:S(2)}, u32[]{:S(2)}) async-start(bf16[32,2,2,2,16,128]{5,4,3,2,1,0:T(8,128)(2,1)} %middle.1), calls=%async_computation.1 | async-start | bytes 2097152 | tf_op jit(solution)/shard_map/all_to_all | solution.py:477
  148.9 26.8 %copy-start = (bf16[2,4,128,4,128]{4,3,2,1,0:T(4,128)(2,1)S(1)}, bf16[2,4,128,4,128]{4,3,2,1,0:T(4,128)(2,1)}, u32[]{:S(2)}) copy-start(bf16[2,4,128,4,128]{4,3,2,1,0:T(4,128)(2,1)} %param.12) | copy-start | bytes 3145732
  149.0 28.7 %collective-permute-start.3 = (f32[2,4,40,128]{3,2,1,0:T(8,128)S(1)}, f32[2,4,40,128]{3,2,1,0:T(8,128)S(1)}, u32[]{:S(2)}, u32[]{:S(2)}) collective-permute-start(f32[2,4,40,128]{3,2,1,0:T(8,128)S(1)} %fusion.3), channel_id=1, source_target_pairs={{0,1},{1,0},{2,3},{3,2},{4,5},{5,4},{6,7},{7,6},{8,9},{9,8},{10,11... | collective-permute-start | bytes 491528 | tf_op jit(solution)/shard_map/ppermute | solution.py:453
  175.8 3.8 %collective-permute-start.4 = (bf16[2,2,1,512,128]{4,3,2,1,0:T(8,128)(2,1)S(1)}, bf16[2,2,1,512,128]{4,3,2,1,0:T(8,128)(2,1)S(1)}, u32[]{:S(2)}, u32[]{:S(2)}) collective-permute-start(bf16[2,2,1,512,128]{4,3,2,1,0:T(8,128)(2,1)S(1)} %dynamic-slice_bitcast_fusion), channel_id=1, source_target_pairs={{0,1},{1,0},{2,3},{3,2},{4,5},{5,4},{6,7},{7,6},{8,9},{9,8},{10,11... | collective-permute-start | bytes 1572872 | tf_op jit(solution)/shard_map/ppermute | solution.py:430
  245.9 32.4 %copy-start.3 = (f32[2,7]{1,0:T(2,128)S(1)}, f32[2,7]{1,0:T(2,128)}, u32[]{:S(2)}) copy-start(f32[2,7]{1,0:T(2,128)} %param.15) | copy-start | bytes 172
  245.9 32.4 %copy-start.4 = (f32[2]{0:T(128)S(1)}, f32[2]{0:T(128)}, u32[]{:S(2)}) copy-start(f32[2]{0:T(128)} %constant.50) | copy-start | bytes 28
  245.9 30.3 %collective-permute-start.5 = (bf16[2,8,40,128]{3,2,1,0:T(8,128)(2,1)S(1)}, bf16[2,8,40,128]{3,2,1,0:T(8,128)(2,1)S(1)}, u32[]{:S(2)}, u32[]{:S(2)}) collective-permute-start(bf16[2,8,40,128]{3,2,1,0:T(8,128)(2,1)S(1)} %convert_element_type.32), channel_id=1, source_target_pairs={{0,1},{1,0},{2,3},{3,2},{4,5},{5,4},{6,7},{7,6},{8,9},{9,8},{10,11... | collective-permute-start | bytes 491528 | tf_op jit(solution)/shard_map/ppermute | solution.py:500
  276.3 6.8 %collective-permute-start.6 = (bf16[2,3,40,128]{3,2,1,0:T(8,128)(2,1)S(1)}, bf16[2,3,40,128]{3,2,1,0:T(8,128)(2,1)S(1)}, u32[]{:S(2)}, u32[]{:S(2)}) collective-permute-start(bf16[2,3,40,128]{3,2,1,0:T(8,128)(2,1)S(1)} %dynamic-slice_convert_fusion), channel_id=1, source_target_pairs={{1,8},{8,1},{9,16},{16,9},{17,24},{24,17},{25,32},{32,25},{33,40},... | collective-permute-start | bytes 184328 | tf_op jit(solution)/shard_map/ppermute | solution.py:510

commit v5 on v4

--- a/solution.py
+++ b/solution.py
@@ -11,7 +11,7 @@
 
 step_size = 0.5
 lines_axes = ("slab", "row")
-pause_steps = 6500
+pause_steps = 7100
 
 
 def fourier_table(length, sign, rows=None, columns=None):
@@ -475,7 +475,14 @@
         "middle",
     )(here, *map(resident, (received, chip_measured, wide_mask)), table_depth, inverse_depth)
     returned = lax.all_to_all(returning, "slab", 0, 0, tiled=True)
-    returned, chip_image = lax.optimization_barrier((returned, chip_image))
+    margin = 2 ** thresholds.shape[0] - 1
+    around = []
+    for slab in range(slabs):
+        after = (slab + 1) % slabs
+        around += [(slab * rows + rows - 1, after * rows), (after * rows, slab * rows + rows - 1)]
+    border = jnp.where(row == 0, own_image[:, :margin], own_image[:, planes - margin :])
+    halo_image = lax.ppermute(border, lines_axes, around)
+    returned, chip_image, halo_image = lax.optimization_barrier((returned, chip_image, halo_image))
 
     tall = quarter + 2 * edge
 
@@ -497,17 +504,23 @@
         name="backward",
     )(resident(returned), resident(chip_sens), inverse_phase)
     share = lax.all_to_all(parts, "coil", 0, 0, tiled=True).astype(f32).sum(axis=0)
-    others = lax.ppermute(share.astype(bf16), "row", other)
-    chip = chip_image - step_size * (share + others.astype(f32))
+    narrow = share.astype(bf16)
     margin = 2 ** thresholds.shape[0] - 1
     last = rows * planes - margin
-    edge_planes = lax.dynamic_slice_in_dim(chip, row * last, margin, axis=1).astype(bf16)
-    pairs = []
+    same, across = [], []
     for slab in range(slabs):
         after = (slab + 1) % slabs
-        pairs.append((slab * rows + rows - 1, after * rows))
-        pairs.append((after * rows, slab * rows + rows - 1))
-    halo = lax.ppermute(edge_planes, lines_axes, pairs)
+        same += [(slab * rows, after * rows), (after * rows + rows - 1, slab * rows + rows - 1)]
+        across += [(slab * rows + rows - 1, after * rows), (after * rows, slab * rows + rows - 1)]
+    low_planes, high_planes = narrow[:, :margin], narrow[:, last:]
+    first = row == 0
+    to_same = jnp.where(first, high_planes, low_planes)
+    to_across = jnp.where(first, low_planes, high_planes)
+    others = lax.ppermute(narrow, "row", other)
+    halo_same = lax.ppermute(to_same, lines_axes, same)
+    halo_across = lax.ppermute(to_across, lines_axes, across)
+    chip = chip_image - step_size * (share + others.astype(f32))
+    halo = halo_image - step_size * (halo_same.astype(f32) + halo_across.astype(f32))
     result = shrink(here, chip, halo, thresholds, edge, columns)
     gathered = lax.all_to_all(result, "coil", 0, 0, tiled=True)
     result_rows = jnp.swapaxes(gathered, 0, 1).reshape(2, phase_cells * planes, width)

time: 297 us -> 296 us (level)
  waiting for transfers between devices: 96.1 us -> 84.2 us
  starting transfers between devices: 159 us -> 169 us
    ppermute x2 -> x4, waiting for transfers between devices: 5.18 us -> 55.6 us  [the longest x1 52.9 us: local(): halo_image = lax.ppermute(border, lines_axes, around)]
    all_to_all x1, waiting for transfers between devices: 50.2 us -> 0.01 us  [local(): returned = lax.all_to_all(returning, 'slab', 0, 0, tiled=True)]
    all_to_all x1, waiting for transfers between devices: 37.7 us -> 27.5 us  [local(): received = lax.all_to_all(outgoing, 'slab', 0, 0, tiled=True)]
    ppermute x1, starting transfers between devices: 26.7 us -> 33.7 us  [local(): lax.ppermute(own_image, 'row', other)]
    ppermute x2, starting transfers between devices: 37.5 us -> 40.7 us  [both_rows(): return in_row_order(kept, lax.ppermute(away, 'row', other), axis)]
    ppermute x2 -> x4, starting transfers between devices: 31.2 us -> 29.2 us  [the longest x1 20.6 us: local(): halo_across = lax.ppermute(to_across, lines_axes, across)]
  transfers between devices with their start and end apart: 9 -> 11, of which waited for: 6 -> 4; matrix products, arithmetic and copies ran while one was open for 1% -> 1% of each run, Pallas kernels for 1% -> 1%
where the time goes in v5:
time: 296 us; the launch traced here: 295 us
  starting transfers between devices  169 us (57%)
  waiting for transfers between devices  84.2 us (28%)
  blocking collectives  22.3 us (8%)
  Pallas kernels  16.3 us (6%)
    ppermute x1, waiting for transfers between devices, local(): halo_image = lax.ppermute(border, lines_axes, around)  52.9 us
    all_to_all x1, starting transfers between devices, local(): received = lax.all_to_all(outgoing, 'slab', 0, 0, tiled=True)  45.9 us
    ppermute x2, starting transfers between devices, both_rows(): return in_row_order(kept, lax.ppermute(away, 'row', other), axis)  40.7 us
    ppermute x1, starting transfers between devices, local(): lax.ppermute(own_image, 'row', other)  33.7 us
    all_to_all x1, waiting for transfers between devices, local(): received = lax.all_to_all(outgoing, 'slab', 0, 0, tiled=True)  27.5 us
    ppermute x1, starting transfers between devices, local(): halo_across = lax.ppermute(to_across, lines_axes, across)  20.6 us
    all_to_all x1, starting transfers between devices, local(): returned = lax.all_to_all(returning, 'slab', 0, 0, tiled=True)  15.3 us
    all_to_all x1, blocking collectives, local(): lax.all_to_all(parts, 'coil', 0, 0, tiled=True).astype(f32).sum(axis=0)  13.2 us
  transfers between devices with their start and end apart: 11, of which 4 were waited for; matrix products, arithmetic and copies ran while one was open for 1% of the time, Pallas kernels for 1%

profile of v5, /device:TPU:40, one launch (start us, length us, event | category | flops | bytes accessed | tf_op | source)
XLA Modules:
  0.0 294.8 jit_solution(3978216426939317047)
XLA Ops:
  0.0 2.1 forward_sent.1
  2.1 2.0 collective-permute-start
  4.0 2.8 forward_kept.1._
  6.8 0.0 collective-permute-done.arrived_ref
  6.8 1.4 place.1
  8.3 0.0 copy-start.5
  8.3 0.0 copy-start.6
  8.3 45.9 %all-to-all-start = ((bf16[32,2,2,2,16,128]{5,4,3,2,1,0:T(8,128)(2,1)}), bf16[32,2,2,2,16,128]{5,4,3,2,1,0:T(8,128)(2,1)S(1)}, u32[]{:S(2)}, u32[]{:S(2)}) async-start(bf16[32,2,2,2,16,128]{5,4,3,2,1,0:T(8,128)(2,1)} %get-tuple-element.13), calls=%async_computation | async-start | bytes 2097152 | tf_op jit(solution)/shard_map/all_to_all | solution.py:423
  54.2 0.0 copy-done.5
  54.2 0.0 copy-done.6
  54.2 0.4 bitcast_convert_fusion
  54.7 0.0 copy-start.2
  54.7 38.7 %collective-permute-start.1 = (bf16[2,2,2,256,128]{4,3,2,1,0:T(8,128)(2,1)S(1)}, bf16[2,2,2,256,128]{4,3,2,1,0:T(8,128)(2,1)S(1)}, u32[]{:S(2)}, u32[]{:S(2)}) collective-permute-start(bf16[2,2,2,256,128]{4,3,2,1,0:T(8,128)(2,1)S(1)} %dynamic-slice_bitcast_fusion.1), channel_id=1, source_target_pairs={{0,1},{1,0},{2,3},{3,2},{4,5},{5,4},{6,7},{7,6},{8,9},{9,8},{10,11... | collective-permute-start | bytes 1572872 | tf_op jit(solution)/shard_map/ppermute | solution.py:430
  93.5 2.0 collective-permute-start.2
  95.4 1.1 collective-permute-done.2
  96.6 0.0 collective-permute-done.1
  96.6 0.1 bitcast_select_fusion.3
  96.7 0.1 pad_maximum_fusion.refs_2_
  96.8 27.5 %all-to-all-done.refs_1_ = bf16[32,2,2,2,16,128]{5,4,3,2,1,0:T(8,128)(2,1)S(1)} async-done(((bf16[32,2,2,2,16,128]{5,4,3,2,1,0:T(8,128)(2,1)}), bf16[32,2,2,2,16,128]{5,4,3,2,1,0:T(8,128)(2,1)S(1)}, u32[]{:S(2)}, u32[]{:S(2)}) %all-to-all-start) | async-done | bytes 1048608 | tf_op jit(solution)/shard_map/all_to_all | solution.py:423
  124.2 0.2 broadcast_in_dim.2.refs_3_
  124.4 3.9 %middle.1 = bf16[32,2,2,2,16,128]{5,4,3,2,1,0:T(8,128)(2,1)} custom-call(s32[1]{0:T(128)} %bitcast._.r_ref.refs_0_, bf16[32,2,2,2,16,128]{5,4,3,2,1,0:T(8,128)(2,1)S(1)} %all-to-all-done.refs_1_, bf16[2,2,4,256,128]{4,3,2,1,0:T(8,128)(2,1)S(1)} %pad_maximum_fusion.refs_2_, f32[4,256,128]{2,1,0:T(8,128)S(1)} %broadcast_in_dim.2.refs_3_, ...), custom_call_target="tpu_custom_call" | custom-call | tf_op jit(solution)/shard_map/middle/pallas_call | solution.py:459
  128.3 15.3 %all-to-all-start.1 = ((bf16[32,2,2,2,16,128]{5,4,3,2,1,0:T(8,128)(2,1)}), bf16[32,2,2,2,16,128]{5,4,3,2,1,0:T(8,128)(2,1)S(1)}, u32[]{:S(2)}, u32[]{:S(2)}) async-start(bf16[32,2,2,2,16,128]{5,4,3,2,1,0:T(8,128)(2,1)} %middle.1), calls=%async_computation.1 | async-start | bytes 2097152 | tf_op jit(solution)/shard_map/all_to_all | solution.py:477
  143.7 0.0 copy-start
  143.7 0.0 copy-done.1
  143.8 0.1 fusion.3
  143.8 33.7 %collective-permute-start.3 = (f32[2,4,40,128]{3,2,1,0:T(8,128)S(1)}, f32[2,4,40,128]{3,2,1,0:T(8,128)S(1)}, u32[]{:S(2)}, u32[]{:S(2)}) collective-permute-start(f32[2,4,40,128]{3,2,1,0:T(8,128)S(1)} %fusion.3), channel_id=1, source_target_pairs={{0,1},{1,0},{2,3},{3,2},{4,5},{5,4},{6,7},{7,6},{8,9},{9,8},{10,11... | collective-permute-start | bytes 491528 | tf_op jit(solution)/shard_map/ppermute | solution.py:453
  177.6 2.0 collective-permute-start.5
  179.6 4.6 %collective-permute-start.4 = (f32[2,3,40,128]{3,2,1,0:T(8,128)S(1)}, f32[2,3,40,128]{3,2,1,0:T(8,128)S(1)}, u32[]{:S(2)}, u32[]{:S(2)}) collective-permute-start(f32[2,3,40,128]{3,2,1,0:T(8,128)S(1)} %slice_select_fusion), channel_id=1, source_target_pairs={{1,8},{8,1},{9,16},{16,9},{17,24},{24,17},{25,32},{32,25},{33,40},... | collective-permute-start | bytes 368648 | tf_op jit(solution)/shard_map/ppermute | solution.py:484
  184.2 0.0 collective-permute-done.3
  184.3 0.0 collective-permute-done.5
  184.3 0.1 bitcast_select_fusion.1
  184.4 0.1 pad_maximum_fusion.1.refs_1_
  184.5 52.9 %collective-permute-done.4 = f32[2,3,40,128]{3,2,1,0:T(8,128)S(1)} collective-permute-done((f32[2,3,40,128]{3,2,1,0:T(8,128)S(1)}, f32[2,3,40,128]{3,2,1,0:T(8,128)S(1)}, u32[]{:S(2)}, u32[]{:S(2)}) %collective-permute-start.4) | collective-permute-done | bytes 122912 | tf_op jit(solution)/shard_map/ppermute | solution.py:484
  237.3 0.0 all-to-all-done.1.refs_0_
  237.3 2.6 backward.1
  239.9 13.2 %all_to_all.20 = bf16[4,2,8,40,128]{4,3,2,1,0:T(8,128)(2,1)S(1)} all-to-all(bf16[4,2,8,40,128]{4,3,2,1,0:T(8,128)(2,1)S(1)} %backward.1), channel_id=1, replica_groups=mesh['groups'=2,'slab'=32,'coil'=4,'row'=2] {'coil'}, dimensions={0} | all-to-all | bytes 1310720 | tf_op jit(solution)/shard_map/all_to_all | solution.py:506
  253.1 0.1 convert_reduce_fusion
  253.2 20.6 %collective-permute-start.8 = (bf16[2,3,40,128]{3,2,1,0:T(8,128)(2,1)S(1)}, bf16[2,3,40,128]{3,2,1,0:T(8,128)(2,1)S(1)}, u32[]{:S(2)}, u32[]{:S(2)}) collective-permute-start(bf16[2,3,40,128]{3,2,1,0:T(8,128)(2,1)S(1)} %get-tuple-element.30), channel_id=1, source_target_pairs={{1,8},{8,1},{9,16},{16,9},{17,24},{24,17},{25,32},{32,25},{33,40},... | collective-permute-start | bytes 184328 | tf_op jit(solution)/shard_map/ppermute | solution.py:521
  273.9 2.0 collective-permute-start.7
  275.8 0.6 broadcast_multiply_fusion.refs_3_
  276.5 2.0 collective-permute-start.6
  278.5 0.0 collective-permute-done.8
  278.5 2.7 collective-permute-done.7
  281.3 0.0 collective-permute-done.6
  281.3 0.1 multiply_subtract_fusion.refs_1_
  281.3 3.5 %wavelet.1 = bf16[4,2,128,128]{3,2,1,0:T(8,128)(2,1)S(1)} custom-call(s32[1]{0:T(128)} %bitcast._.r_ref.refs_0_, f32[2,8,40,128]{3,2,1,0:T(8,128)S(1)} %multiply_subtract_fusion.refs_1_, f32[2,3,40,128]{3,2,1,0:T(8,128)S(1)} %multiply_subtract_fusion.1.refs_2_, f32[2,7]{1,0:T(2,128)} %broadcast_multiply_fusion.refs_3_), custom_call_target="tpu_custom_call" | custom-call | tf_op jit(solution)/shard_map/wavelet/pallas_call | solution.py:314
  284.8 9.1 %all_to_all.21 = bf16[4,2,128,128]{3,2,1,0:T(8,128)(2,1)S(1)} all-to-all(bf16[4,2,128,128]{3,2,1,0:T(8,128)(2,1)S(1)} %wavelet.1), channel_id=1, replica_groups=mesh['groups'=2,'slab'=32,'coil'=4,'row'=2] {'coil'}, dimensions={0} | all-to-all | bytes 524288 | tf_op jit(solution)/shard_map/all_to_all | solution.py:525
  294.0 0.8 copy.19
  (21 shorter events, 0.3 us)
Async XLA Ops:
  2.1 4.8 %collective-permute-start = (bf16[32,2,2,16,128]{4,3,2,1,0:T(8,128)(2,1)S(1)}, bf16[32,2,2,16,128]{4,3,2,1,0:T(8,128)(2,1)S(1)}, u32[]{:S(2)}, u32[]{:S(2)}) collective-permute-start(bf16[32,2,2,16,128]{4,3,2,1,0:T(8,128)(2,1)S(1)} %forward_sent.1), channel_id=1, source_target_pairs={{0,1},{1,0},{2,3},{3,2},{4,5},{5,4},{6,7},{7,6},{8,9},{9,8},{10,11... | collective-permute-start | bytes 1572872 | tf_op jit(solution)/shard_map/ppermute | solution.py:379
  8.3 45.9 %copy-start.5 = (bf16[2,4,2,256,128]{4,3,2,1,0:T(8,128)(2,1)S(1)}, bf16[2,4,2,256,128]{4,3,2,1,0:T(8,128)(2,1)}, u32[]{:S(2)}) copy-start(bf16[2,4,2,256,128]{4,3,2,1,0:T(8,128)(2,1)} %param.13) | copy-start | bytes 3145732
  8.3 45.9 %copy-start.6 = (bf16[2,128,2,128,1,1]{3,1,0,5,4,2:T(8,128)(2,1)S(1)}, bf16[2,128,2,128,1,1]{3,1,0,5,4,2:T(8,128)(2,1)}, u32[]{:S(2)}) copy-start(bf16[2,128,2,128,1,1]{3,1,0,5,4,2:T(8,128)(2,1)} %constant.48) | copy-start | bytes 393220
  8.3 115.9 %all-to-all-start = ((bf16[32,2,2,2,16,128]{5,4,3,2,1,0:T(8,128)(2,1)}), bf16[32,2,2,2,16,128]{5,4,3,2,1,0:T(8,128)(2,1)S(1)}, u32[]{:S(2)}, u32[]{:S(2)}) async-start(bf16[32,2,2,2,16,128]{5,4,3,2,1,0:T(8,128)(2,1)} %get-tuple-element.13), calls=%async_computation | async-start | bytes 2097152 | tf_op jit(solution)/shard_map/all_to_all | solution.py:423
  54.7 38.8 %copy-start.2 = (s32[2,256]{1,0:T(2,128)S(1)}, s32[2,256]{1,0:T(2,128)}, u32[]{:S(2)}) copy-start(s32[2,256]{1,0:T(2,128)} %param.14) | copy-start | bytes 6148
  54.7 41.8 %collective-permute-start.1 = (bf16[2,2,2,256,128]{4,3,2,1,0:T(8,128)(2,1)S(1)}, bf16[2,2,2,256,128]{4,3,2,1,0:T(8,128)(2,1)S(1)}, u32[]{:S(2)}, u32[]{:S(2)}) collective-permute-start(bf16[2,2,2,256,128]{4,3,2,1,0:T(8,128)(2,1)S(1)} %dynamic-slice_bitcast_fusion.1), channel_id=1, source_target_pairs={{0,1},{1,0},{2,3},{3,2},{4,5},{5,4},{6,7},{7,6},{8,9},{9,8},{10,11... | collective-permute-start | bytes 1572872 | tf_op jit(solution)/shard_map/ppermute | solution.py:430
  93.5 3.1 %collective-permute-start.2 = (f32[2,256]{1,0:T(2,128)S(1)}, f32[2,256]{1,0:T(2,128)S(1)}, u32[]{:S(2)}, u32[]{:S(2)}) collective-permute-start(f32[2,256]{1,0:T(2,128)S(1)} %convert_element_type.33), channel_id=1, source_target_pairs={{0,1},{1,0},{2,3},{3,2},{4,5},{5,4},{6,7},{7,6},{8,9},{9,8},{10,11... | collective-permute-start | bytes 6152 | tf_op jit(solution)/shard_map/ppermute | solution.py:441
  128.3 15.4 %copy-start.1 = (f32[2,128,4,128]{3,2,1,0:T(4,128)S(1)}, f32[2,128,4,128]{3,2,1,0:T(4,128)}, u32[]{:S(2)}) copy-start(f32[2,128,4,128]{3,2,1,0:T(4,128)} %param.11) | copy-start | bytes 1572868
  128.3 109.0 %all-to-all-start.1 = ((bf16[32,2,2,2,16,128]{5,4,3,2,1,0:T(8,128)(2,1)}), bf16[32,2,2,2,16,128]{5,4,3,2,1,0:T(8,128)(2,1)S(1)}, u32[]{:S(2)}, u32[]{:S(2)}) async-start(bf16[32,2,2,2,16,128]{5,4,3,2,1,0:T(8,128)(2,1)} %middle.1), calls=%async_computation.1 | async-start | bytes 2097152 | tf_op jit(solution)/shard_map/all_to_all | solution.py:477
  143.7 33.9 %copy-start = (bf16[2,4,128,4,128]{4,3,2,1,0:T(4,128)(2,1)S(1)}, bf16[2,4,128,4,128]{4,3,2,1,0:T(4,128)(2,1)}, u32[]{:S(2)}) copy-start(bf16[2,4,128,4,128]{4,3,2,1,0:T(4,128)(2,1)} %param.12) | copy-start | bytes 3145732
  143.8 40.3 %collective-permute-start.3 = (f32[2,4,40,128]{3,2,1,0:T(8,128)S(1)}, f32[2,4,40,128]{3,2,1,0:T(8,128)S(1)}, u32[]{:S(2)}, u32[]{:S(2)}) collective-permute-start(f32[2,4,40,128]{3,2,1,0:T(8,128)S(1)} %fusion.3), channel_id=1, source_target_pairs={{0,1},{1,0},{2,3},{3,2},{4,5},{5,4},{6,7},{7,6},{8,9},{9,8},{10,11... | collective-permute-start | bytes 491528 | tf_op jit(solution)/shard_map/ppermute | solution.py:453
  177.6 6.6 %collective-permute-start.5 = (bf16[2,2,1,512,128]{4,3,2,1,0:T(8,128)(2,1)S(1)}, bf16[2,2,1,512,128]{4,3,2,1,0:T(8,128)(2,1)S(1)}, u32[]{:S(2)}, u32[]{:S(2)}) collective-permute-start(bf16[2,2,1,512,128]{4,3,2,1,0:T(8,128)(2,1)S(1)} %dynamic-slice_bitcast_fusion), channel_id=1, source_target_pairs={{0,1},{1,0},{2,3},{3,2},{4,5},{5,4},{6,7},{7,6},{8,9},{9,8},{10,11... | collective-permute-start | bytes 1572872 | tf_op jit(solution)/shard_map/ppermute | solution.py:430
  179.6 57.7 %collective-permute-start.4 = (f32[2,3,40,128]{3,2,1,0:T(8,128)S(1)}, f32[2,3,40,128]{3,2,1,0:T(8,128)S(1)}, u32[]{:S(2)}, u32[]{:S(2)}) collective-permute-start(f32[2,3,40,128]{3,2,1,0:T(8,128)S(1)} %slice_select_fusion), channel_id=1, source_target_pairs={{1,8},{8,1},{9,16},{16,9},{17,24},{24,17},{25,32},{32,25},{33,40},... | collective-permute-start | bytes 368648 | tf_op jit(solution)/shard_map/ppermute | solution.py:484
  253.1 22.7 %copy-start.3 = (f32[2,7]{1,0:T(2,128)S(1)}, f32[2,7]{1,0:T(2,128)}, u32[]{:S(2)}) copy-start(f32[2,7]{1,0:T(2,128)} %param.15) | copy-start | bytes 172
  253.1 22.7 %copy-start.4 = (f32[2]{0:T(128)S(1)}, f32[2]{0:T(128)}, u32[]{:S(2)}) copy-start(f32[2]{0:T(128)} %constant.47) | copy-start | bytes 28
  253.2 25.3 %collective-permute-start.8 = (bf16[2,3,40,128]{3,2,1,0:T(8,128)(2,1)S(1)}, bf16[2,3,40,128]{3,2,1,0:T(8,128)(2,1)S(1)}, u32[]{:S(2)}, u32[]{:S(2)}) collective-permute-start(bf16[2,3,40,128]{3,2,1,0:T(8,128)(2,1)S(1)} %get-tuple-element.30), channel_id=1, source_target_pairs={{1,8},{8,1},{9,16},{16,9},{17,24},{24,17},{25,32},{32,25},{33,40},... | collective-permute-start | bytes 184328 | tf_op jit(solution)/shard_map/ppermute | solution.py:521
  273.9 7.4 %collective-permute-start.7 = (bf16[2,3,40,128]{3,2,1,0:T(8,128)(2,1)S(1)}, bf16[2,3,40,128]{3,2,1,0:T(8,128)(2,1)S(1)}, u32[]{:S(2)}, u32[]{:S(2)}) collective-permute-start(bf16[2,3,40,128]{3,2,1,0:T(8,128)(2,1)S(1)} %get-tuple-element.29), channel_id=1, source_target_pairs={{0,8},{9,1},{8,16},{17,9},{16,24},{25,17},{24,32},{33,25},{32,40},... | collective-permute-start | bytes 184328 | tf_op jit(solution)/shard_map/ppermute | solution.py:520
  276.5 4.8 %collective-permute-start.6 = (bf16[2,8,40,128]{3,2,1,0:T(8,128)(2,1)S(1)}, bf16[2,8,40,128]{3,2,1,0:T(8,128)(2,1)S(1)}, u32[]{:S(2)}, u32[]{:S(2)}) collective-permute-start(bf16[2,8,40,128]{3,2,1,0:T(8,128)(2,1)S(1)} %convert_element_type.35), channel_id=1, source_target_pairs={{0,1},{1,0},{2,3},{3,2},{4,5},{5,4},{6,7},{7,6},{8,9},{9,8},{10,11... | collective-permute-start | bytes 491528 | tf_op jit(solution)/shard_map/ppermute | solution.py:519

commit v6 on v4

--- a/solution.py
+++ b/solution.py
@@ -11,7 +11,7 @@
 
 step_size = 0.5
 lines_axes = ("slab", "row")
-pause_steps = 6500
+pause_steps = 7100
 
 
 def fourier_table(length, sign, rows=None, columns=None):

time: 297 us -> 292 us (0.983)
  waiting for transfers between devices: 96.1 us -> 72.8 us
  starting transfers between devices: 159 us -> 177 us
    all_to_all x1, waiting for transfers between devices: 37.7 us -> 27.5 us  [local(): received = lax.all_to_all(outgoing, 'slab', 0, 0, tiled=True)]
    all_to_all x1, waiting for transfers between devices: 50.2 us -> 40.1 us  [local(): returned = lax.all_to_all(returning, 'slab', 0, 0, tiled=True)]
    ppermute x1, starting transfers between devices: 26.7 us -> 33.7 us  [local(): lax.ppermute(own_image, 'row', other)]
    ppermute x1, starting transfers between devices: 1.95 us -> 5.28 us  [local(): halo = lax.ppermute(edge_planes, lines_axes, pairs)]
    ppermute x2, starting transfers between devices: 37.5 us -> 40.7 us  [both_rows(): return in_row_order(kept, lax.ppermute(away, 'row', other), axis)]
where the time goes in v6:
time: 292 us; the launch traced here: 291 us
  starting transfers between devices  177 us (61%)
  waiting for transfers between devices  72.8 us (25%)
  blocking collectives  22.3 us (8%)
  Pallas kernels  16.2 us (6%)
    all_to_all x1, starting transfers between devices, local(): received = lax.all_to_all(outgoing, 'slab', 0, 0, tiled=True)  45.9 us
    ppermute x2, starting transfers between devices, both_rows(): return in_row_order(kept, lax.ppermute(away, 'row', other), axis)  40.7 us
    all_to_all x1, waiting for transfers between devices, local(): returned = lax.all_to_all(returning, 'slab', 0, 0, tiled=True)  40.1 us
    ppermute x1, starting transfers between devices, local(): lax.ppermute(own_image, 'row', other)  33.7 us
    ppermute x1, starting transfers between devices, local(): others = lax.ppermute(share.astype(bf16), 'row', other)  32 us
    all_to_all x1, waiting for transfers between devices, local(): received = lax.all_to_all(outgoing, 'slab', 0, 0, tiled=True)  27.5 us
    all_to_all x1, starting transfers between devices, local(): returned = lax.all_to_all(returning, 'slab', 0, 0, tiled=True)  15.3 us
    all_to_all x1, blocking collectives, local(): lax.all_to_all(parts, 'coil', 0, 0, tiled=True).astype(f32).sum(axis=0)  13.2 us
  transfers between devices with their start and end apart: 9, of which 6 were waited for; matrix products, arithmetic and copies ran while one was open for 1% of the time, Pallas kernels for 1%

profile of v6, /device:TPU:40, one launch (start us, length us, event | category | flops | bytes accessed | tf_op | source)
XLA Modules:
  0.0 291.4 jit_solution(15513499713485314839)
XLA Ops:
  0.0 2.1 forward_sent.1
  2.1 2.0 collective-permute-start
  4.0 2.8 forward_kept.1._
  6.8 0.0 collective-permute-done.arrived_ref
  6.8 1.4 place.1
  8.2 0.0 copy-start.5
  8.2 0.0 copy-start.6
  8.2 45.9 %all-to-all-start = ((bf16[32,2,2,2,16,128]{5,4,3,2,1,0:T(8,128)(2,1)}), bf16[32,2,2,2,16,128]{5,4,3,2,1,0:T(8,128)(2,1)S(1)}, u32[]{:S(2)}, u32[]{:S(2)}) async-start(bf16[32,2,2,2,16,128]{5,4,3,2,1,0:T(8,128)(2,1)} %get-tuple-element.12), calls=%async_computation | async-start | bytes 2097152 | tf_op jit(solution)/shard_map/all_to_all | solution.py:423
  54.2 0.0 copy-done.5
  54.2 0.0 copy-done.6
  54.2 0.4 bitcast_convert_fusion
  54.6 0.0 copy-start.2
  54.7 38.7 %collective-permute-start.1 = (bf16[2,2,2,256,128]{4,3,2,1,0:T(8,128)(2,1)S(1)}, bf16[2,2,2,256,128]{4,3,2,1,0:T(8,128)(2,1)S(1)}, u32[]{:S(2)}, u32[]{:S(2)}) collective-permute-start(bf16[2,2,2,256,128]{4,3,2,1,0:T(8,128)(2,1)S(1)} %dynamic-slice_bitcast_fusion.1), channel_id=1, source_target_pairs={{0,1},{1,0},{2,3},{3,2},{4,5},{5,4},{6,7},{7,6},{8,9},{9,8},{10,11... | collective-permute-start | bytes 1572872 | tf_op jit(solution)/shard_map/ppermute | solution.py:430
  93.4 0.0 copy-done.2
  93.4 2.0 collective-permute-start.2
  95.4 1.1 collective-permute-done.2
  96.5 0.0 collective-permute-done.1
  96.6 0.1 bitcast_select_fusion.3
  96.6 0.1 pad_maximum_fusion.refs_2_
  96.7 27.5 %all-to-all-done.refs_1_ = bf16[32,2,2,2,16,128]{5,4,3,2,1,0:T(8,128)(2,1)S(1)} async-done(((bf16[32,2,2,2,16,128]{5,4,3,2,1,0:T(8,128)(2,1)}), bf16[32,2,2,2,16,128]{5,4,3,2,1,0:T(8,128)(2,1)S(1)}, u32[]{:S(2)}, u32[]{:S(2)}) %all-to-all-start) | async-done | bytes 1048608 | tf_op jit(solution)/shard_map/all_to_all | solution.py:423
  124.2 0.2 broadcast_in_dim.2.refs_3_
  124.4 3.9 %middle.1 = bf16[32,2,2,2,16,128]{5,4,3,2,1,0:T(8,128)(2,1)} custom-call(s32[1]{0:T(128)} %bitcast._.r_ref.refs_0_, bf16[32,2,2,2,16,128]{5,4,3,2,1,0:T(8,128)(2,1)S(1)} %all-to-all-done.refs_1_, bf16[2,2,4,256,128]{4,3,2,1,0:T(8,128)(2,1)S(1)} %pad_maximum_fusion.refs_2_, f32[4,256,128]{2,1,0:T(8,128)S(1)} %broadcast_in_dim.2.refs_3_, ...), custom_call_target="tpu_custom_call" | custom-call | tf_op jit(solution)/shard_map/middle/pallas_call | solution.py:459
  128.3 15.3 %all-to-all-start.1 = ((bf16[32,2,2,2,16,128]{5,4,3,2,1,0:T(8,128)(2,1)}), bf16[32,2,2,2,16,128]{5,4,3,2,1,0:T(8,128)(2,1)S(1)}, u32[]{:S(2)}, u32[]{:S(2)}) async-start(bf16[32,2,2,2,16,128]{5,4,3,2,1,0:T(8,128)(2,1)} %middle.1), calls=%async_computation.1 | async-start | bytes 2097152 | tf_op jit(solution)/shard_map/all_to_all | solution.py:477
  143.7 0.0 copy-start
  143.7 0.0 copy-done.1
  143.7 0.1 fusion.3
  143.8 33.7 %collective-permute-start.3 = (f32[2,4,40,128]{3,2,1,0:T(8,128)S(1)}, f32[2,4,40,128]{3,2,1,0:T(8,128)S(1)}, u32[]{:S(2)}, u32[]{:S(2)}) collective-permute-start(f32[2,4,40,128]{3,2,1,0:T(8,128)S(1)} %fusion.3), channel_id=1, source_target_pairs={{0,1},{1,0},{2,3},{3,2},{4,5},{5,4},{6,7},{7,6},{8,9},{9,8},{10,11... | collective-permute-start | bytes 491528 | tf_op jit(solution)/shard_map/ppermute | solution.py:453
  177.6 0.0 copy-done
  177.6 2.0 collective-permute-start.4
  179.6 0.0 collective-permute-done.3
  179.6 1.8 collective-permute-done.4
  181.4 0.1 bitcast_select_fusion.1
  181.5 0.1 pad_maximum_fusion.1.refs_1_
  181.6 40.1 %all-to-all-done.1.refs_0_ = bf16[32,2,2,2,16,128]{5,4,3,2,1,0:T(8,128)(2,1)S(1)} async-done(((bf16[32,2,2,2,16,128]{5,4,3,2,1,0:T(8,128)(2,1)}), bf16[32,2,2,2,16,128]{5,4,3,2,1,0:T(8,128)(2,1)S(1)}, u32[]{:S(2)}, u32[]{:S(2)}) %all-to-all-start.1) | async-done | bytes 1048608 | tf_op jit(solution)/shard_map/all_to_all | solution.py:477
  221.8 2.6 backward.1
  224.4 13.2 %all_to_all.20 = bf16[4,2,8,40,128]{4,3,2,1,0:T(8,128)(2,1)S(1)} all-to-all(bf16[4,2,8,40,128]{4,3,2,1,0:T(8,128)(2,1)S(1)} %backward.1), channel_id=1, replica_groups=mesh['groups'=2,'slab'=32,'coil'=4,'row'=2] {'coil'}, dimensions={0} | all-to-all | bytes 1310720 | tf_op jit(solution)/shard_map/all_to_all | solution.py:499
  237.5 0.1 convert_reduce_fusion
  237.6 0.0 copy-start.3
  237.6 0.0 copy-start.4
  237.7 32.0 %collective-permute-start.5 = (bf16[2,8,40,128]{3,2,1,0:T(8,128)(2,1)S(1)}, bf16[2,8,40,128]{3,2,1,0:T(8,128)(2,1)S(1)}, u32[]{:S(2)}, u32[]{:S(2)}) collective-permute-start(bf16[2,8,40,128]{3,2,1,0:T(8,128)(2,1)S(1)} %convert_element_type.32), channel_id=1, source_target_pairs={{0,1},{1,0},{2,3},{3,2},{4,5},{5,4},{6,7},{7,6},{8,9},{9,8},{10,11... | collective-permute-start | bytes 491528 | tf_op jit(solution)/shard_map/ppermute | solution.py:500
  269.7 1.0 collective-permute-done.5
  270.8 5.3 %collective-permute-start.6 = (bf16[2,3,40,128]{3,2,1,0:T(8,128)(2,1)S(1)}, bf16[2,3,40,128]{3,2,1,0:T(8,128)(2,1)S(1)}, u32[]{:S(2)}, u32[]{:S(2)}) collective-permute-start(bf16[2,3,40,128]{3,2,1,0:T(8,128)(2,1)S(1)} %dynamic-slice_convert_fusion), channel_id=1, source_target_pairs={{1,8},{8,1},{9,16},{16,9},{17,24},{24,17},{25,32},{32,25},{33,40},... | collective-permute-start | bytes 184328 | tf_op jit(solution)/shard_map/ppermute | solution.py:510
  276.0 0.0 copy-done.3
  276.1 0.6 broadcast_multiply_fusion.refs_3_
  276.7 1.2 collective-permute-done.6.refs_2_
  277.9 3.5 %wavelet.1 = bf16[4,2,128,128]{3,2,1,0:T(8,128)(2,1)S(1)} custom-call(s32[1]{0:T(128)} %bitcast._.r_ref.refs_0_, f32[2,8,40,128]{3,2,1,0:T(8,128)S(1)} %multiply_subtract_fusion.refs_1_, bf16[2,3,40,128]{3,2,1,0:T(8,128)(2,1)S(1)} %collective-permute-done.6.refs_2_, f32[2,7]{1,0:T(2,128)} %broadcast_multiply_fusion.refs_3_), custom_call_target="tpu_custom_call" | custom-call | tf_op jit(solution)/shard_map/wavelet/pallas_call | solution.py:314
  281.4 9.1 %all_to_all.21 = bf16[4,2,128,128]{3,2,1,0:T(8,128)(2,1)S(1)} all-to-all(bf16[4,2,128,128]{3,2,1,0:T(8,128)(2,1)S(1)} %wavelet.1), channel_id=1, replica_groups=mesh['groups'=2,'slab'=32,'coil'=4,'row'=2] {'coil'}, dimensions={0} | all-to-all | bytes 524288 | tf_op jit(solution)/shard_map/all_to_all | solution.py:512
  290.6 0.8 copy.19
  (15 shorter events, 0.3 us)
Async XLA Ops:
  2.1 4.7 %collective-permute-start = (bf16[32,2,2,16,128]{4,3,2,1,0:T(8,128)(2,1)S(1)}, bf16[32,2,2,16,128]{4,3,2,1,0:T(8,128)(2,1)S(1)}, u32[]{:S(2)}, u32[]{:S(2)}) collective-permute-start(bf16[32,2,2,16,128]{4,3,2,1,0:T(8,128)(2,1)S(1)} %forward_sent.1), channel_id=1, source_target_pairs={{0,1},{1,0},{2,3},{3,2},{4,5},{5,4},{6,7},{7,6},{8,9},{9,8},{10,11... | collective-permute-start | bytes 1572872 | tf_op jit(solution)/shard_map/ppermute | solution.py:379
  8.2 45.9 %copy-start.5 = (bf16[2,4,2,256,128]{4,3,2,1,0:T(8,128)(2,1)S(1)}, bf16[2,4,2,256,128]{4,3,2,1,0:T(8,128)(2,1)}, u32[]{:S(2)}) copy-start(bf16[2,4,2,256,128]{4,3,2,1,0:T(8,128)(2,1)} %param.13) | copy-start | bytes 3145732
  8.2 45.9 %copy-start.6 = (bf16[2,128,2,128,1,1]{3,1,0,5,4,2:T(8,128)(2,1)S(1)}, bf16[2,128,2,128,1,1]{3,1,0,5,4,2:T(8,128)(2,1)}, u32[]{:S(2)}) copy-start(bf16[2,128,2,128,1,1]{3,1,0,5,4,2:T(8,128)(2,1)} %constant.51) | copy-start | bytes 393220
  8.2 116.0 %all-to-all-start = ((bf16[32,2,2,2,16,128]{5,4,3,2,1,0:T(8,128)(2,1)}), bf16[32,2,2,2,16,128]{5,4,3,2,1,0:T(8,128)(2,1)S(1)}, u32[]{:S(2)}, u32[]{:S(2)}) async-start(bf16[32,2,2,2,16,128]{5,4,3,2,1,0:T(8,128)(2,1)} %get-tuple-element.12), calls=%async_computation | async-start | bytes 2097152 | tf_op jit(solution)/shard_map/all_to_all | solution.py:423
  54.6 38.8 %copy-start.2 = (s32[2,256]{1,0:T(2,128)S(1)}, s32[2,256]{1,0:T(2,128)}, u32[]{:S(2)}) copy-start(s32[2,256]{1,0:T(2,128)} %param.14) | copy-start | bytes 6148
  54.7 41.9 %collective-permute-start.1 = (bf16[2,2,2,256,128]{4,3,2,1,0:T(8,128)(2,1)S(1)}, bf16[2,2,2,256,128]{4,3,2,1,0:T(8,128)(2,1)S(1)}, u32[]{:S(2)}, u32[]{:S(2)}) collective-permute-start(bf16[2,2,2,256,128]{4,3,2,1,0:T(8,128)(2,1)S(1)} %dynamic-slice_bitcast_fusion.1), channel_id=1, source_target_pairs={{0,1},{1,0},{2,3},{3,2},{4,5},{5,4},{6,7},{7,6},{8,9},{9,8},{10,11... | collective-permute-start | bytes 1572872 | tf_op jit(solution)/shard_map/ppermute | solution.py:430
  93.4 3.1 %collective-permute-start.2 = (f32[2,256]{1,0:T(2,128)S(1)}, f32[2,256]{1,0:T(2,128)S(1)}, u32[]{:S(2)}, u32[]{:S(2)}) collective-permute-start(f32[2,256]{1,0:T(2,128)S(1)} %convert_element_type.30), channel_id=1, source_target_pairs={{0,1},{1,0},{2,3},{3,2},{4,5},{5,4},{6,7},{7,6},{8,9},{9,8},{10,11... | collective-permute-start | bytes 6152 | tf_op jit(solution)/shard_map/ppermute | solution.py:441
  128.3 15.4 %copy-start.1 = (f32[2,128,4,128]{3,2,1,0:T(4,128)S(1)}, f32[2,128,4,128]{3,2,1,0:T(4,128)}, u32[]{:S(2)}) copy-start(f32[2,128,4,128]{3,2,1,0:T(4,128)} %param.11) | copy-start | bytes 1572868
  128.3 93.5 %all-to-all-start.1 = ((bf16[32,2,2,2,16,128]{5,4,3,2,1,0:T(8,128)(2,1)}), bf16[32,2,2,2,16,128]{5,4,3,2,1,0:T(8,128)(2,1)S(1)}, u32[]{:S(2)}, u32[]{:S(2)}) async-start(bf16[32,2,2,2,16,128]{5,4,3,2,1,0:T(8,128)(2,1)} %middle.1), calls=%async_computation.1 | async-start | bytes 2097152 | tf_op jit(solution)/shard_map/all_to_all | solution.py:477
  143.7 33.9 %copy-start = (bf16[2,4,128,4,128]{4,3,2,1,0:T(4,128)(2,1)S(1)}, bf16[2,4,128,4,128]{4,3,2,1,0:T(4,128)(2,1)}, u32[]{:S(2)}) copy-start(bf16[2,4,128,4,128]{4,3,2,1,0:T(4,128)(2,1)} %param.12) | copy-start | bytes 3145732
  143.8 35.8 %collective-permute-start.3 = (f32[2,4,40,128]{3,2,1,0:T(8,128)S(1)}, f32[2,4,40,128]{3,2,1,0:T(8,128)S(1)}, u32[]{:S(2)}, u32[]{:S(2)}) collective-permute-start(f32[2,4,40,128]{3,2,1,0:T(8,128)S(1)} %fusion.3), channel_id=1, source_target_pairs={{0,1},{1,0},{2,3},{3,2},{4,5},{5,4},{6,7},{7,6},{8,9},{9,8},{10,11... | collective-permute-start | bytes 491528 | tf_op jit(solution)/shard_map/ppermute | solution.py:453
  177.6 3.8 %collective-permute-start.4 = (bf16[2,2,1,512,128]{4,3,2,1,0:T(8,128)(2,1)S(1)}, bf16[2,2,1,512,128]{4,3,2,1,0:T(8,128)(2,1)S(1)}, u32[]{:S(2)}, u32[]{:S(2)}) collective-permute-start(bf16[2,2,1,512,128]{4,3,2,1,0:T(8,128)(2,1)S(1)} %dynamic-slice_bitcast_fusion), channel_id=1, source_target_pairs={{0,1},{1,0},{2,3},{3,2},{4,5},{5,4},{6,7},{7,6},{8,9},{9,8},{10,11... | collective-permute-start | bytes 1572872 | tf_op jit(solution)/shard_map/ppermute | solution.py:430
  237.6 38.4 %copy-start.3 = (f32[2,7]{1,0:T(2,128)S(1)}, f32[2,7]{1,0:T(2,128)}, u32[]{:S(2)}) copy-start(f32[2,7]{1,0:T(2,128)} %param.15) | copy-start | bytes 172
  237.6 38.4 %copy-start.4 = (f32[2]{0:T(128)S(1)}, f32[2]{0:T(128)}, u32[]{:S(2)}) copy-start(f32[2]{0:T(128)} %constant.50) | copy-start | bytes 28
  237.7 33.0 %collective-permute-start.5 = (bf16[2,8,40,128]{3,2,1,0:T(8,128)(2,1)S(1)}, bf16[2,8,40,128]{3,2,1,0:T(8,128)(2,1)S(1)}, u32[]{:S(2)}, u32[]{:S(2)}) collective-permute-start(bf16[2,8,40,128]{3,2,1,0:T(8,128)(2,1)S(1)} %convert_element_type.32), channel_id=1, source_target_pairs={{0,1},{1,0},{2,3},{3,2},{4,5},{5,4},{6,7},{7,6},{8,9},{9,8},{10,11... | collective-permute-start | bytes 491528 | tf_op jit(solution)/shard_map/ppermute | solution.py:500
  270.8 7.2 %collective-permute-start.6 = (bf16[2,3,40,128]{3,2,1,0:T(8,128)(2,1)S(1)}, bf16[2,3,40,128]{3,2,1,0:T(8,128)(2,1)S(1)}, u32[]{:S(2)}, u32[]{:S(2)}) collective-permute-start(bf16[2,3,40,128]{3,2,1,0:T(8,128)(2,1)S(1)} %dynamic-slice_convert_fusion), channel_id=1, source_target_pairs={{1,8},{8,1},{9,16},{16,9},{17,24},{24,17},{25,32},{32,25},{33,40},... | collective-permute-start | bytes 184328 | tf_op jit(solution)/shard_map/ppermute | solution.py:510
